TPU v7x, 32 devices: a whole 2x2x4 slice. The times are simulated.
32 devices in a mesh: space: 8 (over y, x, core), tm: 4 (over z).
Axes of the slice: x: 2, y: 2, z: 4, core: 2. Of those that a mesh axis runs over, the one named last changes fastest.
Arguments:
- links: float32 [4, 3, 2, 3, 3, 16, 4096], P('tm', None, None, None, None, 'space'), may hold values from -1 to 1, as said below
- propagator: float32 [2, 144, 16, 4096], P(None, 'tm', 'space'), may hold values from -6 to 6
- sink_time: int32 [1], replicated, may hold values from 0 to 16383
- src_time: int32 [1], replicated, may hold values from 0 to 16383
- src_site: int32 [1], replicated, may hold values from 0 to 65535
Outputs:
- fixed_links: float32 [4, 3, 2, 3, 3, 16, 4096], P('tm', None, None, None, None, 'space')
- wall: float32 [2, 144], replicated
Inputs may be any that keep to these rules, and one draw needn't show every extreme that they name: `links`: every link is a special unitary 3 x 3 matrix up to rounding.
All inputs are finite; a program needn't handle non-finite values.
Results may differ from a plain program's by a relative error of at most 0.0001.
Values sent between devices are 32-bit elements; how exact they have to be, the bound alone decides.
No kernel may reach another device: no remote copies, remote signals or barrier semaphores. Data moves between devices by JAX's collectives and lax.ppermute only.
A program may use at most 128 MiB of HBM per device.

v0:
```python
import functools
import math

import jax
import jax.numpy as jnp
import numpy as np
from jax import lax
from jax.experimental import pallas as pl
from jax.experimental.pallas import tpu as pltpu
from jax.sharding import PartitionSpec as P

SC = 12
STEP_SIZE = 0.08
PEAK_SQUARE = 12.0
F32 = jnp.float32
BF16 = jnp.bfloat16
VMEM = pltpu.VMEM
PAIRS = ((0, 1), (0, 2), (1, 2))


def split_table(table):
    high = table.astype(jnp.bfloat16)
    low = (table - high.astype(np.float64)).astype(jnp.bfloat16)
    return high, low


def as_real(real, imag):
    return np.block([[real, imag], [-imag, real]])


@functools.lru_cache(None)
def transform_tables(side, inverse):
    half = side // 2
    sign = 1.0 if inverse else -1.0
    k = np.arange(half)
    row_phase = sign * 2.0 * np.pi * np.outer(k, k) / half
    rows_left = as_real(np.cos(row_phase), -np.sin(row_phase))
    high, low = split_table(rows_left)
    left = np.concatenate([high, low, high], axis=1)
    z = np.arange(side)
    depth_phase = sign * 2.0 * np.pi * np.outer(z, z) / side
    parity = np.array([[1.0, 1.0], [1.0, -1.0]])
    right = as_real(np.kron(parity, np.cos(depth_phase)), np.kron(parity, np.sin(depth_phase)))
    high, low = split_table(right)
    right = np.stack([high, low])
    twiddle_phase = sign * 2.0 * np.pi * k / side
    lanes = np.arange(2 * side) >= side
    phase = np.where(lanes[None, :], twiddle_phase[:, None], 0.0)
    twiddle = np.stack([np.cos(phase), np.sin(phase)]).astype(np.float32)
    return left, right, twiddle


@functools.lru_cache(None)
def filter_table(side, across, blocks):
    half = side // 2
    squares = 4.0 * np.sin(np.pi * np.arange(side) / side) ** 2
    squares_across = 4.0 * np.sin(np.pi * np.arange(across) / across) ** 2
    column = (squares[:, None] + squares[None, :]).reshape(2, half, side)
    column = np.swapaxes(column, 0, 1).reshape(half, 2 * side)
    momentum = squares_across[:, None, None] + column[None]
    weight = np.where(momentum > 0.0, PEAK_SQUARE / np.where(momentum > 0.0, momentum, 1.0), 0.0)
    offsets = np.arange(across // 2 + 1)
    phase = np.cos(2.0 * np.pi * np.outer(offsets, np.arange(across)) / across)
    table = np.einsum("dk,krl->drl", phase, weight) / (across * side * side)
    table = table * (STEP_SIZE / 16.0)
    table = table.reshape(len(offsets), blocks, half // blocks, 2 * side)
    return np.ascontiguousarray(np.swapaxes(table, 0, 1)).astype(np.float32)


def cmul(x, y):
    return x[0] * y[0] - x[1] * y[1], x[0] * y[1] + x[1] * y[0]


def csquare(x):
    return x[0] * x[0] - x[1] * x[1], 2.0 * (x[0] * x[1])


def row_times(row, matrix):
    out = []
    for b in range(3):
        re = row[0][0] * matrix[0][b][0] - row[0][1] * matrix[0][b][1]
        im = row[0][0] * matrix[0][b][1] + row[0][1] * matrix[0][b][0]
        for k in (1, 2):
            re = re + row[k][0] * matrix[k][b][0] - row[k][1] * matrix[k][b][1]
            im = im + row[k][0] * matrix[k][b][1] + row[k][1] * matrix[k][b][0]
        out.append((re, im))
    return out


def row_times_dagger(row, matrix):
    out = []
    for b in range(3):
        re = row[0][0] * matrix[b][0][0] + row[0][1] * matrix[b][0][1]
        im = row[0][1] * matrix[b][0][0] - row[0][0] * matrix[b][0][1]
        for k in (1, 2):
            re = re + row[k][0] * matrix[b][k][0] + row[k][1] * matrix[b][k][1]
            im = im + row[k][1] * matrix[b][k][0] - row[k][0] * matrix[b][k][1]
        out.append((re, im))
    return out


def exponential(x):
    t0, t1 = x[0], x[1]
    a, b, e = (x[2], x[3]), (x[4], x[5]), (x[6], x[7])
    t2 = -(t0 + t1)
    na = a[0] * a[0] + a[1] * a[1]
    nb = b[0] * b[0] + b[1] * b[1]
    ne = e[0] * e[0] + e[1] * e[1]
    s0, s1, s2 = t0 * t0, t1 * t1, t2 * t2
    ae = cmul(a, e)
    c = -(0.5 * (s0 + s1 + s2) + (na + nb + ne))
    cross = ae[1] * b[0] - ae[0] * b[1]
    d = t0 * ne + t1 * nb + t2 * na - t0 * t1 * t2 - 2.0 * cross
    c30 = c * (1.0 / 30.0)
    q0 = (None, d * (1.0 / 120.0))
    q1 = ((1.0 + c30) * 0.25, None)
    q2r = 1.0 / 20.0
    n0i = d * (q2r / 3.0)
    n1 = ((1.0 + c * q2r) * (1.0 / 3.0), q0[1] * (1.0 / 3.0))
    n2r = q1[0] * (1.0 / 3.0)
    m0 = (None, d * (0.5 * n2r))
    m1 = (0.5 + 0.5 * (c * n2r), 0.5 * n0i)
    m2 = (0.5 * n1[0], 0.5 * n1[1])
    q0 = (1.0 - d * m2[1], d * m2[0])
    q1 = (1.0 + c * m2[0], m0[1] + c * m2[1])
    q2 = m1
    for _ in range(3):
        q12 = cmul(q1, q2)
        q22 = csquare(q2)
        q00 = csquare(q0)
        q11 = csquare(q1)
        q01 = cmul(q0, q1)
        q02 = cmul(q0, q2)
        d2 = 2.0 * d
        q0 = (q00[0] - d2 * q12[1], q00[1] + d2 * q12[0])
        q1 = (
            2.0 * (q01[0] + c * q12[0]) - d * q22[1],
            2.0 * (q01[1] + c * q12[1]) + d * q22[0],
        )
        q2 = (q11[0] + 2.0 * q02[0] + c * q22[0], q11[1] + 2.0 * q02[1] + c * q22[1])
    u, v = q1
    s, t = q2
    result = [[None] * 3 for _ in range(3)]
    for at, (theta, m) in enumerate(
        ((t0, -(s0 + na + nb)), (t1, -(s1 + na + ne)), (t2, -(s2 + nb + ne)))
    ):
        result[at][at] = (q0[0] - v * theta + s * m, q0[1] + u * theta + t * m)
    y01 = (t2 * a[1] - (b[0] * e[0] + b[1] * e[1]), -t2 * a[0] - (b[1] * e[0] - b[0] * e[1]))
    y02 = (t1 * b[1] + ae[0], -t1 * b[0] + ae[1])
    y12 = (t0 * e[1] - (a[0] * b[0] + a[1] * b[1]), -t0 * e[0] - (a[0] * b[1] - a[1] * b[0]))
    for (i, j), xx, yy in zip(PAIRS, (a, b, e), (y01, y02, y12)):
        ur, vi, ui, vr = u * xx[0], v * xx[1], u * xx[1], v * xx[0]
        sr, ti, si, tr = s * yy[0], t * yy[1], s * yy[1], t * yy[0]
        result[i][j] = ((ur - vi) + (sr - ti), (ui + vr) + (si + tr))
        result[j][i] = ((sr + ti) - (ur + vi), (tr - si) + (ui - vr))
    return result


def project(rows):
    third = (rows[0][0][1] + rows[1][1][1] + rows[2][2][1]) * (1.0 / 3.0)
    out = [rows[0][0][1] - third, rows[1][1][1] - third]
    for i, j in PAIRS:
        out.append(0.5 * (rows[i][j][0] - rows[j][i][0]))
        out.append(0.5 * (rows[i][j][1] + rows[j][i][1]))
    return out


def lane_of(shape):
    return lax.broadcasted_iota(jnp.int32, shape, 1)


def ahead_y(v):
    half = v.shape[1] // 2
    r = pltpu.roll(v, half, axis=1)
    return jnp.where(lane_of(v.shape) < half, r, pltpu.roll(r, v.shape[0] - 1, axis=0))


def behind_y(v):
    half = v.shape[1] // 2
    r = pltpu.roll(v, half, axis=1)
    return jnp.where(lane_of(v.shape) >= half, r, pltpu.roll(r, 1, axis=0))


def ahead_z(v):
    lanes = v.shape[1]
    half = lanes // 2
    inner = pltpu.roll(v, lanes - 1, axis=1)
    edge = pltpu.roll(v, half - 1, axis=1)
    return jnp.where(lane_of(v.shape) % half == half - 1, edge, inner)


def behind_z(v):
    lanes = v.shape[1]
    half = lanes // 2
    inner = pltpu.roll(v, 1, axis=1)
    edge = pltpu.roll(v, half + 1, axis=1)
    return jnp.where(lane_of(v.shape) % half == 0, edge, inner)


def halves(x):
    high = x.astype(BF16)
    low = (x - high.astype(F32)).astype(BF16)
    return high, low


def dot(x, y):
    return jnp.dot(x, y, preferred_element_type=F32)


def left_transform(stacked, left_ref):
    high, low = halves(stacked)
    return dot(left_ref[...], jnp.concatenate([high, high, low], axis=0))


def right_transform(high_ref, low_ref, right_ref, out_ref):
    high = high_ref[...]
    out_ref[...] = (
        dot(high, right_ref[0]) + dot(low_ref[...], right_ref[0]) + dot(high, right_ref[1])
    )


def forward_transform(d_ref, left_ref, right_ref, twiddle_ref, high_ref, low_ref, spec_ref, out_ref):
    slots, _, half, lanes = d_ref.shape
    parts = out_ref.shape[0] // 4
    rows = half // parts
    tr, ti = twiddle_ref[0], twiddle_ref[1]
    for slot in range(slots):
        stacked = jnp.concatenate(
            [
                jnp.concatenate([d_ref[slot, 2 * f], d_ref[slot, 2 * f + 1]], axis=0)
                for f in range(4)
            ],
            axis=1,
        )
        y = left_transform(stacked, left_ref)
        for f in range(4):
            re = y[:half, f * lanes : (f + 1) * lanes]
            im = y[half:, f * lanes : (f + 1) * lanes]
            both = jnp.concatenate([re * tr - im * ti, re * ti + im * tr], axis=1)
            high, low = halves(both)
            at = (slot * 4 + f) * half
            high_ref[at : at + half, :] = high
            low_ref[at : at + half, :] = low
    right_transform(high_ref, low_ref, right_ref, spec_ref)
    for slot in range(slots):
        for f in range(4):
            for part in range(parts):
                at = (slot * 4 + f) * half + part * rows
                for c in range(2):
                    to = (slot * 2 + c) * rows
                    out_ref[f * parts + part, to : to + rows, :] = spec_ref[
                        at : at + rows, c * lanes : (c + 1) * lanes
                    ]


def inverse_transform(in_ref, left_ref, right_ref, twiddle_ref, high_ref, low_ref, spec_ref, x_ref):
    _, slots, half, lanes = x_ref.shape
    parts = in_ref.shape[0] // 4
    rows = half // parts
    tr, ti = twiddle_ref[0], twiddle_ref[1]
    for slot in range(slots):
        for f in range(4):
            columns = []
            for c in range(2):
                to = (slot * 2 + c) * rows
                pieces = [in_ref[f * parts + part, to : to + rows, :] for part in range(parts)]
                columns.append(jnp.concatenate(pieces, axis=0))
            high, low = halves(jnp.concatenate(columns, axis=1))
            at = (slot * 4 + f) * half
            high_ref[at : at + half, :] = high
            low_ref[at : at + half, :] = low
    right_transform(high_ref, low_ref, right_ref, spec_ref)
    for slot in range(slots):
        stacks = []
        for f in range(4):
            at = (slot * 4 + f) * half
            re = spec_ref[at : at + half, :lanes]
            im = spec_ref[at : at + half, lanes:]
            stacks.append(jnp.concatenate([re * tr - im * ti, re * ti + im * tr], axis=0))
        y = left_transform(jnp.concatenate(stacks, axis=1), left_ref)
        for f in range(4):
            x_ref[2 * f, slot] = y[:half, f * lanes : (f + 1) * lanes]
            x_ref[2 * f + 1, slot] = y[half:, f * lanes : (f + 1) * lanes]


def site_rows(plane, chunk, planes):
    return pl.ds(chunk * (8 * planes) + plane, 8, stride=planes)


def load_link(links_ref, direction, rows):
    base = direction * 18
    return [
        [(links_ref[base + 3 * i + j, rows, :], links_ref[base + 9 + 3 * i + j, rows, :]) for j in range(3)]
        for i in range(3)
    ]


def load_gauge(ref, plane, rows):
    return [
        [(ref[3 * i + j, plane, rows, :], ref[9 + 3 * i + j, plane, rows, :]) for j in range(3)]
        for i in range(3)
    ]


def store_gauge(ref, plane, rows, matrix):
    for i in range(3):
        for j in range(3):
            ref[3 * i + j, plane, rows, :] = matrix[i][j][0]
            ref[9 + 3 * i + j, plane, rows, :] = matrix[i][j][1]


def chunk_loop(planes, chunks, step):
    def run(index, carry):
        step(index // chunks, index % chunks)
        return carry

    lax.fori_loop(0, planes * chunks, run, 0)


def aligned(chunk):
    return pl.ds(pl.multiple_of(chunk * 8, 8), 8)


def shift_gauge(g_ref, y_ref, z_ref):
    planes = y_ref.shape[1]

    def run(index, carry):
        for plane in range(planes):
            v = g_ref[index, plane]
            y_ref[index, plane] = ahead_y(v)
            z_ref[index, plane] = ahead_z(v)
        return carry

    lax.fori_loop(0, 18, run, 0)


def divergence(v_ref, d_ref):
    planes = v_ref.shape[2]

    def run(comp, carry):
        before = None
        for plane in range(planes):
            vx = v_ref[0, comp, plane]
            vy = v_ref[1, comp, plane]
            vz = v_ref[2, comp, plane]
            total = (behind_y(vy) - vy) + (behind_z(vz) - vz) - vx
            if before is not None:
                total = total + before
            before = vx
            d_ref[plane, comp] = total
        d_ref[planes, comp] = before
        return carry

    lax.fori_loop(0, 8, run, 0)


def start_kernel(links_ref, left_ref, right_ref, twiddle_ref, out_ref, v_ref, d_ref, high_ref, low_ref, spec_ref):
    _, _, planes, half, _ = v_ref.shape

    def step(plane, chunk):
        rows = site_rows(plane, chunk, planes)
        for direction in range(3):
            for comp, value in enumerate(project(load_link(links_ref, direction, rows))):
                v_ref[direction, comp, plane, aligned(chunk), :] = value

    chunk_loop(planes, half // 8, step)
    divergence(v_ref, d_ref)
    forward_transform(d_ref, left_ref, right_ref, twiddle_ref, high_ref, low_ref, spec_ref, out_ref)


def convolve_kernel(planes, in_ref, table_ref, out_ref):
    count = in_ref.shape[0]
    parts, offsets, rows, _ = table_ref.shape
    across = planes * count
    part = lax.axis_index("space") % parts
    step = min(8, rows)

    def run(index, carry):
        c = index // (rows // step)
        chunk = index % (rows // step)

        def at(slot):
            return pl.ds((slot * 2 + c) * rows + chunk * step, step)

        table = [table_ref[part, k, pl.ds(chunk * step, step), :] for k in range(offsets)]
        data = []
        for x in range(across):
            owner, plane = divmod(x, planes)
            value = in_ref[owner, at(plane), :]
            if plane == 0:
                value = value + in_ref[(owner - 1) % count, at(planes), :]
            data.append(value)
        for x in range(across):
            owner, plane = divmod(x, planes)
            total = table[0] * data[x] + table[offsets - 1] * data[(x + across // 2) % across]
            for k in range(1, offsets - 1):
                total = total + table[k] * (data[(x + k) % across] + data[(x - k) % across])
            out_ref[owner, at(plane), :] = total
            if plane == 0:
                out_ref[(owner - 1) % count, at(planes), :] = total
        return carry

    lax.fori_loop(0, 2 * (rows // step), run, 0)


def emit_shares(x_ref, flat_ref, share_refs, planes):
    half = x_ref.shape[2]
    count = len(share_refs)
    per = share_refs[0].shape[1]
    if per * count > planes * half:
        flat_ref[...] = jnp.zeros_like(flat_ref)
    for comp in range(8):
        for plane in range(planes):
            flat_ref[comp, pl.ds(plane, half, stride=planes), :] = x_ref[comp, plane]
    mine = lax.axis_index("tm")
    for shift in range(count):
        start = pl.multiple_of((mine + shift) % count * per, 8)
        for comp in range(8):
            share_refs[shift][comp] = flat_ref[comp, pl.ds(start, per), :]


def middle_kernel(shares, in_ref, links_ref, ileft_ref, iright_ref, itwiddle_ref, left_ref, right_ref, twiddle_ref, *rest):
    out_ref, x_ref = rest[:2]
    share_refs = rest[2 : 2 + shares]
    g_ref, y_ref, z_ref, v_ref, d_ref, high_ref, low_ref, spec_ref, flat_ref = rest[2 + shares :]
    _, slots, half, _ = x_ref.shape
    planes = slots - 1
    inverse_transform(in_ref, ileft_ref, iright_ref, itwiddle_ref, high_ref, low_ref, spec_ref, x_ref)
    emit_shares(x_ref, flat_ref, share_refs, planes)

    def raise_step(plane, chunk):
        rows = aligned(chunk)
        store_gauge(g_ref, plane, rows, exponential([x_ref[k, plane, rows, :] for k in range(8)]))

    chunk_loop(slots, half // 8, raise_step)
    shift_gauge(g_ref, y_ref, z_ref)

    def rotate_step(plane, chunk):
        rows = aligned(chunk)
        gauge = load_gauge(g_ref, plane, rows)
        link_rows = site_rows(plane, chunk, planes)
        for direction in range(3):
            link = load_link(links_ref, direction, link_rows)
            if direction == 0:
                ahead = load_gauge(g_ref, plane + 1, rows)
            else:
                ahead = load_gauge((y_ref, z_ref)[direction - 1], plane, rows)
            turned = [row_times_dagger(row_times(gauge[i], link), ahead) for i in range(3)]
            for comp, value in enumerate(project(turned)):
                v_ref[direction, comp, plane, rows, :] = value

    chunk_loop(planes, half // 8, rotate_step)
    divergence(v_ref, d_ref)
    forward_transform(d_ref, left_ref, right_ref, twiddle_ref, high_ref, low_ref, spec_ref, out_ref)


def last_transform_kernel(shares, in_ref, ileft_ref, iright_ref, itwiddle_ref, *rest):
    x_ref = rest[0]
    share_refs = rest[1 : 1 + shares]
    high_ref, low_ref, spec_ref, flat_ref = rest[1 + shares :]
    inverse_transform(in_ref, ileft_ref, iright_ref, itwiddle_ref, high_ref, low_ref, spec_ref, x_ref)
    emit_shares(x_ref, flat_ref, share_refs, x_ref.shape[1] - 1)


def total_of(first, second):
    earlier = exponential(first)
    later = exponential(second)
    return [row_times(later[i], earlier) for i in range(3)]


def finish_kernel(times, src_time_ref, src_site_ref, links_ref, first_ref, second_ref, out_ref, anchor_ref, g_ref, y_ref, z_ref):
    _, slots, half, lanes = first_ref.shape
    planes = slots - 1

    def raise_step(plane, chunk):
        rows = aligned(chunk)
        store_gauge(
            g_ref,
            plane,
            rows,
            total_of(
                [first_ref[k, plane, rows, :] for k in range(8)],
                [second_ref[k, plane, rows, :] for k in range(8)],
            ),
        )

    chunk_loop(slots, half // 8, raise_step)
    shift_gauge(g_ref, y_ref, z_ref)

    def rotate_step(plane, chunk):
        rows = aligned(chunk)
        gauge = load_gauge(g_ref, plane, rows)
        link_rows = site_rows(plane, chunk, planes)
        for direction in range(3):
            link = load_link(links_ref, direction, link_rows)
            if direction == 0:
                ahead = load_gauge(g_ref, plane + 1, rows)
            else:
                ahead = load_gauge((y_ref, z_ref)[direction - 1], plane, rows)
            for i in range(3):
                row = row_times_dagger(row_times(gauge[i], link), ahead)
                for j in range(3):
                    out_ref[direction * 18 + 3 * i + j, link_rows, :] = row[j][0]
                    out_ref[direction * 18 + 9 + 3 * i + j, link_rows, :] = row[j][1]

    chunk_loop(planes, half // 8, rotate_step)

    site = src_site_ref[0]
    volume = half * lanes
    plane = site // volume - lax.axis_index("space") * planes
    column = site % volume
    present = (src_time_ref[0] % times == lax.axis_index("tm")) & (plane >= 0) & (plane < planes)
    safe = jnp.clip(plane, 0, planes - 1)
    wanted = jnp.where(present, column % lanes, -1)
    keep = lane_of((1, lanes)) == wanted
    anchor_ref[...] = jnp.zeros_like(anchor_ref)
    for k in range(18):
        row = g_ref[k, safe, pl.ds(column // lanes, 1), :]
        anchor_ref[k : k + 1, :] = jnp.where(keep, row, 0.0)


def lane_sums(rows):
    ones = jnp.ones((8, rows.shape[1]), BF16)
    total = None
    rest = rows
    for _ in range(3):
        piece = rest.astype(BF16)
        rest = rest - piece.astype(F32)
        part = lax.dot_general(ones, piece, (((1,), (1,)), ((), ())), preferred_element_type=F32)
        total = part if total is None else total + part
    return total


def sink_kernel(times, sink_ref, anchor_ref, *rest):
    first = rest[:times]
    second = rest[times : 2 * times]
    sources = rest[2 * times : 3 * times]
    out_ref, x_ref, sum_ref = rest[3 * times :]
    per = first[0].shape[1]
    pairs = sources[0].shape[0] // 2
    groups = pairs // 3
    mine = lax.axis_index("tm")
    wanted = (mine - sink_ref[0]) % times
    for shift in range(times):

        @pl.when(wanted == shift)
        def _(shift=shift):
            x_ref[0] = first[shift][...]
            x_ref[1] = second[shift][...]

    for chunk in range(per // 8):
        rows = slice(chunk * 8, chunk * 8 + 8)
        gauge = total_of([x_ref[0, k, rows, :] for k in range(8)], [x_ref[1, k, rows, :] for k in range(8)])
        for shift in range(times):
            base = (mine - shift) % times * pairs

            def run(group, carry, shift=shift, base=base):
                column = [
                    (sources[shift][3 * group + c, rows, :], sources[shift][pairs + 3 * group + c, rows, :])
                    for c in range(3)
                ]
                for a in range(3):
                    re, im = cmul(gauge[a][0], column[0])
                    for c in (1, 2):
                        more = cmul(gauge[a][c], column[c])
                        re = re + more[0]
                        im = im + more[1]
                    to = pl.ds(pl.multiple_of((base + 3 * group + a) * 8, 8), 8)
                    if chunk:
                        re = re + sum_ref[0, to, :]
                        im = im + sum_ref[1, to, :]
                    sum_ref[0, to, :] = re
                    sum_ref[1, to, :] = im
                return carry

            lax.fori_loop(0, groups, run, 0)
    whole = SC * SC
    lanes = anchor_ref.shape[1]
    width = -(-(whole + 24) // lanes) * lanes
    rows = []
    for part in range(2):
        total = sum_ref[part, pl.ds(0, whole, stride=8), :]
        for k in range(1, 8):
            total = total + sum_ref[part, pl.ds(k, whole, stride=8), :]
        fill = jnp.zeros((width - whole - 24, lanes), F32)
        extra = anchor_ref[...] if part == 0 else jnp.zeros((24, lanes), F32)
        sums = lane_sums(jnp.concatenate([total, extra, fill], axis=0))
        for k in range(width // lanes):
            rows.append(sums[0:1, k * lanes : (k + 1) * lanes])
    block = jnp.concatenate(rows, axis=0)

    def spread(index, carry):
        out_ref[index] = block
        return carry

    lax.fori_loop(0, out_ref.shape[0], spread, 0)


def wall_kernel(scale, in_ref, out_ref):
    whole = SC * SC
    total = jnp.sum(in_ref[...], axis=0)
    half = total.shape[0] // 2
    re = jnp.concatenate([total[k : k + 1] for k in range(half)], axis=1)
    im = jnp.concatenate([total[half + k : half + k + 1] for k in range(half)], axis=1)
    width = re.shape[1]
    colour = lane_of((1, width)) // SC % 3
    out_re = jnp.zeros((1, width), F32)
    out_im = jnp.zeros((1, width), F32)
    for b in range(3):
        for c in range(3):
            at = whole + 3 * b + c
            ar = re[:, at : at + 1]
            ai = re[:, at + 9 : at + 10]
            amount = (SC * (b - c)) % width
            wr = pltpu.roll(re, amount, axis=1) if amount else re
            wi = pltpu.roll(im, amount, axis=1) if amount else im
            here = colour == b
            out_re = out_re + jnp.where(here, wr * ar + wi * ai, 0.0)
            out_im = out_im + jnp.where(here, wi * ar - wr * ai, 0.0)
    out_ref[0:1, :] = out_re[:, :whole] * scale
    out_ref[1:2, :] = out_im[:, :whole] * scale


def shape(*dims):
    return jax.ShapeDtypeStruct(dims, F32)


def call(kernel, outs, inputs, scratch, scalars=0):
    smem = pl.BlockSpec(memory_space=pltpu.SMEM)
    vmem = pl.BlockSpec(memory_space=pltpu.VMEM)
    return pl.pallas_call(
        kernel,
        out_shape=outs,
        in_specs=[smem] * scalars + [vmem] * (len(inputs) - scalars),
        out_specs=[vmem] * len(outs),
        scratch_shapes=scratch,
        compiler_params=pltpu.CompilerParams(vmem_limit_bytes=50 * 1024 * 1024),
    )(*inputs)


def body(links, propagator, sink_time, src_time, src_site):
    count = lax.axis_size("space")
    times = lax.axis_size("tm")
    planes = links.shape[5]
    side = math.isqrt(links.shape[6])
    half, lanes = side // 2, 2 * side
    across = planes * count
    slots = planes + 1
    parts = count // 4
    rows = half // parts
    sites = planes * half
    per = 8 * -(-sites // (8 * times))
    pairs = propagator.shape[1]
    mine = lax.axis_index("tm")

    forward = [jnp.asarray(t) for t in transform_tables(side, False)]
    inverse = [jnp.asarray(t) for t in transform_tables(side, True)]
    table = jnp.asarray(filter_table(side, across, parts))

    def interleave(array, lead):
        return array.reshape(lead, planes, half, lanes).transpose(0, 2, 1, 3).reshape(lead, sites, lanes)

    lattice = interleave(links, 54)
    source = interleave(propagator, 2 * pairs)
    if per * times > sites:
        source = jnp.pad(source, ((0, 0), (0, per * times - sites), (0, 0)))

    def forwarded(value, shift):
        if shift == 0:
            return value
        return lax.ppermute(value, "tm", [(i, (i + shift) % times) for i in range(times)])

    sources = []
    for shift in range(times):
        block = lax.dynamic_slice_in_dim(source, (mine + shift) % times * per, per, 1)
        sources.append(forwarded(block, shift))

    spectrum_shape = shape(count, slots * 2 * rows, lanes)
    transform_scratch = [
        VMEM((4 * slots * half, 2 * lanes), BF16),
        VMEM((4 * slots * half, 2 * lanes), BF16),
        VMEM((4 * slots * half, 2 * lanes), F32),
    ]
    divergence_scratch = [
        VMEM((3, 8, planes, half, lanes), F32),
        VMEM((slots, 8, half, lanes), F32),
    ]
    gauge_scratch = [
        VMEM((18, slots, half, lanes), F32),
        VMEM((18, planes, half, lanes), F32),
        VMEM((18, planes, half, lanes), F32),
    ]
    flat_scratch = [VMEM((8, per * times, lanes), F32)]
    algebra_shape = shape(8, slots, half, lanes)
    share_shapes = [shape(8, per, lanes)] * times

    def turn(spectrum):
        return lax.all_to_all(spectrum, "space", 0, 0, tiled=True)

    def filtered(spectrum):
        (out,) = call(
            functools.partial(convolve_kernel, planes), [spectrum_shape], [turn(spectrum), table], []
        )
        return turn(out)

    (spectrum,) = call(
        start_kernel, [spectrum_shape], [lattice] + forward, divergence_scratch + transform_scratch
    )
    spectrum, first, *shares = call(
        functools.partial(middle_kernel, times),
        [spectrum_shape, algebra_shape] + share_shapes,
        [filtered(spectrum), lattice] + inverse + forward,
        gauge_scratch + divergence_scratch + transform_scratch + flat_scratch,
    )
    first_shares = [forwarded(share, shift) for shift, share in enumerate(shares)]
    second, *shares = call(
        functools.partial(last_transform_kernel, times),
        [algebra_shape] + share_shapes,
        [filtered(spectrum)] + inverse,
        transform_scratch + flat_scratch,
    )
    second_shares = [forwarded(share, shift) for shift, share in enumerate(shares)]
    fixed, anchor = call(
        functools.partial(finish_kernel, times),
        [shape(54, sites, lanes), shape(24, lanes)],
        [src_time, src_site, lattice, first, second],
        gauge_scratch,
        scalars=2,
    )
    width = -(-(SC * SC + 24) // lanes)
    devices = count * times
    (payload,) = call(
        functools.partial(sink_kernel, times),
        [shape(devices, 2 * width, lanes)],
        [sink_time, anchor] + first_shares + second_shares + sources,
        [VMEM((2, 8, per, lanes), F32), VMEM((2, SC * SC * 8, lanes), F32)],
        scalars=1,
    )
    gathered = lax.all_to_all(payload, ("space", "tm"), 0, 0, tiled=True)
    scale = float(across * side * side) ** (-0.5)
    (wall,) = call(functools.partial(wall_kernel, scale), [shape(2, SC * SC)], [gathered], [])
    fixed = fixed.reshape(54, half, planes, lanes).transpose(0, 2, 1, 3).reshape(links.shape)
    return fixed, wall


def solution(mesh):
    placed = (
        P("tm", None, None, None, None, "space", None),
        P(None, "tm", "space", None),
        P(),
        P(),
        P(),
    )
    return jax.shard_map(
        body,
        mesh=mesh,
        in_specs=placed,
        out_specs=(P("tm", None, None, None, None, "space", None), P()),
        check_vma=False,
    )
```

profile of v0, /device:TPU:0, one launch (start us, length us, event | category | flops | bytes accessed | tf_op | source)
XLA Modules:
  0.0 133.3 jit_solution(1906466981190059448)
XLA Ops:
  0.6 1.5 %copy-done = f32[1,3,2,3,3,2,4096]{6,5,4,3,2,1,0:T(2,128)S(1)} copy-done((f32[1,3,2,3,3,2,4096]{6,5,4,3,2,1,0:T(2,128)S(1)}, f32[1,3,2,3,3,2,4096]{6,5,4,3,2,1,0:T(2,128)}, u32[]{:S(2)}) %copy-start) | copy-done | bytes 1769496
  2.1 0.9 copy-done.2
  3.1 0.8 copy-done.7
  3.8 0.8 copy-done.9
  4.6 1.5 %shard_map.131 = f32[8,96,128]{2,1,0:T(8,128)S(1)} custom-call(f32[54,64,128]{2,1,0:T(8,128)S(1)} %bitcast.15, bf16[64,192]{1,0:T(8,128)(2,1)S(1)} %copy-done.9, bf16[2,256,256]{2,1,0:T(8,128)(2,1)S(1)} %copy-done.2, f32[2,32,128]{2,1,0:T(8,128)S(1)} %copy-done.7), custom_call_target="tpu_custom_call" | custom-call | tf_op jit(solution)/shard_map/pallas_call | solution.py:631
  6.2 13.3 %all_to_all.25.in_ref = f32[8,96,128]{2,1,0:T(8,128)S(1)} all-to-all(f32[8,96,128]{2,1,0:T(8,128)S(1)} %shard_map.131), channel_id=1, replica_groups=mesh['space'=8,'tm'=4] {'space'}, dimensions={0} | all-to-all | bytes 786432 | tf_op jit(solution)/shard_map/all_to_all | solution.py:698
  19.5 1.0 shard_map.132
  20.5 3.5 %all-to-all-start.1 = ((f32[8,96,128]{2,1,0:T(8,128)}), f32[8,96,128]{2,1,0:T(8,128)S(1)}, u32[]{:S(2)}, u32[]{:S(2)}) async-start(f32[8,96,128]{2,1,0:T(8,128)} %shard_map.132), calls=%async_computation.1 | async-start | bytes 786432 | tf_op jit(solution)/shard_map/all_to_all | solution.py:698
  24.0 8.2 %all-to-all-done.1.in_ref = f32[8,96,128]{2,1,0:T(8,128)S(1)} async-done(((f32[8,96,128]{2,1,0:T(8,128)}), f32[8,96,128]{2,1,0:T(8,128)S(1)}, u32[]{:S(2)}, u32[]{:S(2)}) %all-to-all-start.1) | async-done | bytes 393248 | tf_op jit(solution)/shard_map/all_to_all | solution.py:698
  32.2 5.7 %shard_map.133 = (f32[8,96,128]{2,1,0:T(8,128)S(1)}, f32[8,3,32,128]{3,2,1,0:T(8,128)S(1)}, f32[8,16,128]{2,1,0:T(8,128)S(1)}, f32[8,16,128]{2,1,0:T(8,128)S(1)}...) custom-call(f32[8,96,128]{2,1,0:T(8,128)S(1)} %all-to-all-done.1.in_ref, f32[54,64,128]{2,1,0:T(8,128)S(1)} %bitcast.16, ...), custom_call_target="tpu_custom_call" | custom-call | tf_op jit(solution)/shard_map/pallas_call | solution.py:631
  38.0 0.7 copy-done.6
  40.6 3.5 %all-to-all-start.2 = ((f32[8,96,128]{2,1,0:T(8,128)}), f32[8,96,128]{2,1,0:T(8,128)S(1)}, u32[]{:S(2)}, u32[]{:S(2)}) async-start(f32[8,96,128]{2,1,0:T(8,128)} %copy-done.6), calls=%async_computation.2 | async-start | bytes 786432 | tf_op jit(solution)/shard_map/all_to_all | solution.py:698
  44.1 2.9 %constant_dynamic-slice_fusion = (f32[72,16,128]{2,1,0:T(8,128)}, f32[72,16,128]{2,1,0:T(8,128)}, f32[72,16,128]{2,1,0:T(8,128)}, f32[72,16,128]{2,1,0:T(8,128)S(1)}) fusion(f32[72,64,128]{2,1,0:T(8,128)} %bitcast.18, s32[]{:T(128)S(6)} %select_n.38, s32[]{:T(128)S(6)} %select_n.36, s32[]{:T(128)S(6)} %select_n.34, s32[]{:T(128)S(6)} %select_n.32), kind=kLoop, calls=%fused_computation | loop fusion | bytes 4718608 | tf_op jit(solution)/shard_map/dynamic_slice | solution.py:675
  46.9 3.6 %collective-permute-start.8 = (f32[72,16,128]{2,1,0:T(8,128)}, f32[72,16,128]{2,1,0:T(8,128)}, u32[]{:S(2)}, u32[]{:S(2)}) collective-permute-start(f32[72,16,128]{2,1,0:T(8,128)} %get-tuple-element.28), channel_id=1, source_target_pairs={{0,3},{1,0},{2,1},{3,2},{4,7},{5,4},{6,5},{7,6},{8,11},{9,8},{10,9... | collective-permute-start | bytes 1769480 | tf_op jit(solution)/shard_map/ppermute | solution.py:671
  50.5 1.0 collective-permute-start.6
  51.6 0.7 all-to-all-done.2.in_ref
  52.3 1.0 shard_map.134
  53.3 3.6 %all-to-all-start.3 = ((f32[8,96,128]{2,1,0:T(8,128)}), f32[8,96,128]{2,1,0:T(8,128)S(1)}, u32[]{:S(2)}, u32[]{:S(2)}) async-start(f32[8,96,128]{2,1,0:T(8,128)} %shard_map.134), calls=%async_computation.3 | async-start | bytes 786432 | tf_op jit(solution)/shard_map/all_to_all | solution.py:698
  56.9 2.4 %collective-permute-start = (f32[8,16,128]{2,1,0:T(8,128)}, f32[8,16,128]{2,1,0:T(8,128)}, u32[]{:S(2)}, u32[]{:S(2)}) collective-permute-start(f32[8,16,128]{2,1,0:T(8,128)} %copy-done.19), channel_id=1, source_target_pairs={{0,1},{1,2},{2,3},{3,0},{4,5},{5,6},{6,7},{7,4},{8,9},{9,10},{10,1... | collective-permute-start | bytes 196616 | tf_op jit(solution)/shard_map/ppermute | solution.py:671
  59.3 1.8 %collective-permute-start.1 = (f32[8,16,128]{2,1,0:T(8,128)}, f32[8,16,128]{2,1,0:T(8,128)}, u32[]{:S(2)}, u32[]{:S(2)}) collective-permute-start(f32[8,16,128]{2,1,0:T(8,128)} %copy-done.18), channel_id=1, source_target_pairs={{0,2},{1,3},{2,0},{3,1},{4,6},{5,7},{6,4},{7,5},{8,10},{9,11},{10,... | collective-permute-start | bytes 196616 | tf_op jit(solution)/shard_map/ppermute | solution.py:671
  61.1 4.0 %all-to-all-done.3.in_ref = f32[8,96,128]{2,1,0:T(8,128)S(1)} async-done(((f32[8,96,128]{2,1,0:T(8,128)}), f32[8,96,128]{2,1,0:T(8,128)S(1)}, u32[]{:S(2)}, u32[]{:S(2)}) %all-to-all-start.3) | async-done | bytes 393248 | tf_op jit(solution)/shard_map/all_to_all | solution.py:698
  65.1 0.8 copy-done.12
  65.9 0.8 copy-done.14
  66.6 0.7 shard_map.135
  67.3 3.7 %collective-permute-start.2 = (f32[8,16,128]{2,1,0:T(8,128)}, f32[8,16,128]{2,1,0:T(8,128)S(1)}, u32[]{:S(2)}, u32[]{:S(2)}) collective-permute-start(f32[8,16,128]{2,1,0:T(8,128)} %copy-done.17), channel_id=1, source_target_pairs={{0,3},{1,0},{2,1},{3,2},{4,7},{5,4},{6,5},{7,6},{8,11},{9,8},{10,9... | collective-permute-start | bytes 196616 | tf_op jit(solution)/shard_map/ppermute | solution.py:671
  71.0 34.2 %collective-permute-done.7.rest_10_ = f32[72,16,128]{2,1,0:T(8,128)} collective-permute-done((f32[72,16,128]{2,1,0:T(8,128)}, f32[72,16,128]{2,1,0:T(8,128)}, u32[]{:S(2)}, u32[]{:S(2)}) %collective-permute-start.7) | collective-permute-done | bytes 589856 | tf_op jit(solution)/shard_map/ppermute | solution.py:671
  105.2 3.1 %collective-permute-start.4 = (f32[8,16,128]{2,1,0:T(8,128)S(1)}, f32[8,16,128]{2,1,0:T(8,128)S(1)}, u32[]{:S(2)}, u32[]{:S(2)}) collective-permute-start(f32[8,16,128]{2,1,0:T(8,128)S(1)} %get-tuple-element.26), channel_id=1, source_target_pairs={{0,2},{1,3},{2,0},{3,1},{4,6},{5,7},{6,4},{7,5},{8,10},{9,11},{10,... | collective-permute-start | bytes 196616 | tf_op jit(solution)/shard_map/ppermute | solution.py:671
  108.3 0.8 collective-permute-start.5
  111.0 5.9 %shard_map.136 = (f32[54,64,128]{2,1,0:T(8,128)}, f32[24,128]{1,0:T(8,128)S(1)}) custom-call(s32[1]{0:T(128)S(6)} %copy.18.src_time_ref, s32[1]{0:T(128)S(6)} %copy.19.src_site_ref, f32[54,64,128]{2,1,0:T(8,128)S(1)} %bitcast.17, f32[8,3,32,128]{3,2,1,0:T(8,128)S(1)} %get-tuple-element.15.first_ref, f32[8,3,32,128]{3,2,1,0:T(8,128)S(1)} %get-tuple-element.17.second_ref), custom_call_target="tpu_custom_call" | custom-call | tf_op jit(solution)/shard_map/pallas_call | solution.py:631
  117.0 3.7 %shard_map.137 = f32[32,4,128]{2,1,0:T(4,128)S(1)} custom-call(s32[1]{0:T(128)S(6)} %copy.17.sink_ref, f32[24,128]{1,0:T(8,128)S(1)} %get-tuple-element.19.anchor_ref, f32[8,16,128]{2,1,0:T(8,128)S(1)} %copy-done.16, f32[8,16,128]{2,1,0:T(8,128)} %collective-permute-done.rest_1_, f32[8,16,128]{2,1,0:T(8,128)} %collective-permute-done.1.rest_2_, ...), custom_call_target="tpu_custom_call" | custom-call | tf_op jit(solution)/shard_map/pallas_call | solution.py:631
  120.7 11.9 %all_to_all.26.in_ref = f32[32,4,128]{2,1,0:T(4,128)S(1)} all-to-all(f32[32,4,128]{2,1,0:T(4,128)S(1)} %shard_map.137), channel_id=1, replica_groups=mesh['space'=8,'tm'=4] {'space','tm'}, dimensions={0} | all-to-all | bytes 131072 | tf_op jit(solution)/shard_map/all_to_all | solution.py:739
  132.6 0.7 shard_map.138
  (43 shorter events, 2.0 us)
Async XLA Ops:
  0.6 1.5 %copy-start = (f32[1,3,2,3,3,2,4096]{6,5,4,3,2,1,0:T(2,128)S(1)}, f32[1,3,2,3,3,2,4096]{6,5,4,3,2,1,0:T(2,128)}, u32[]{:S(2)}) copy-start(f32[1,3,2,3,3,2,4096]{6,5,4,3,2,1,0:T(2,128)} %param.12) | copy-start | bytes 5308420
  2.1 0.9 copy-start.2
  3.1 0.8 copy-start.7
  3.8 0.8 copy-start.9
  4.6 14.9 %copy-start.5 = (f32[2,9,16,128]{3,2,1,0:T(8,128)S(1)}, f32[2,9,16,128]{3,2,1,0:T(8,128)}, u32[]{:S(2)}) copy-start(f32[2,9,16,128]{3,2,1,0:T(8,128)} %constant.59.clone.table_ref) | copy-start | bytes 442372
  4.6 27.6 %copy-start.1 = (f32[1,3,2,3,3,2,4096]{6,5,4,3,2,1,0:T(2,128)S(1)}, f32[1,3,2,3,3,2,4096]{6,5,4,3,2,1,0:T(2,128)}, u32[]{:S(2)}) copy-start(f32[1,3,2,3,3,2,4096]{6,5,4,3,2,1,0:T(2,128)} %param.12) | copy-start | bytes 5308420
  4.6 27.6 %copy-start.3 = (bf16[2,256,256]{2,1,0:T(8,128)(2,1)S(1)}, bf16[2,256,256]{2,1,0:T(8,128)(2,1)}, u32[]{:S(2)}) copy-start(bf16[2,256,256]{2,1,0:T(8,128)(2,1)} %constant.54.clone.right_ref) | copy-start | bytes 786436
  4.6 27.6 %copy-start.4 = (bf16[2,256,256]{2,1,0:T(8,128)(2,1)S(1)}, bf16[2,256,256]{2,1,0:T(8,128)(2,1)}, u32[]{:S(2)}) copy-start(bf16[2,256,256]{2,1,0:T(8,128)(2,1)} %constant.57.clone.iright_ref) | copy-start | bytes 786436
  4.6 27.6 %copy-start.8 = (f32[2,32,128]{2,1,0:T(8,128)S(1)}, f32[2,32,128]{2,1,0:T(8,128)}, u32[]{:S(2)}) copy-start(f32[2,32,128]{2,1,0:T(8,128)} %constant.55.clone.twiddle_ref) | copy-start | bytes 98308
  4.6 27.6 %copy-start.10 = (bf16[64,192]{1,0:T(8,128)(2,1)S(1)}, bf16[64,192]{1,0:T(8,128)(2,1)}, u32[]{:S(2)}) copy-start(bf16[64,192]{1,0:T(8,128)(2,1)} %constant.53.clone.left_ref) | copy-start | bytes 73732
  4.6 27.6 %copy-start.11 = (f32[2,32,128]{2,1,0:T(8,128)S(1)}, f32[2,32,128]{2,1,0:T(8,128)}, u32[]{:S(2)}) copy-start(f32[2,32,128]{2,1,0:T(8,128)} %constant.58.clone.itwiddle_ref) | copy-start | bytes 98308
  4.6 27.6 %copy-start.13 = (bf16[64,192]{1,0:T(8,128)(2,1)S(1)}, bf16[64,192]{1,0:T(8,128)(2,1)}, u32[]{:S(2)}) copy-start(bf16[64,192]{1,0:T(8,128)(2,1)} %constant.56.clone.ileft_ref) | copy-start | bytes 73732
  20.5 11.7 %all-to-all-start.1 = ((f32[8,96,128]{2,1,0:T(8,128)}), f32[8,96,128]{2,1,0:T(8,128)S(1)}, u32[]{:S(2)}, u32[]{:S(2)}) async-start(f32[8,96,128]{2,1,0:T(8,128)} %shard_map.132), calls=%async_computation.1 | async-start | bytes 786432 | tf_op jit(solution)/shard_map/all_to_all | solution.py:698
  37.9 0.7 copy-start.6
  38.7 0.6 copy-start.15
  39.3 0.6 copy-start.19
  39.9 0.6 copy-start.17
  39.9 0.7 copy-start.18
  40.6 11.7 %all-to-all-start.2 = ((f32[8,96,128]{2,1,0:T(8,128)}), f32[8,96,128]{2,1,0:T(8,128)S(1)}, u32[]{:S(2)}, u32[]{:S(2)}) async-start(f32[8,96,128]{2,1,0:T(8,128)} %copy-done.6), calls=%async_computation.2 | async-start | bytes 786432 | tf_op jit(solution)/shard_map/all_to_all | solution.py:698
  46.9 20.4 %collective-permute-start.8 = (f32[72,16,128]{2,1,0:T(8,128)}, f32[72,16,128]{2,1,0:T(8,128)}, u32[]{:S(2)}, u32[]{:S(2)}) collective-permute-start(f32[72,16,128]{2,1,0:T(8,128)} %get-tuple-element.28), channel_id=1, source_target_pairs={{0,3},{1,0},{2,1},{3,2},{4,7},{5,4},{6,5},{7,6},{8,11},{9,8},{10,9... | collective-permute-start | bytes 1769480 | tf_op jit(solution)/shard_map/ppermute | solution.py:671
  50.5 54.7 %collective-permute-start.7 = (f32[72,16,128]{2,1,0:T(8,128)}, f32[72,16,128]{2,1,0:T(8,128)}, u32[]{:S(2)}, u32[]{:S(2)}) collective-permute-start(f32[72,16,128]{2,1,0:T(8,128)} %get-tuple-element.29), channel_id=1, source_target_pairs={{0,2},{1,3},{2,0},{3,1},{4,6},{5,7},{6,4},{7,5},{8,10},{9,11},{10,... | collective-permute-start | bytes 1769480 | tf_op jit(solution)/shard_map/ppermute | solution.py:671
  50.5 54.7 %collective-permute-start.6 = (f32[72,16,128]{2,1,0:T(8,128)}, f32[72,16,128]{2,1,0:T(8,128)}, u32[]{:S(2)}, u32[]{:S(2)}) collective-permute-start(f32[72,16,128]{2,1,0:T(8,128)} %get-tuple-element.30), channel_id=1, source_target_pairs={{0,1},{1,2},{2,3},{3,0},{4,5},{5,6},{6,7},{7,4},{8,9},{9,10},{10,1... | collective-permute-start | bytes 1769480 | tf_op jit(solution)/shard_map/ppermute | solution.py:671
  53.3 63.7 %copy-start.16 = (f32[8,16,128]{2,1,0:T(8,128)S(1)}, f32[8,16,128]{2,1,0:T(8,128)}, u32[]{:S(2)}) copy-start(f32[8,16,128]{2,1,0:T(8,128)} %copy-done.15) | copy-start | bytes 196612
  53.3 11.8 %all-to-all-start.3 = ((f32[8,96,128]{2,1,0:T(8,128)}), f32[8,96,128]{2,1,0:T(8,128)S(1)}, u32[]{:S(2)}, u32[]{:S(2)}) async-start(f32[8,96,128]{2,1,0:T(8,128)} %shard_map.134), calls=%async_computation.3 | async-start | bytes 786432 | tf_op jit(solution)/shard_map/all_to_all | solution.py:698
  56.9 51.4 %collective-permute-start = (f32[8,16,128]{2,1,0:T(8,128)}, f32[8,16,128]{2,1,0:T(8,128)}, u32[]{:S(2)}, u32[]{:S(2)}) collective-permute-start(f32[8,16,128]{2,1,0:T(8,128)} %copy-done.19), channel_id=1, source_target_pairs={{0,1},{1,2},{2,3},{3,0},{4,5},{5,6},{6,7},{7,4},{8,9},{9,10},{10,1... | collective-permute-start | bytes 196616 | tf_op jit(solution)/shard_map/ppermute | solution.py:671
  59.3 57.7 %collective-permute-start.1 = (f32[8,16,128]{2,1,0:T(8,128)}, f32[8,16,128]{2,1,0:T(8,128)}, u32[]{:S(2)}, u32[]{:S(2)}) collective-permute-start(f32[8,16,128]{2,1,0:T(8,128)} %copy-done.18), channel_id=1, source_target_pairs={{0,2},{1,3},{2,0},{3,1},{4,6},{5,7},{6,4},{7,5},{8,10},{9,11},{10,... | collective-permute-start | bytes 196616 | tf_op jit(solution)/shard_map/ppermute | solution.py:671
  65.1 0.8 copy-start.12
  65.9 0.8 copy-start.14
  67.3 49.7 %collective-permute-start.2 = (f32[8,16,128]{2,1,0:T(8,128)}, f32[8,16,128]{2,1,0:T(8,128)S(1)}, u32[]{:S(2)}, u32[]{:S(2)}) collective-permute-start(f32[8,16,128]{2,1,0:T(8,128)} %copy-done.17), channel_id=1, source_target_pairs={{0,3},{1,0},{2,1},{3,2},{4,7},{5,4},{6,5},{7,6},{8,11},{9,8},{10,9... | collective-permute-start | bytes 196616 | tf_op jit(solution)/shard_map/ppermute | solution.py:671
  105.2 11.8 %collective-permute-start.3 = (f32[8,16,128]{2,1,0:T(8,128)S(1)}, f32[8,16,128]{2,1,0:T(8,128)S(1)}, u32[]{:S(2)}, u32[]{:S(2)}) collective-permute-start(f32[8,16,128]{2,1,0:T(8,128)S(1)} %get-tuple-element.25), channel_id=1, source_target_pairs={{0,1},{1,2},{2,3},{3,0},{4,5},{5,6},{6,7},{7,4},{8,9},{9,10},{10,1... | collective-permute-start | bytes 196616 | tf_op jit(solution)/shard_map/ppermute | solution.py:671
  105.2 11.8 %collective-permute-start.4 = (f32[8,16,128]{2,1,0:T(8,128)S(1)}, f32[8,16,128]{2,1,0:T(8,128)S(1)}, u32[]{:S(2)}, u32[]{:S(2)}) collective-permute-start(f32[8,16,128]{2,1,0:T(8,128)S(1)} %get-tuple-element.26), channel_id=1, source_target_pairs={{0,2},{1,3},{2,0},{3,1},{4,6},{5,7},{6,4},{7,5},{8,10},{9,11},{10,... | collective-permute-start | bytes 196616 | tf_op jit(solution)/shard_map/ppermute | solution.py:671
  108.3 8.7 %collective-permute-start.5 = (f32[8,16,128]{2,1,0:T(8,128)S(1)}, f32[8,16,128]{2,1,0:T(8,128)S(1)}, u32[]{:S(2)}, u32[]{:S(2)}) collective-permute-start(f32[8,16,128]{2,1,0:T(8,128)S(1)} %get-tuple-element.27), channel_id=1, source_target_pairs={{0,3},{1,0},{2,1},{3,2},{4,7},{5,4},{6,5},{7,6},{8,11},{9,8},{10,9... | collective-permute-start | bytes 196616 | tf_op jit(solution)/shard_map/ppermute | solution.py:671
where the time goes:
time: 134 us; the launch traced here: 133 us
  waiting for transfers between devices  47.2 us (35%)
  starting transfers between devices  26.9 us (20%)
  blocking collectives  25.2 us (19%)
  Pallas kernels  20.2 us (15%)
  local copies, waits for them, and re-layouts  11 us (8%)
  between operations  2.83 us (2%)
    ppermute x9, waiting for transfers between devices, forwarded(): lax.ppermute(value, 'tm', [(i, (i + shift) % times) for i in range(times)])  34.2 us
    pallas_call x8, Pallas kernels, call(): pl.pallas_call(kernel, out_shape=outs, in_specs=[smem] * scalars + [vmem]...  20.2 us
    ppermute x9, starting transfers between devices, forwarded(): lax.ppermute(value, 'tm', [(i, (i + shift) % times) for i in range(times)])  16.4 us
    all_to_all x1, blocking collectives, turn(): return lax.all_to_all(spectrum, 'space', 0, 0, tiled=True)  13.3 us
    all_to_all x3, waiting for transfers between devices, turn(): return lax.all_to_all(spectrum, 'space', 0, 0, tiled=True)  13 us
    all_to_all x1, blocking collectives, body(): gathered = lax.all_to_all(payload, ('space', 'tm'), 0, 0, tiled=True)  11.9 us
    all_to_all x3, starting transfers between devices, turn(): return lax.all_to_all(spectrum, 'space', 0, 0, tiled=True)  10.5 us
    unnamed x40, local copies, waits for them, and re-layouts  8.14 us
  transfers between devices with their start and end apart: 12, of which 4 were waited for; matrix products, arithmetic and copies ran while one was open for 2% of the time, Pallas kernels for 6%

commit v1 on v0

--- a/solution.py
+++ b/solution.py
@@ -9,6 +9,7 @@
 from jax.experimental.pallas import tpu as pltpu
 from jax.sharding import PartitionSpec as P
 
+
 SC = 12
 STEP_SIZE = 0.08
 PEAK_SQUARE = 12.0
@@ -29,25 +30,23 @@
 
 
 @functools.lru_cache(None)
-def transform_tables(side, inverse):
+def transform_table(side, inverse):
     half = side // 2
     sign = 1.0 if inverse else -1.0
     k = np.arange(half)
-    row_phase = sign * 2.0 * np.pi * np.outer(k, k) / half
-    rows_left = as_real(np.cos(row_phase), -np.sin(row_phase))
-    high, low = split_table(rows_left)
-    left = np.concatenate([high, low, high], axis=1)
+    twist = np.exp(1j * sign * 2.0 * np.pi * k / side)
+    even = np.exp(1j * sign * 2.0 * np.pi * np.outer(k, k) / half)
+    odd = even * (twist[None, :] if inverse else twist[:, None])
+    left = np.concatenate([as_real(m.real, -m.imag) for m in (even, odd)], axis=0)
+    high, low = split_table(left)
+    fill = np.zeros((left.shape[0], 4 * side - 3 * side), high.dtype)
+    left = np.concatenate([high, low, high, fill], axis=1)
     z = np.arange(side)
     depth_phase = sign * 2.0 * np.pi * np.outer(z, z) / side
     parity = np.array([[1.0, 1.0], [1.0, -1.0]])
     right = as_real(np.kron(parity, np.cos(depth_phase)), np.kron(parity, np.sin(depth_phase)))
     high, low = split_table(right)
-    right = np.stack([high, low])
-    twiddle_phase = sign * 2.0 * np.pi * k / side
-    lanes = np.arange(2 * side) >= side
-    phase = np.where(lanes[None, :], twiddle_phase[:, None], 0.0)
-    twiddle = np.stack([np.cos(phase), np.sin(phase)]).astype(np.float32)
-    return left, right, twiddle
+    return np.concatenate([high, low, left], axis=0)
 
 
 @functools.lru_cache(None)
@@ -207,23 +206,28 @@
     return jnp.dot(x, y, preferred_element_type=F32)
 
 
-def left_transform(stacked, left_ref):
+def left_transform(stacked, table_ref):
     high, low = halves(stacked)
-    return dot(left_ref[...], jnp.concatenate([high, high, low], axis=0))
-
-
-def right_transform(high_ref, low_ref, right_ref, out_ref):
+    depth, width = stacked.shape
+    at = 2 * table_ref.shape[1]
+    both = dot(
+        table_ref[at : at + 2 * depth, : 3 * depth], jnp.concatenate([high, high, low], axis=0)
+    )
+    even = lane_of((depth, width)) % (2 * depth) < depth
+    return jnp.where(even, both[:depth], both[depth:])
+
+
+def right_transform(high_ref, low_ref, table_ref, out_ref):
+    size = table_ref.shape[1]
     high = high_ref[...]
-    out_ref[...] = (
-        dot(high, right_ref[0]) + dot(low_ref[...], right_ref[0]) + dot(high, right_ref[1])
-    )
-
-
-def forward_transform(d_ref, left_ref, right_ref, twiddle_ref, high_ref, low_ref, spec_ref, out_ref):
+    first = table_ref[:size]
+    out_ref[...] = dot(high, first) + dot(low_ref[...], first) + dot(high, table_ref[size : 2 * size])
+
+
+def forward_transform(d_ref, table_ref, high_ref, low_ref, spec_ref, out_ref):
     slots, _, half, lanes = d_ref.shape
     parts = out_ref.shape[0] // 4
     rows = half // parts
-    tr, ti = twiddle_ref[0], twiddle_ref[1]
     for slot in range(slots):
         stacked = jnp.concatenate(
             [
@@ -232,16 +236,15 @@
             ],
             axis=1,
         )
-        y = left_transform(stacked, left_ref)
+        y = left_transform(stacked, table_ref)
         for f in range(4):
             re = y[:half, f * lanes : (f + 1) * lanes]
             im = y[half:, f * lanes : (f + 1) * lanes]
-            both = jnp.concatenate([re * tr - im * ti, re * ti + im * tr], axis=1)
-            high, low = halves(both)
+            high, low = halves(jnp.concatenate([re, im], axis=1))
             at = (slot * 4 + f) * half
             high_ref[at : at + half, :] = high
             low_ref[at : at + half, :] = low
-    right_transform(high_ref, low_ref, right_ref, spec_ref)
+    right_transform(high_ref, low_ref, table_ref, spec_ref)
     for slot in range(slots):
         for f in range(4):
             for part in range(parts):
@@ -253,11 +256,10 @@
                     ]
 
 
-def inverse_transform(in_ref, left_ref, right_ref, twiddle_ref, high_ref, low_ref, spec_ref, x_ref):
+def inverse_transform(in_ref, table_ref, high_ref, low_ref, spec_ref, x_ref):
     _, slots, half, lanes = x_ref.shape
     parts = in_ref.shape[0] // 4
     rows = half // parts
-    tr, ti = twiddle_ref[0], twiddle_ref[1]
     for slot in range(slots):
         for f in range(4):
             columns = []
@@ -269,15 +271,15 @@
             at = (slot * 4 + f) * half
             high_ref[at : at + half, :] = high
             low_ref[at : at + half, :] = low
-    right_transform(high_ref, low_ref, right_ref, spec_ref)
+    right_transform(high_ref, low_ref, table_ref, spec_ref)
     for slot in range(slots):
         stacks = []
         for f in range(4):
             at = (slot * 4 + f) * half
-            re = spec_ref[at : at + half, :lanes]
-            im = spec_ref[at : at + half, lanes:]
-            stacks.append(jnp.concatenate([re * tr - im * ti, re * ti + im * tr], axis=0))
-        y = left_transform(jnp.concatenate(stacks, axis=1), left_ref)
+            stacks.append(
+                jnp.concatenate([spec_ref[at : at + half, :lanes], spec_ref[at : at + half, lanes:]], axis=0)
+            )
+        y = left_transform(jnp.concatenate(stacks, axis=1), table_ref)
         for f in range(4):
             x_ref[2 * f, slot] = y[:half, f * lanes : (f + 1) * lanes]
             x_ref[2 * f + 1, slot] = y[half:, f * lanes : (f + 1) * lanes]
@@ -354,18 +356,44 @@
     lax.fori_loop(0, 8, run, 0)
 
 
-def start_kernel(links_ref, left_ref, right_ref, twiddle_ref, out_ref, v_ref, d_ref, high_ref, low_ref, spec_ref):
+def start_kernel(times, links_any, table_any, source_any, out_ref, *rest):
+    cut_refs = rest[: times - 1]
+    held_ref, links_ref, table_ref, v_ref, d_ref, high_ref, low_ref, spec_ref, sems, cut_sems = rest[times - 1 :]
     _, _, planes, half, _ = v_ref.shape
-
-    def step(plane, chunk):
-        rows = site_rows(plane, chunk, planes)
-        for direction in range(3):
+    per = held_ref.shape[2]
+    reads, writes = [], []
+    for shift, cut in enumerate(cut_refs, 1):
+        rows = pl.ds(share_start(shift, times, per), per)
+        reads.append(
+            pltpu.make_async_copy(source_any.at[:, rows, :], held_ref.at[shift - 1], cut_sems.at[0, shift - 1])
+        )
+        writes.append(pltpu.make_async_copy(held_ref.at[shift - 1], cut, cut_sems.at[1, shift - 1]))
+    copies = [
+        pltpu.make_async_copy(
+            links_any.at[pl.ds(18 * direction, 18)], links_ref.at[pl.ds(18 * direction, 18)], sems.at[direction]
+        )
+        for direction in range(3)
+    ]
+    copies.append(pltpu.make_async_copy(table_any, table_ref, sems.at[3]))
+    for copy in copies + reads:
+        copy.start()
+    for direction in range(3):
+        copies[direction].wait()
+
+        def step(plane, chunk, direction=direction):
+            rows = site_rows(plane, chunk, planes)
             for comp, value in enumerate(project(load_link(links_ref, direction, rows))):
                 v_ref[direction, comp, plane, aligned(chunk), :] = value
 
-    chunk_loop(planes, half // 8, step)
+        chunk_loop(planes, half // 8, step)
+    for read, write in zip(reads, writes):
+        read.wait()
+        write.start()
     divergence(v_ref, d_ref)
-    forward_transform(d_ref, left_ref, right_ref, twiddle_ref, high_ref, low_ref, spec_ref, out_ref)
+    copies[3].wait()
+    forward_transform(d_ref, table_ref, high_ref, low_ref, spec_ref, out_ref)
+    for write in writes:
+        write.wait()
 
 
 def convolve_kernel(planes, in_ref, table_ref, out_ref):
@@ -403,30 +431,37 @@
     lax.fori_loop(0, 2 * (rows // step), run, 0)
 
 
-def emit_shares(x_ref, flat_ref, share_refs, planes):
+def flatten_shares(x_ref, flat_ref, planes):
     half = x_ref.shape[2]
-    count = len(share_refs)
-    per = share_refs[0].shape[1]
-    if per * count > planes * half:
+    if flat_ref.shape[1] > planes * half:
         flat_ref[...] = jnp.zeros_like(flat_ref)
     for comp in range(8):
         for plane in range(planes):
             flat_ref[comp, pl.ds(plane, half, stride=planes), :] = x_ref[comp, plane]
-    mine = lax.axis_index("tm")
-    for shift in range(count):
-        start = pl.multiple_of((mine + shift) % count * per, 8)
-        for comp in range(8):
-            share_refs[shift][comp] = flat_ref[comp, pl.ds(start, per), :]
-
-
-def middle_kernel(shares, in_ref, links_ref, ileft_ref, iright_ref, itwiddle_ref, left_ref, right_ref, twiddle_ref, *rest):
-    out_ref, x_ref = rest[:2]
+
+
+def share_start(shift, count, per):
+    return pl.multiple_of((lax.axis_index("tm") + shift) % count * per, 8)
+
+
+def middle_kernel(shares, in_ref, links_ref, inverse_ref, forward_ref, *rest):
+    out_ref, x_any = rest[:2]
     share_refs = rest[2 : 2 + shares]
-    g_ref, y_ref, z_ref, v_ref, d_ref, high_ref, low_ref, spec_ref, flat_ref = rest[2 + shares :]
+    x_ref, g_ref, y_ref, z_ref, v_ref, d_ref, high_ref, low_ref, spec_ref, flat_ref, sems = rest[2 + shares :]
     _, slots, half, _ = x_ref.shape
     planes = slots - 1
-    inverse_transform(in_ref, ileft_ref, iright_ref, itwiddle_ref, high_ref, low_ref, spec_ref, x_ref)
-    emit_shares(x_ref, flat_ref, share_refs, planes)
+    per = share_refs[0].shape[1]
+    inverse_transform(in_ref, inverse_ref, high_ref, low_ref, spec_ref, x_ref)
+    flatten_shares(x_ref, flat_ref, planes)
+    copies = [
+        pltpu.make_async_copy(
+            flat_ref.at[:, pl.ds(share_start(shift, shares, per), per), :], share_refs[shift], sems.at[shift]
+        )
+        for shift in range(shares)
+    ]
+    copies.append(pltpu.make_async_copy(x_ref, x_any, sems.at[shares]))
+    for copy in copies:
+        copy.start()
 
     def raise_step(plane, chunk):
         rows = aligned(chunk)
@@ -451,15 +486,19 @@
 
     chunk_loop(planes, half // 8, rotate_step)
     divergence(v_ref, d_ref)
-    forward_transform(d_ref, left_ref, right_ref, twiddle_ref, high_ref, low_ref, spec_ref, out_ref)
-
-
-def last_transform_kernel(shares, in_ref, ileft_ref, iright_ref, itwiddle_ref, *rest):
-    x_ref = rest[0]
-    share_refs = rest[1 : 1 + shares]
-    high_ref, low_ref, spec_ref, flat_ref = rest[1 + shares :]
-    inverse_transform(in_ref, ileft_ref, iright_ref, itwiddle_ref, high_ref, low_ref, spec_ref, x_ref)
-    emit_shares(x_ref, flat_ref, share_refs, x_ref.shape[1] - 1)
+    forward_transform(d_ref, forward_ref, high_ref, low_ref, spec_ref, out_ref)
+    for copy in copies:
+        copy.wait()
+
+
+def last_transform_kernel(in_ref, inverse_ref, x_ref, *rest):
+    share_refs = rest[:-4]
+    high_ref, low_ref, spec_ref, flat_ref = rest[-4:]
+    per = share_refs[0].shape[1]
+    inverse_transform(in_ref, inverse_ref, high_ref, low_ref, spec_ref, x_ref)
+    flatten_shares(x_ref, flat_ref, x_ref.shape[1] - 1)
+    for to, share_ref in enumerate(share_refs):
+        share_ref[...] = flat_ref[:, to * per : (to + 1) * per, :]
 
 
 def total_of(first, second):
@@ -468,9 +507,17 @@
     return [row_times(later[i], earlier) for i in range(3)]
 
 
-def finish_kernel(times, src_time_ref, src_site_ref, links_ref, first_ref, second_ref, out_ref, anchor_ref, g_ref, y_ref, z_ref):
-    _, slots, half, lanes = first_ref.shape
+def finish_kernel(links_any, first_any, second_ref, out_any, g_ref, y_ref, z_ref, links_ref, first_ref, out_ref, sems):
+    _, slots, half, _ = first_ref.shape
     planes = slots - 1
+    chunks = half // 8
+    copies = [
+        pltpu.make_async_copy(first_any, first_ref, sems.at[0]),
+        pltpu.make_async_copy(links_any, links_ref, sems.at[1]),
+    ]
+    for copy in copies:
+        copy.start()
+    copies[0].wait()
 
     def raise_step(plane, chunk):
         rows = aligned(chunk)
@@ -486,8 +533,13 @@
 
     chunk_loop(slots, half // 8, raise_step)
     shift_gauge(g_ref, y_ref, z_ref)
-
-    def rotate_step(plane, chunk):
+    copies[1].wait()
+
+    def piece(chunk):
+        rows = pl.ds(pl.multiple_of(chunk * (8 * planes), 8), 8 * planes)
+        return pltpu.make_async_copy(out_ref.at[:, rows, :], out_any.at[:, rows, :], sems.at[2 + chunk])
+
+    def rotate_step(chunk, plane):
         rows = aligned(chunk)
         gauge = load_gauge(g_ref, plane, rows)
         link_rows = site_rows(plane, chunk, planes)
@@ -503,20 +555,14 @@
                     out_ref[direction * 18 + 3 * i + j, link_rows, :] = row[j][0]
                     out_ref[direction * 18 + 9 + 3 * i + j, link_rows, :] = row[j][1]
 
-    chunk_loop(planes, half // 8, rotate_step)
-
-    site = src_site_ref[0]
-    volume = half * lanes
-    plane = site // volume - lax.axis_index("space") * planes
-    column = site % volume
-    present = (src_time_ref[0] % times == lax.axis_index("tm")) & (plane >= 0) & (plane < planes)
-    safe = jnp.clip(plane, 0, planes - 1)
-    wanted = jnp.where(present, column % lanes, -1)
-    keep = lane_of((1, lanes)) == wanted
-    anchor_ref[...] = jnp.zeros_like(anchor_ref)
-    for k in range(18):
-        row = g_ref[k, safe, pl.ds(column // lanes, 1), :]
-        anchor_ref[k : k + 1, :] = jnp.where(keep, row, 0.0)
+        @pl.when(plane == planes - 1)
+        def _():
+            piece(chunk).start()
+
+    chunk_loop(chunks, planes, rotate_step)
+
+    for chunk in range(chunks):
+        piece(chunk).wait()
 
 
 def lane_sums(rows):
@@ -531,63 +577,113 @@
     return total
 
 
-def sink_kernel(times, sink_ref, anchor_ref, *rest):
-    first = rest[:times]
-    second = rest[times : 2 * times]
-    sources = rest[2 * times : 3 * times]
-    out_ref, x_ref, sum_ref = rest[3 * times :]
-    per = first[0].shape[1]
-    pairs = sources[0].shape[0] // 2
+def sink_kernel(times, split, scalar_ref, first_any, second_ref, own_early_ref, *rest):
+    early = (own_early_ref,) + rest[: times - 1]
+    own = rest[times - 1 : times - 1 + split]
+    late = rest[times - 1 + split : 2 * times - 2 + split]
+    sources_any = rest[2 * times - 2 + split : 2 * times - 2 + 2 * split]
+    out_ref, source_ref, x_ref, gauge_ref, sum_ref, before_ref, anchor_ref, sems = rest[2 * times - 2 + 2 * split :]
+    per = early[0].shape[1]
+    pairs = source_ref.shape[1] // 2
     groups = pairs // 3
+    _, slots, half, lanes = second_ref.shape
+    planes = slots - 1
     mine = lax.axis_index("tm")
-    wanted = (mine - sink_ref[0]) % times
+    local = sources_any[0].at[:, pl.ds(share_start(0, split, per), per), :]
+    sink = scalar_ref[0]
+    column = scalar_ref[2] % (half * lanes)
+    plane = scalar_ref[2] // (half * lanes) - lax.axis_index("space") * planes
+    present = (scalar_ref[1] == mine) & (plane >= 0) & (plane < planes)
+    safe = jnp.clip(plane, 0, planes - 1)
+    row = column // lanes
+    block = pl.ds(pl.multiple_of(row // 8 * 8, 8), 8)
+    before = pltpu.make_async_copy(first_any.at[:, safe, block, :], before_ref, sems.at[split])
+    copies = [
+        pltpu.make_async_copy(sources_any[shift] if shift else local, source_ref.at[shift], sems.at[shift])
+        for shift in range(split)
+    ]
+    before.start()
+    for copy in copies:
+        copy.start()
+    wanted = (mine - sink) % times
     for shift in range(times):
 
         @pl.when(wanted == shift)
         def _(shift=shift):
-            x_ref[0] = first[shift][...]
-            x_ref[1] = second[shift][...]
-
-    for chunk in range(per // 8):
+            x_ref[0] = early[shift][...]
+
+    for at in range(split):
+
+        @pl.when((mine == sink) & (mine % split == at))
+        def _(at=at):
+            x_ref[1] = own[at][...]
+
+    for at in range(times - 1):
+
+        @pl.when((mine != sink) & (jnp.where(mine > sink, mine - 1, mine) == at))
+        def _(at=at):
+            x_ref[1] = late[at][...]
+
+    chunks = per // 8
+    for chunk in range(chunks):
         rows = slice(chunk * 8, chunk * 8 + 8)
         gauge = total_of([x_ref[0, k, rows, :] for k in range(8)], [x_ref[1, k, rows, :] for k in range(8)])
-        for shift in range(times):
-            base = (mine - shift) % times * pairs
-
-            def run(group, carry, shift=shift, base=base):
+        for i in range(3):
+            for j in range(3):
+                gauge_ref[3 * i + j, rows, :] = gauge[i][j][0]
+                gauge_ref[9 + 3 * i + j, rows, :] = gauge[i][j][1]
+    sum_ref[...] = jnp.zeros_like(sum_ref)
+    for shift in range(split):
+        copies[shift].wait()
+        base = (mine - mine % split + (mine - shift) % split) * pairs
+
+        def run(group, carry, shift=shift, base=base):
+            sums = [None] * 3
+            for chunk in range(chunks):
+                rows = slice(chunk * 8, chunk * 8 + 8)
                 column = [
-                    (sources[shift][3 * group + c, rows, :], sources[shift][pairs + 3 * group + c, rows, :])
+                    (
+                        source_ref[shift, 3 * group + c, rows, :],
+                        source_ref[shift, pairs + 3 * group + c, rows, :],
+                    )
                     for c in range(3)
                 ]
                 for a in range(3):
-                    re, im = cmul(gauge[a][0], column[0])
-                    for c in (1, 2):
-                        more = cmul(gauge[a][c], column[c])
-                        re = re + more[0]
-                        im = im + more[1]
-                    to = pl.ds(pl.multiple_of((base + 3 * group + a) * 8, 8), 8)
-                    if chunk:
-                        re = re + sum_ref[0, to, :]
-                        im = im + sum_ref[1, to, :]
-                    sum_ref[0, to, :] = re
-                    sum_ref[1, to, :] = im
-                return carry
-
-            lax.fori_loop(0, groups, run, 0)
+                    for c in range(3):
+                        part = cmul(
+                            (gauge_ref[3 * a + c, rows, :], gauge_ref[9 + 3 * a + c, rows, :]), column[c]
+                        )
+                        sums[a] = part if sums[a] is None else (sums[a][0] + part[0], sums[a][1] + part[1])
+            for a in range(3):
+                to = pl.ds(pl.multiple_of((base + 3 * group + a) * 8, 8), 8)
+                sum_ref[0, to, :] = sums[a][0]
+                sum_ref[1, to, :] = sums[a][1]
+            return carry
+
+        lax.fori_loop(0, groups, run, 0, unroll=2 if groups % 2 == 0 else 1)
+    before.wait()
+    total = total_of([before_ref[k] for k in range(8)], [second_ref[k, safe, block, :] for k in range(8)])
+    wide = (8, lanes)
+    keep = (lane_of(wide) == jnp.where(present, column % lanes, -1)) & (
+        lax.broadcasted_iota(jnp.int32, wide, 0) == row % 8
+    )
+    anchor_ref[...] = jnp.zeros_like(anchor_ref)
+    for k in range(18):
+        value = total[k % 9 // 3][k % 3][k // 9]
+        anchor_ref[k : k + 1, :] = jnp.sum(jnp.where(keep, value, 0.0), axis=0, keepdims=True)
     whole = SC * SC
-    lanes = anchor_ref.shape[1]
     width = -(-(whole + 24) // lanes) * lanes
-    rows = []
+    pieces = []
     for part in range(2):
         total = sum_ref[part, pl.ds(0, whole, stride=8), :]
         for k in range(1, 8):
             total = total + sum_ref[part, pl.ds(k, whole, stride=8), :]
-        fill = jnp.zeros((width - whole - 24, lanes), F32)
         extra = anchor_ref[...] if part == 0 else jnp.zeros((24, lanes), F32)
-        sums = lane_sums(jnp.concatenate([total, extra, fill], axis=0))
-        for k in range(width // lanes):
-            rows.append(sums[0:1, k * lanes : (k + 1) * lanes])
-    block = jnp.concatenate(rows, axis=0)
+        pieces += [total, extra, jnp.zeros((width - whole - 24, lanes), F32)]
+    sums = lane_sums(jnp.concatenate(pieces, axis=0))
+    block = jnp.concatenate(
+        [sums[0:1, k * lanes : (k + 1) * lanes] for k in range(2 * width // lanes)], axis=0
+    )
 
     def spread(index, carry):
         out_ref[index] = block
@@ -625,16 +721,28 @@
     return jax.ShapeDtypeStruct(dims, F32)
 
 
-def call(kernel, outs, inputs, scratch, scalars=0):
-    smem = pl.BlockSpec(memory_space=pltpu.SMEM)
-    vmem = pl.BlockSpec(memory_space=pltpu.VMEM)
+SMEM_SPEC = pl.BlockSpec(memory_space=pltpu.SMEM)
+VMEM_SPEC = pl.BlockSpec(memory_space=pltpu.VMEM)
+ANY_SPEC = pl.BlockSpec(memory_space=pl.ANY)
+HBM_SPEC = pl.BlockSpec(memory_space=pltpu.HBM)
+
+
+def call(kernel, outs, out_specs, inputs, in_specs, scratch):
+    inputs = [
+        pltpu.with_memory_space_constraint(x, pltpu.HBM) if spec is HBM_SPEC else x
+        for x, spec in zip(inputs, in_specs)
+    ]
+    outs = [
+        pltpu.HBM(out.shape, out.dtype) if spec is HBM_SPEC else out
+        for out, spec in zip(outs, out_specs)
+    ]
     return pl.pallas_call(
         kernel,
         out_shape=outs,
-        in_specs=[smem] * scalars + [vmem] * (len(inputs) - scalars),
-        out_specs=[vmem] * len(outs),
+        in_specs=in_specs,
+        out_specs=out_specs,
         scratch_shapes=scratch,
-        compiler_params=pltpu.CompilerParams(vmem_limit_bytes=50 * 1024 * 1024),
+        compiler_params=pltpu.CompilerParams(vmem_limit_bytes=20 * 1024 * 1024),
     )(*inputs)
 
 
@@ -649,31 +757,24 @@
     parts = count // 4
     rows = half // parts
     sites = planes * half
-    per = 8 * -(-sites // (8 * times))
+    split = 2 if times % 2 == 0 else 1
+    per = 8 * -(-sites // (8 * split))
     pairs = propagator.shape[1]
-    mine = lax.axis_index("tm")
-
-    forward = [jnp.asarray(t) for t in transform_tables(side, False)]
-    inverse = [jnp.asarray(t) for t in transform_tables(side, True)]
+
+    forward = jnp.asarray(transform_table(side, False))
+    inverse = jnp.asarray(transform_table(side, True))
     table = jnp.asarray(filter_table(side, across, parts))
 
     def interleave(array, lead):
         return array.reshape(lead, planes, half, lanes).transpose(0, 2, 1, 3).reshape(lead, sites, lanes)
 
     lattice = interleave(links, 54)
-    source = interleave(propagator, 2 * pairs)
-    if per * times > sites:
-        source = jnp.pad(source, ((0, 0), (0, per * times - sites), (0, 0)))
 
     def forwarded(value, shift):
-        if shift == 0:
-            return value
         return lax.ppermute(value, "tm", [(i, (i + shift) % times) for i in range(times)])
 
-    sources = []
-    for shift in range(times):
-        block = lax.dynamic_slice_in_dim(source, (mine + shift) % times * per, per, 1)
-        sources.append(forwarded(block, shift))
+    def within(i, shift):
+        return i - i % split + (i + shift) % split
 
     spectrum_shape = shape(count, slots * 2 * rows, lanes)
     transform_scratch = [
@@ -690,55 +791,122 @@
         VMEM((18, planes, half, lanes), F32),
         VMEM((18, planes, half, lanes), F32),
     ]
-    flat_scratch = [VMEM((8, per * times, lanes), F32)]
+    flat_scratch = [VMEM((8, per * split, lanes), F32)]
     algebra_shape = shape(8, slots, half, lanes)
-    share_shapes = [shape(8, per, lanes)] * times
+    share_shapes = [shape(8, per, lanes)] * split
 
     def turn(spectrum):
         return lax.all_to_all(spectrum, "space", 0, 0, tiled=True)
 
-    def filtered(spectrum):
+    def convolve(spectrum):
         (out,) = call(
-            functools.partial(convolve_kernel, planes), [spectrum_shape], [turn(spectrum), table], []
+            functools.partial(convolve_kernel, planes),
+            [spectrum_shape],
+            [VMEM_SPEC],
+            [spectrum, table],
+            [VMEM_SPEC] * 2,
+            [],
         )
-        return turn(out)
-
-    (spectrum,) = call(
-        start_kernel, [spectrum_shape], [lattice] + forward, divergence_scratch + transform_scratch
+        return out
+
+    source = interleave(propagator, 2 * pairs)
+    if per * split > sites:
+        source = jnp.pad(source, ((0, 0), (0, per * split - sites), (0, 0)))
+    scalars = jnp.concatenate([sink_time % times, src_time % times, src_site])
+    spectrum, *cuts = call(
+        functools.partial(start_kernel, split),
+        [spectrum_shape] + [shape(2 * pairs, per, lanes)] * (split - 1),
+        [VMEM_SPEC] + [HBM_SPEC] * (split - 1),
+        [lattice, forward, source],
+        [HBM_SPEC] * 3,
+        [
+            VMEM((split - 1, 2 * pairs, per, lanes), F32),
+            VMEM(lattice.shape, F32),
+            VMEM(forward.shape, BF16),
+        ]
+        + divergence_scratch
+        + transform_scratch
+        + [pltpu.SemaphoreType.DMA((4,)), pltpu.SemaphoreType.DMA((2, split - 1))],
     )
-    spectrum, first, *shares = call(
-        functools.partial(middle_kernel, times),
+    sources = [
+        lax.ppermute(block, "tm", [(i, within(i, shift)) for i in range(times)])
+        for shift, block in enumerate(cuts, 1)
+    ]
+    spectrum = turn(spectrum)
+    spectrum = convolve(spectrum)
+    spectrum = turn(spectrum)
+    spectrum, first, *early = call(
+        functools.partial(middle_kernel, split),
         [spectrum_shape, algebra_shape] + share_shapes,
-        [filtered(spectrum), lattice] + inverse + forward,
-        gauge_scratch + divergence_scratch + transform_scratch + flat_scratch,
+        [VMEM_SPEC] + [HBM_SPEC] * (1 + split),
+        [spectrum, lattice, inverse, forward],
+        [VMEM_SPEC] * 4,
+        [VMEM(algebra_shape.shape, F32)]
+        + gauge_scratch
+        + divergence_scratch
+        + transform_scratch
+        + flat_scratch
+        + [pltpu.SemaphoreType.DMA((split + 1,))],
     )
-    first_shares = [forwarded(share, shift) for shift, share in enumerate(shares)]
+    first_shares = [forwarded(early[shift % split], shift) for shift in range(1, times)]
+    spectrum = turn(spectrum)
+    spectrum = convolve(spectrum)
+    spectrum = turn(spectrum)
     second, *shares = call(
-        functools.partial(last_transform_kernel, times),
+        last_transform_kernel,
         [algebra_shape] + share_shapes,
-        [filtered(spectrum)] + inverse,
+        [VMEM_SPEC] * (1 + split),
+        [spectrum, inverse],
+        [VMEM_SPEC] * 2,
         transform_scratch + flat_scratch,
     )
-    second_shares = [forwarded(share, shift) for shift, share in enumerate(shares)]
-    fixed, anchor = call(
-        functools.partial(finish_kernel, times),
-        [shape(54, sites, lanes), shape(24, lanes)],
-        [src_time, src_site, lattice, first, second],
-        gauge_scratch,
-        scalars=2,
+
+    def sent_from(source_index):
+        def send(*blocks):
+            return tuple(
+                lax.ppermute(blocks[to % split], "tm", [(source_index, to)])
+                for to in range(times)
+                if to != source_index
+            )
+
+        return send
+
+    second_shares = lax.switch(sink_time[0] % times, [sent_from(k) for k in range(times)], *shares)
+    (fixed,) = call(
+        finish_kernel,
+        [shape(54, sites, lanes)],
+        [HBM_SPEC],
+        [lattice, first, second],
+        [HBM_SPEC] * 2 + [VMEM_SPEC],
+        gauge_scratch
+        + [
+            VMEM(lattice.shape, F32),
+            VMEM(algebra_shape.shape, F32),
+            VMEM(lattice.shape, F32),
+            pltpu.SemaphoreType.DMA((2 + half // 8,)),
+        ],
     )
     width = -(-(SC * SC + 24) // lanes)
     devices = count * times
     (payload,) = call(
-        functools.partial(sink_kernel, times),
+        functools.partial(sink_kernel, times, split),
         [shape(devices, 2 * width, lanes)],
-        [sink_time, anchor] + first_shares + second_shares + sources,
-        [VMEM((2, 8, per, lanes), F32), VMEM((2, SC * SC * 8, lanes), F32)],
-        scalars=1,
+        [VMEM_SPEC],
+        [scalars, first, second, early[0]] + first_shares + shares + list(second_shares) + [source] + sources,
+        [SMEM_SPEC, HBM_SPEC] + [VMEM_SPEC] * (2 * times + split) + [HBM_SPEC] + [ANY_SPEC] * (split - 1),
+        [
+            VMEM((split, 2 * pairs, per, lanes), F32),
+            VMEM((2, 8, per, lanes), F32),
+            VMEM((18, per, lanes), F32),
+            VMEM((2, SC * SC * 8, lanes), F32),
+            VMEM((8, 8, lanes), F32),
+            VMEM((24, lanes), F32),
+            pltpu.SemaphoreType.DMA((split + 1,)),
+        ],
     )
     gathered = lax.all_to_all(payload, ("space", "tm"), 0, 0, tiled=True)
     scale = float(across * side * side) ** (-0.5)
-    (wall,) = call(functools.partial(wall_kernel, scale), [shape(2, SC * SC)], [gathered], [])
+    (wall,) = call(functools.partial(wall_kernel, scale), [shape(2, SC * SC)], [VMEM_SPEC], [gathered], [VMEM_SPEC], [])
     fixed = fixed.reshape(54, half, planes, lanes).transpose(0, 2, 1, 3).reshape(links.shape)
     return fixed, wall
 

time: 134 us -> 95.8 us (0.71)
  waiting for transfers between devices: 47.2 us -> 25 us
  local copies, waits for them, and re-layouts: 11 us -> 0.04 us
  starting transfers between devices: 26.9 us -> 22.1 us
  blocking collectives: 25.2 us -> 21.5 us
  Pallas kernels: 20.2 us -> 23.7 us
    ppermute x9 -> x3, waiting for transfers between devices: 34.2 us -> 3.33 us  [forwarded(): lax.ppermute(value, 'tm', [(i, (i + shift) % times) for i in range(times)])]
    all_to_all x1 -> x0, blocking collectives: 11.9 us -> none  [body(): gathered = lax.all_to_all(payload, ('space', 'tm'), 0, 0, tiled=True)]
    ppermute x9 -> x3, starting transfers between devices: 16.4 us -> 4.68 us  [forwarded(): lax.ppermute(value, 'tm', [(i, (i + shift) % times) for i in range(times)])]
    ppermute x0 -> x4, waiting for transfers between devices: none -> 9.05 us  [the longest x3 9.05 us: send(): lax.ppermute(blocks[to % split], 'tm', [(source_index, to)])]
    all_to_all x1 -> x2, blocking collectives: 13.3 us -> 21.5 us  [turn(): return lax.all_to_all(spectrum, 'space', 0, 0, tiled=True)]
    unnamed x40 -> x12, local copies, waits for them, and re-layouts: 8.14 us -> 0.04 us
    ppermute x0 -> x4, starting transfers between devices: none -> 5.48 us  [the longest x3 3.91 us: send(): lax.ppermute(blocks[to % split], 'tm', [(source_index, to)])]
    pallas_call x8, Pallas kernels: 20.2 us -> 23.7 us  [call(): pl.pallas_call(kernel, out_shape=outs, in_specs=in_specs, out_specs=out_s...]
  transfers between devices with their start and end apart: 12 -> 10, of which waited for: 4 -> 6; matrix products, arithmetic and copies ran while one was open for 2% -> 0% of each run, Pallas kernels for 6% -> 15%
where the time goes in v1:
time: 95.8 us; the launch traced here: 95.2 us
  waiting for transfers between devices  25 us (26%)
  Pallas kernels  23.7 us (25%)
  starting transfers between devices  22.1 us (23%)
  blocking collectives  21.5 us (22%)
  between operations  2.76 us (3%)
    pallas_call x8, Pallas kernels, call(): pl.pallas_call(kernel, out_shape=outs, in_specs=in_specs, out_specs=out_s...  23.7 us
    all_to_all x2, blocking collectives, turn(): return lax.all_to_all(spectrum, 'space', 0, 0, tiled=True)  21.5 us
    all_to_all x2, waiting for transfers between devices, turn(): return lax.all_to_all(spectrum, 'space', 0, 0, tiled=True)  11.6 us
    ppermute x3, waiting for transfers between devices, send(): lax.ppermute(blocks[to % split], 'tm', [(source_index, to)])  9.05 us
    all_to_all x2, starting transfers between devices, turn(): return lax.all_to_all(spectrum, 'space', 0, 0, tiled=True)  8.79 us
    ppermute x3, starting transfers between devices, forwarded(): lax.ppermute(value, 'tm', [(i, (i + shift) % times) for i in range(times)])  4.68 us
    ppermute x3, starting transfers between devices, send(): lax.ppermute(blocks[to % split], 'tm', [(source_index, to)])  3.91 us
    ppermute x3, waiting for transfers between devices, forwarded(): lax.ppermute(value, 'tm', [(i, (i + shift) % times) for i in range(times)])  3.33 us
  transfers between devices with their start and end apart: 10, of which 6 were waited for; matrix products, arithmetic and copies ran while one was open for 0% of the time, Pallas kernels for 15%

profile of v1, /device:TPU:0, one launch (start us, length us, event | category | flops | bytes accessed | tf_op | source)
XLA Modules:
  0.0 95.2 jit_solution(5694677871730003998)
XLA Ops:
  0.6 0.0 copy-start.3
  0.6 4.0 %shard_map.95 = (f32[8,96,128]{2,1,0:T(8,128)}, f32[72,32,128]{2,1,0:T(8,128)}) custom-call(f32[54,64,128]{2,1,0:T(8,128)} %bitcast.19, bf16[640,256]{1,0:T(8,128)(2,1)} %constant.43.clone.table_any.forward_ref, f32[72,64,128]{2,1,0:T(8,128)} %bitcast.22), custom_call_target="tpu_custom_call" | custom-call | tf_op jit(solution)/shard_map/pallas_call | solution.py:739
  4.6 0.0 copy-start
  4.6 0.0 copy-start.1
  4.7 0.0 copy-start.2
  4.7 5.3 %all-to-all-start = ((f32[8,96,128]{2,1,0:T(8,128)}), f32[8,96,128]{2,1,0:T(8,128)S(1)}, u32[]{:S(2)}, u32[]{:S(2)}) async-start(f32[8,96,128]{2,1,0:T(8,128)} %get-tuple-element.38), calls=%async_computation | async-start | bytes 786432 | tf_op jit(solution)/shard_map/all_to_all | solution.py:799
  10.0 1.6 %collective-permute-start.15 = (f32[72,32,128]{2,1,0:T(8,128)}, f32[72,32,128]{2,1,0:T(8,128)}, u32[]{:S(2)}, u32[]{:S(2)}) collective-permute-start(f32[72,32,128]{2,1,0:T(8,128)} %get-tuple-element.49), channel_id=1, source_target_pairs={{0,1},{1,0},{2,3},{3,2},{4,5},{5,4},{6,7},{7,6},{8,9},{9,8},{10,11... | collective-permute-start | bytes 3538952 | tf_op jit(solution)/shard_map/ppermute | solution.py:832
  11.6 6.7 %all-to-all-done.in_ref = f32[8,96,128]{2,1,0:T(8,128)S(1)} async-done(((f32[8,96,128]{2,1,0:T(8,128)}), f32[8,96,128]{2,1,0:T(8,128)S(1)}, u32[]{:S(2)}, u32[]{:S(2)}) %all-to-all-start) | async-done | bytes 393248 | tf_op jit(solution)/shard_map/all_to_all | solution.py:799
  18.3 0.2 shard_map.96
  18.6 10.7 %all_to_all.25.in_ref = f32[8,96,128]{2,1,0:T(8,128)S(1)} all-to-all(f32[8,96,128]{2,1,0:T(8,128)S(1)} %shard_map.96), channel_id=1, replica_groups=mesh['space'=8,'tm'=4] {'space'}, dimensions={0} | all-to-all | bytes 786432 | tf_op jit(solution)/shard_map/all_to_all | solution.py:799
  29.3 5.8 %shard_map.97 = (f32[8,96,128]{2,1,0:T(8,128)S(1)}, f32[8,3,32,128]{3,2,1,0:T(8,128)}, f32[8,32,128]{2,1,0:T(8,128)}, f32[8,32,128]{2,1,0:T(8,128)}) custom-call(f32[8,96,128]{2,1,0:T(8,128)S(1)} %all_to_all.25.in_ref, f32[54,64,128]{2,1,0:T(8,128)S(1)} %bitcast.21, bf16[640,256]{1,0:T(8,128)(2,1)S(1)} %copy-done.2, bf16[640,256]{1,0:T(8,128)(2,1)S(1)} %copy-done.1), custom_call_target="tpu_custom_call" | custom-call | tf_op jit(solution)/shard_map/pallas_call | solution.py:739
  35.2 10.8 %all_to_all.26.in_ref = f32[8,96,128]{2,1,0:T(8,128)S(1)} all-to-all(f32[8,96,128]{2,1,0:T(8,128)S(1)} %get-tuple-element.40), channel_id=1, replica_groups=mesh['space'=8,'tm'=4] {'space'}, dimensions={0} | all-to-all | bytes 786432 | tf_op jit(solution)/shard_map/all_to_all | solution.py:799
  46.0 1.0 %shard_map.98 = f32[8,96,128]{2,1,0:T(8,128)} custom-call(f32[8,96,128]{2,1,0:T(8,128)S(1)} %all_to_all.26.in_ref, f32[2,9,16,128]{3,2,1,0:T(8,128)S(1)} %copy-done.3), custom_call_target="tpu_custom_call" | custom-call | tf_op jit(solution)/shard_map/pallas_call | solution.py:739
  47.0 3.5 %all-to-all-start.3 = ((f32[8,96,128]{2,1,0:T(8,128)}), f32[8,96,128]{2,1,0:T(8,128)S(1)}, u32[]{:S(2)}, u32[]{:S(2)}) async-start(f32[8,96,128]{2,1,0:T(8,128)} %shard_map.98), calls=%async_computation.3 | async-start | bytes 786432 | tf_op jit(solution)/shard_map/all_to_all | solution.py:799
  51.1 2.7 %collective-permute-start.13 = (f32[8,32,128]{2,1,0:T(8,128)S(1)}, f32[8,32,128]{2,1,0:T(8,128)S(1)}, u32[]{:S(2)}, u32[]{:S(2)}) collective-permute-start(f32[8,32,128]{2,1,0:T(8,128)S(1)} %copy-done.4), channel_id=1, source_target_pairs={{0,2},{1,3},{2,0},{3,1},{4,6},{5,7},{6,4},{7,5},{8,10},{9,11},{10,... | collective-permute-start | bytes 393224 | tf_op jit(solution)/shard_map/ppermute | solution.py:774
  53.8 4.9 %all-to-all-done.3.in_ref = f32[8,96,128]{2,1,0:T(8,128)S(1)} async-done(((f32[8,96,128]{2,1,0:T(8,128)}), f32[8,96,128]{2,1,0:T(8,128)S(1)}, u32[]{:S(2)}, u32[]{:S(2)}) %all-to-all-start.3) | async-done | bytes 393248 | tf_op jit(solution)/shard_map/all_to_all | solution.py:799
  58.7 0.7 shard_map.99
  59.4 13.0 %conditional.1 = (f32[8,32,128]{2,1,0:T(8,128)}, f32[8,32,128]{2,1,0:T(8,128)}, f32[8,32,128]{2,1,0:T(8,128)}) conditional(s32[]{:T(128)} %clamp.3, (f32[8,32,128]{2,1,0:T(8,128)S(1)}, f32[8,32,128]{2,1,0:T(8,128)S(1)}) %tuple.24, (f32[8,32,128]{2,1,0:T(8,128)S(1)}, f32[8,32,128]{2,1,0:T(8,128)S(1)}) %tuple.25, ...), branch_computations={%region_0.1_spmd, %region_1.2_spmd, %region_2.3_spmd, %region_3.4_... | conditional | bytes 1573008 | solution.py:874
  59.4 1.3 %collective-permute-start.5 = (f32[8,32,128]{2,1,0:T(8,128)S(1)}, f32[8,32,128]{2,1,0:T(8,128)}, u32[]{:S(2)}, u32[]{:S(2)}) collective-permute-start(f32[8,32,128]{2,1,0:T(8,128)S(1)} %get-tuple-element.19), channel_id=1, source_target_pairs={{1,3},{5,7},{9,11},{13,15},{17,19},{21,23},{25,27},{29,31}} | collective-permute-start | bytes 393224 | tf_op jit(solution)/shard_map/cond/branch_1_fun/ppermute | solution.py:867
  60.7 1.3 %collective-permute-start.4 = (f32[8,32,128]{2,1,0:T(8,128)S(1)}, f32[8,32,128]{2,1,0:T(8,128)}, u32[]{:S(2)}, u32[]{:S(2)}) collective-permute-start(f32[8,32,128]{2,1,0:T(8,128)S(1)} %get-tuple-element.18), channel_id=1, source_target_pairs={{1,2},{5,6},{9,10},{13,14},{17,18},{21,22},{25,26},{29,30}} | collective-permute-start | bytes 393224 | tf_op jit(solution)/shard_map/cond/branch_1_fun/ppermute | solution.py:867
  62.0 1.3 %collective-permute-start.3 = (f32[8,32,128]{2,1,0:T(8,128)S(1)}, f32[8,32,128]{2,1,0:T(8,128)}, u32[]{:S(2)}, u32[]{:S(2)}) collective-permute-start(f32[8,32,128]{2,1,0:T(8,128)S(1)} %get-tuple-element.18), channel_id=1, source_target_pairs={{1,0},{5,4},{9,8},{13,12},{17,16},{21,20},{25,24},{29,28}} | collective-permute-start | bytes 393224 | tf_op jit(solution)/shard_map/cond/branch_1_fun/ppermute | solution.py:867
  63.3 0.0 collective-permute-done.5
  63.3 9.0 %collective-permute-done.3 = f32[8,32,128]{2,1,0:T(8,128)} collective-permute-done((f32[8,32,128]{2,1,0:T(8,128)S(1)}, f32[8,32,128]{2,1,0:T(8,128)}, u32[]{:S(2)}, u32[]{:S(2)}) %collective-permute-start.3) | collective-permute-done | bytes 131104 | tf_op jit(solution)/shard_map/cond/branch_1_fun/ppermute | solution.py:867
  72.4 2.0 %collective-permute-start.12 = (f32[8,32,128]{2,1,0:T(8,128)S(1)}, f32[8,32,128]{2,1,0:T(8,128)S(1)}, u32[]{:S(2)}, u32[]{:S(2)}) collective-permute-start(f32[8,32,128]{2,1,0:T(8,128)S(1)} %copy-done.5), channel_id=1, source_target_pairs={{0,1},{1,2},{2,3},{3,0},{4,5},{5,6},{6,7},{7,4},{8,9},{9,10},{10,1... | collective-permute-start | bytes 393224 | tf_op jit(solution)/shard_map/ppermute | solution.py:774
  75.7 0.1 pad_add_fusion.scalar_ref
  75.8 1.5 %collective-permute-done.14.rest_2_ = f32[8,32,128]{2,1,0:T(8,128)S(1)} collective-permute-done((f32[8,32,128]{2,1,0:T(8,128)S(1)}, f32[8,32,128]{2,1,0:T(8,128)S(1)}, u32[]{:S(2)}, u32[]{:S(2)}) %collective-permute-start.14) | collective-permute-done | bytes 131104 | tf_op jit(solution)/shard_map/ppermute | solution.py:774
  77.3 1.8 %collective-permute-done.12.rest_0_ = f32[8,32,128]{2,1,0:T(8,128)S(1)} collective-permute-done((f32[8,32,128]{2,1,0:T(8,128)S(1)}, f32[8,32,128]{2,1,0:T(8,128)S(1)}, u32[]{:S(2)}, u32[]{:S(2)}) %collective-permute-start.12) | collective-permute-done | bytes 131104 | tf_op jit(solution)/shard_map/ppermute | solution.py:774
  79.2 4.7 %shard_map.101 = f32[32,4,128]{2,1,0:T(4,128)} custom-call(s32[3]{0:T(128)S(1)} %pad_add_fusion.scalar_ref, f32[8,3,32,128]{3,2,1,0:T(8,128)} %get-tuple-element.39.first_any, f32[8,3,32,128]{3,2,1,0:T(8,128)S(1)} %get-tuple-element.41.second_ref, f32[8,32,128]{2,1,0:T(8,128)S(1)} %copy-done.4, f32[8,32,128]{2,1,0:T(8,128)S(1)} %collective-permute-done.12.rest_0_, ...), custom_call_target="tpu_custom_call" | custom-call | tf_op jit(solution)/shard_map/pallas_call | solution.py:739
  83.8 3.1 %all-to-all-start.4 = ((f32[32,4,128]{2,1,0:T(4,128)}), f32[32,4,128]{2,1,0:T(4,128)S(1)}, u32[]{:S(2)}, u32[]{:S(2)}) async-start(f32[32,4,128]{2,1,0:T(4,128)} %shard_map.101), calls=%async_computation.4 | async-start | bytes 131072 | tf_op jit(solution)/shard_map/all_to_all | solution.py:907
  87.0 6.5 %shard_map.100 = f32[54,64,128]{2,1,0:T(8,128)} custom-call(f32[54,64,128]{2,1,0:T(8,128)} %bitcast.20, f32[8,3,32,128]{3,2,1,0:T(8,128)} %get-tuple-element.39.first_any, f32[8,3,32,128]{3,2,1,0:T(8,128)S(1)} %get-tuple-element.41.second_ref), custom_call_target="tpu_custom_call" | custom-call | tf_op jit(solution)/shard_map/pallas_call | solution.py:739
  93.5 0.9 all-to-all-done.4.in_ref
  94.5 0.7 shard_map.102
  (12 shorter events, 0.0 us)
Async XLA Ops:
  0.6 17.7 %copy-start.3 = (f32[2,9,16,128]{3,2,1,0:T(8,128)S(1)}, f32[2,9,16,128]{3,2,1,0:T(8,128)}, u32[]{:S(2)}) copy-start(f32[2,9,16,128]{3,2,1,0:T(8,128)} %constant.45.clone.table_ref) | copy-start | bytes 442372
  4.6 24.7 %copy-start = (f32[1,3,2,3,3,2,4096]{6,5,4,3,2,1,0:T(2,128)S(1)}, f32[1,3,2,3,3,2,4096]{6,5,4,3,2,1,0:T(2,128)}, u32[]{:S(2)}) copy-start(f32[1,3,2,3,3,2,4096]{6,5,4,3,2,1,0:T(2,128)} %param.12) | copy-start | bytes 5308420
  4.6 24.6 %copy-start.1 = (bf16[640,256]{1,0:T(8,128)(2,1)S(1)}, bf16[640,256]{1,0:T(8,128)(2,1)}, u32[]{:S(2)}) copy-start(bf16[640,256]{1,0:T(8,128)(2,1)} %constant.43.clone.table_any.forward_ref) | copy-start | bytes 983044
  4.7 24.6 %copy-start.2 = (bf16[640,256]{1,0:T(8,128)(2,1)S(1)}, bf16[640,256]{1,0:T(8,128)(2,1)}, u32[]{:S(2)}) copy-start(bf16[640,256]{1,0:T(8,128)(2,1)} %constant.44.clone.inverse_ref) | copy-start | bytes 983044
  4.7 13.7 %all-to-all-start = ((f32[8,96,128]{2,1,0:T(8,128)}), f32[8,96,128]{2,1,0:T(8,128)S(1)}, u32[]{:S(2)}, u32[]{:S(2)}) async-start(f32[8,96,128]{2,1,0:T(8,128)} %get-tuple-element.38), calls=%async_computation | async-start | bytes 786432 | tf_op jit(solution)/shard_map/all_to_all | solution.py:799
  10.0 69.1 %collective-permute-start.15 = (f32[72,32,128]{2,1,0:T(8,128)}, f32[72,32,128]{2,1,0:T(8,128)}, u32[]{:S(2)}, u32[]{:S(2)}) collective-permute-start(f32[72,32,128]{2,1,0:T(8,128)} %get-tuple-element.49), channel_id=1, source_target_pairs={{0,1},{1,0},{2,3},{3,2},{4,5},{5,4},{6,7},{7,6},{8,9},{9,8},{10,11... | collective-permute-start | bytes 3538952 | tf_op jit(solution)/shard_map/ppermute | solution.py:832
  35.2 16.0 %copy-start.4 = (f32[8,32,128]{2,1,0:T(8,128)S(1)}, f32[8,32,128]{2,1,0:T(8,128)}, u32[]{:S(2)}) copy-start(f32[8,32,128]{2,1,0:T(8,128)} %get-tuple-element.42.own_early_ref) | copy-start | bytes 393220
  35.2 37.2 %copy-start.5 = (f32[8,32,128]{2,1,0:T(8,128)S(1)}, f32[8,32,128]{2,1,0:T(8,128)}, u32[]{:S(2)}) copy-start(f32[8,32,128]{2,1,0:T(8,128)} %get-tuple-element.43) | copy-start | bytes 393220
  47.0 11.7 %all-to-all-start.3 = ((f32[8,96,128]{2,1,0:T(8,128)}), f32[8,96,128]{2,1,0:T(8,128)S(1)}, u32[]{:S(2)}, u32[]{:S(2)}) async-start(f32[8,96,128]{2,1,0:T(8,128)} %shard_map.98), calls=%async_computation.3 | async-start | bytes 786432 | tf_op jit(solution)/shard_map/all_to_all | solution.py:799
  51.1 24.7 %collective-permute-start.13 = (f32[8,32,128]{2,1,0:T(8,128)S(1)}, f32[8,32,128]{2,1,0:T(8,128)S(1)}, u32[]{:S(2)}, u32[]{:S(2)}) collective-permute-start(f32[8,32,128]{2,1,0:T(8,128)S(1)} %copy-done.4), channel_id=1, source_target_pairs={{0,2},{1,3},{2,0},{3,1},{4,6},{5,7},{6,4},{7,5},{8,10},{9,11},{10,... | collective-permute-start | bytes 393224 | tf_op jit(solution)/shard_map/ppermute | solution.py:774
  59.4 3.9 %collective-permute-start.5 = (f32[8,32,128]{2,1,0:T(8,128)S(1)}, f32[8,32,128]{2,1,0:T(8,128)}, u32[]{:S(2)}, u32[]{:S(2)}) collective-permute-start(f32[8,32,128]{2,1,0:T(8,128)S(1)} %get-tuple-element.19), channel_id=1, source_target_pairs={{1,3},{5,7},{9,11},{13,15},{17,19},{21,23},{25,27},{29,31}} | collective-permute-start | bytes 393224 | tf_op jit(solution)/shard_map/cond/branch_1_fun/ppermute | solution.py:867
  60.7 2.6 %collective-permute-start.4 = (f32[8,32,128]{2,1,0:T(8,128)S(1)}, f32[8,32,128]{2,1,0:T(8,128)}, u32[]{:S(2)}, u32[]{:S(2)}) collective-permute-start(f32[8,32,128]{2,1,0:T(8,128)S(1)} %get-tuple-element.18), channel_id=1, source_target_pairs={{1,2},{5,6},{9,10},{13,14},{17,18},{21,22},{25,26},{29,30}} | collective-permute-start | bytes 393224 | tf_op jit(solution)/shard_map/cond/branch_1_fun/ppermute | solution.py:867
  62.0 10.4 %collective-permute-start.3 = (f32[8,32,128]{2,1,0:T(8,128)S(1)}, f32[8,32,128]{2,1,0:T(8,128)}, u32[]{:S(2)}, u32[]{:S(2)}) collective-permute-start(f32[8,32,128]{2,1,0:T(8,128)S(1)} %get-tuple-element.18), channel_id=1, source_target_pairs={{1,0},{5,4},{9,8},{13,12},{17,16},{21,20},{25,24},{29,28}} | collective-permute-start | bytes 393224 | tf_op jit(solution)/shard_map/cond/branch_1_fun/ppermute | solution.py:867
  72.4 5.0 %collective-permute-start.14 = (f32[8,32,128]{2,1,0:T(8,128)S(1)}, f32[8,32,128]{2,1,0:T(8,128)S(1)}, u32[]{:S(2)}, u32[]{:S(2)}) collective-permute-start(f32[8,32,128]{2,1,0:T(8,128)S(1)} %copy-done.5), channel_id=1, source_target_pairs={{0,3},{1,0},{2,1},{3,2},{4,7},{5,4},{6,5},{7,6},{8,11},{9,8},{10,9... | collective-permute-start | bytes 393224 | tf_op jit(solution)/shard_map/ppermute | solution.py:774
  72.4 6.8 %collective-permute-start.12 = (f32[8,32,128]{2,1,0:T(8,128)S(1)}, f32[8,32,128]{2,1,0:T(8,128)S(1)}, u32[]{:S(2)}, u32[]{:S(2)}) collective-permute-start(f32[8,32,128]{2,1,0:T(8,128)S(1)} %copy-done.5), channel_id=1, source_target_pairs={{0,1},{1,2},{2,3},{3,0},{4,5},{5,6},{6,7},{7,4},{8,9},{9,10},{10,1... | collective-permute-start | bytes 393224 | tf_op jit(solution)/shard_map/ppermute | solution.py:774
  83.8 10.6 %all-to-all-start.4 = ((f32[32,4,128]{2,1,0:T(4,128)}), f32[32,4,128]{2,1,0:T(4,128)S(1)}, u32[]{:S(2)}, u32[]{:S(2)}) async-start(f32[32,4,128]{2,1,0:T(4,128)} %shard_map.101), calls=%async_computation.4 | async-start | bytes 131072 | tf_op jit(solution)/shard_map/all_to_all | solution.py:907

commit v2 on v1

--- a/solution.py
+++ b/solution.py
@@ -46,7 +46,12 @@
     parity = np.array([[1.0, 1.0], [1.0, -1.0]])
     right = as_real(np.kron(parity, np.cos(depth_phase)), np.kron(parity, np.sin(depth_phase)))
     high, low = split_table(right)
-    return np.concatenate([high, low, left], axis=0)
+    lanes = np.arange(2 * side)
+    from_depth = lanes - lanes % side + (lanes + (1 if inverse else -1)) % side
+    moves = [np.eye(2 * side)[:, (lanes + side) % (2 * side)], np.eye(2 * side)[:, from_depth]]
+    shift = np.concatenate(moves, axis=1)
+    shift = np.concatenate([shift, shift], axis=0).astype(high.dtype)
+    return np.concatenate([high, low, left, shift], axis=0)
 
 
 @functools.lru_cache(None)
@@ -168,34 +173,6 @@
     return lax.broadcasted_iota(jnp.int32, shape, 1)
 
 
-def ahead_y(v):
-    half = v.shape[1] // 2
-    r = pltpu.roll(v, half, axis=1)
-    return jnp.where(lane_of(v.shape) < half, r, pltpu.roll(r, v.shape[0] - 1, axis=0))
-
-
-def behind_y(v):
-    half = v.shape[1] // 2
-    r = pltpu.roll(v, half, axis=1)
-    return jnp.where(lane_of(v.shape) >= half, r, pltpu.roll(r, 1, axis=0))
-
-
-def ahead_z(v):
-    lanes = v.shape[1]
-    half = lanes // 2
-    inner = pltpu.roll(v, lanes - 1, axis=1)
-    edge = pltpu.roll(v, half - 1, axis=1)
-    return jnp.where(lane_of(v.shape) % half == half - 1, edge, inner)
-
-
-def behind_z(v):
-    lanes = v.shape[1]
-    half = lanes // 2
-    inner = pltpu.roll(v, 1, axis=1)
-    edge = pltpu.roll(v, half + 1, axis=1)
-    return jnp.where(lane_of(v.shape) % half == 0, edge, inner)
-
-
 def halves(x):
     high = x.astype(BF16)
     low = (x - high.astype(F32)).astype(BF16)
@@ -204,6 +181,18 @@
 
 def dot(x, y):
     return jnp.dot(x, y, preferred_element_type=F32)
+
+
+def pick_ahead(swapped):
+    half = swapped.shape[1] // 2
+    return jnp.where(
+        lane_of(swapped.shape) < half, swapped, pltpu.roll(swapped, swapped.shape[0] - 1, axis=0)
+    )
+
+
+def pick_behind(swapped):
+    half = swapped.shape[1] // 2
+    return jnp.where(lane_of(swapped.shape) >= half, swapped, pltpu.roll(swapped, 1, axis=0))
 
 
 def left_transform(stacked, table_ref):
@@ -323,51 +312,84 @@
     return pl.ds(pl.multiple_of(chunk * 8, 8), 8)
 
 
-def shift_gauge(g_ref, y_ref, z_ref):
-    planes = y_ref.shape[1]
-
-    def run(index, carry):
+def shift_gauge(g_ref, shift, stack_ref, moved_ref, y_ref):
+    planes, half, lanes = y_ref.shape[1:]
+    for comp in range(18):
         for plane in range(planes):
-            v = g_ref[index, plane]
-            y_ref[index, plane] = ahead_y(v)
-            z_ref[index, plane] = ahead_z(v)
-        return carry
-
-    lax.fori_loop(0, 18, run, 0)
-
-
-def divergence(v_ref, d_ref):
-    planes = v_ref.shape[2]
-
-    def run(comp, carry):
+            at = (comp * planes + plane) * half
+            stack_ref[at : at + half, :] = jnp.concatenate(halves(g_ref[comp, plane]), axis=1)
+    moved_ref[...] = dot(stack_ref[...], shift)
+    for comp in range(18):
+        for plane in range(planes):
+            at = (comp * planes + plane) * half
+            y_ref[comp, plane] = pick_ahead(moved_ref[at : at + half, :lanes])
+
+
+def load_ahead(direction, g_ref, y_ref, moved_ref, plane, chunk):
+    rows = aligned(chunk)
+    if direction == 0:
+        return load_gauge(g_ref, plane + 1, rows)
+    if direction == 1:
+        return load_gauge(y_ref, plane, rows)
+    planes, half, lanes = y_ref.shape[1:]
+
+    def at(comp):
+        return moved_ref[pl.ds(pl.multiple_of((comp * planes + plane) * half + chunk * 8, 8), 8), lanes:]
+
+    return [[(at(3 * i + j), at(9 + 3 * i + j)) for j in range(3)] for i in range(3)]
+
+
+def divergence(v_ref, shift_ref, stack_ref, moved_ref, d_ref):
+    _, comps, planes, half, lanes = v_ref.shape
+    size = comps * planes * half
+    for direction in (1, 2):
+        for comp in range(comps):
+            for plane in range(planes):
+                at = (direction - 1) * size + (comp * planes + plane) * half
+                stack_ref[at : at + half, :] = jnp.concatenate(
+                    halves(v_ref[direction, comp, plane]), axis=1
+                )
+    first = shift_ref.shape[0] - 2 * lanes
+    moved_ref[:size, :lanes] = dot(stack_ref[:size], shift_ref[first:, :lanes])
+    moved_ref[size : 2 * size, :lanes] = dot(stack_ref[size : 2 * size], shift_ref[first:, lanes:])
+    for comp in range(comps):
         before = None
         for plane in range(planes):
+            at = (comp * planes + plane) * half
             vx = v_ref[0, comp, plane]
-            vy = v_ref[1, comp, plane]
-            vz = v_ref[2, comp, plane]
-            total = (behind_y(vy) - vy) + (behind_z(vz) - vz) - vx
+            total = (pick_behind(moved_ref[at : at + half, :lanes]) - v_ref[1, comp, plane]) + (
+                moved_ref[size + at : size + at + half, :lanes] - v_ref[2, comp, plane]
+            )
+            total = total - vx
             if before is not None:
                 total = total + before
             before = vx
             d_ref[plane, comp] = total
         d_ref[planes, comp] = before
-        return carry
-
-    lax.fori_loop(0, 8, run, 0)
-
-
-def start_kernel(times, links_any, table_any, source_any, out_ref, *rest):
-    cut_refs = rest[: times - 1]
-    held_ref, links_ref, table_ref, v_ref, d_ref, high_ref, low_ref, spec_ref, sems, cut_sems = rest[times - 1 :]
-    _, _, planes, half, _ = v_ref.shape
+
+
+def cut_kernel(split, source_any, *rest):
+    cut_refs = rest[: split - 1]
+    held_ref, sems = rest[split - 1 :]
     per = held_ref.shape[2]
     reads, writes = [], []
     for shift, cut in enumerate(cut_refs, 1):
-        rows = pl.ds(share_start(shift, times, per), per)
+        rows = pl.ds(share_start(shift, split, per), per)
         reads.append(
-            pltpu.make_async_copy(source_any.at[:, rows, :], held_ref.at[shift - 1], cut_sems.at[0, shift - 1])
+            pltpu.make_async_copy(source_any.at[:, rows, :], held_ref.at[shift - 1], sems.at[0, shift - 1])
         )
-        writes.append(pltpu.make_async_copy(held_ref.at[shift - 1], cut, cut_sems.at[1, shift - 1]))
+        writes.append(pltpu.make_async_copy(held_ref.at[shift - 1], cut, sems.at[1, shift - 1]))
+    for copy in reads:
+        copy.start()
+    for read, write in zip(reads, writes):
+        read.wait()
+        write.start()
+    for write in writes:
+        write.wait()
+
+
+def start_kernel(links_any, table_any, out_ref, links_ref, table_ref, v_ref, d_ref, stack_ref, moved_ref, high_ref, low_ref, spec_ref, sems):
+    _, _, planes, half, _ = v_ref.shape
     copies = [
         pltpu.make_async_copy(
             links_any.at[pl.ds(18 * direction, 18)], links_ref.at[pl.ds(18 * direction, 18)], sems.at[direction]
@@ -375,7 +397,7 @@
         for direction in range(3)
     ]
     copies.append(pltpu.make_async_copy(table_any, table_ref, sems.at[3]))
-    for copy in copies + reads:
+    for copy in copies:
         copy.start()
     for direction in range(3):
         copies[direction].wait()
@@ -386,14 +408,9 @@
                 v_ref[direction, comp, plane, aligned(chunk), :] = value
 
         chunk_loop(planes, half // 8, step)
-    for read, write in zip(reads, writes):
-        read.wait()
-        write.start()
-    divergence(v_ref, d_ref)
     copies[3].wait()
+    divergence(v_ref, table_ref, stack_ref, moved_ref, d_ref)
     forward_transform(d_ref, table_ref, high_ref, low_ref, spec_ref, out_ref)
-    for write in writes:
-        write.wait()
 
 
 def convolve_kernel(planes, in_ref, table_ref, out_ref):
@@ -447,7 +464,7 @@
 def middle_kernel(shares, in_ref, links_ref, inverse_ref, forward_ref, *rest):
     out_ref, x_any = rest[:2]
     share_refs = rest[2 : 2 + shares]
-    x_ref, g_ref, y_ref, z_ref, v_ref, d_ref, high_ref, low_ref, spec_ref, flat_ref, sems = rest[2 + shares :]
+    x_ref, g_ref, y_ref, v_ref, d_ref, stack_ref, moved_ref, high_ref, low_ref, spec_ref, flat_ref, sems = rest[2 + shares :]
     _, slots, half, _ = x_ref.shape
     planes = slots - 1
     per = share_refs[0].shape[1]
@@ -468,7 +485,8 @@
         store_gauge(g_ref, plane, rows, exponential([x_ref[k, plane, rows, :] for k in range(8)]))
 
     chunk_loop(slots, half // 8, raise_step)
-    shift_gauge(g_ref, y_ref, z_ref)
+    lanes = x_ref.shape[3]
+    shift_gauge(g_ref, inverse_ref[inverse_ref.shape[0] - 2 * lanes :], stack_ref, moved_ref, y_ref)
 
     def rotate_step(plane, chunk):
         rows = aligned(chunk)
@@ -476,29 +494,32 @@
         link_rows = site_rows(plane, chunk, planes)
         for direction in range(3):
             link = load_link(links_ref, direction, link_rows)
-            if direction == 0:
-                ahead = load_gauge(g_ref, plane + 1, rows)
-            else:
-                ahead = load_gauge((y_ref, z_ref)[direction - 1], plane, rows)
+            ahead = load_ahead(direction, g_ref, y_ref, moved_ref, plane, chunk)
             turned = [row_times_dagger(row_times(gauge[i], link), ahead) for i in range(3)]
             for comp, value in enumerate(project(turned)):
                 v_ref[direction, comp, plane, rows, :] = value
 
     chunk_loop(planes, half // 8, rotate_step)
-    divergence(v_ref, d_ref)
+    divergence(v_ref, forward_ref, stack_ref, moved_ref, d_ref)
     forward_transform(d_ref, forward_ref, high_ref, low_ref, spec_ref, out_ref)
     for copy in copies:
         copy.wait()
 
 
 def last_transform_kernel(in_ref, inverse_ref, x_ref, *rest):
-    share_refs = rest[:-4]
-    high_ref, low_ref, spec_ref, flat_ref = rest[-4:]
+    share_refs = rest[:-5]
+    high_ref, low_ref, spec_ref, flat_ref, sems = rest[-5:]
     per = share_refs[0].shape[1]
     inverse_transform(in_ref, inverse_ref, high_ref, low_ref, spec_ref, x_ref)
     flatten_shares(x_ref, flat_ref, x_ref.shape[1] - 1)
-    for to, share_ref in enumerate(share_refs):
-        share_ref[...] = flat_ref[:, to * per : (to + 1) * per, :]
+    copies = [
+        pltpu.make_async_copy(flat_ref.at[:, to * per : (to + 1) * per, :], share_ref, sems.at[to])
+        for to, share_ref in enumerate(share_refs)
+    ]
+    for copy in copies:
+        copy.start()
+    for copy in copies:
+        copy.wait()
 
 
 def total_of(first, second):
@@ -507,13 +528,16 @@
     return [row_times(later[i], earlier) for i in range(3)]
 
 
-def finish_kernel(links_any, first_any, second_ref, out_any, g_ref, y_ref, z_ref, links_ref, first_ref, out_ref, sems):
-    _, slots, half, _ = first_ref.shape
+def finish_kernel(links_any, first_any, table_any, second_ref, out_any, g_ref, y_ref, stack_ref, moved_ref, links_ref, first_ref, shift_ref, out_ref, sems):
+    _, slots, half, lanes = first_ref.shape
     planes = slots - 1
     chunks = half // 8
     copies = [
         pltpu.make_async_copy(first_any, first_ref, sems.at[0]),
         pltpu.make_async_copy(links_any, links_ref, sems.at[1]),
+        pltpu.make_async_copy(
+            table_any.at[pl.ds(table_any.shape[0] - 2 * lanes, 2 * lanes)], shift_ref, sems.at[2]
+        ),
     ]
     for copy in copies:
         copy.start()
@@ -532,12 +556,13 @@
         )
 
     chunk_loop(slots, half // 8, raise_step)
-    shift_gauge(g_ref, y_ref, z_ref)
+    copies[2].wait()
+    shift_gauge(g_ref, shift_ref[...], stack_ref, moved_ref, y_ref)
     copies[1].wait()
 
     def piece(chunk):
         rows = pl.ds(pl.multiple_of(chunk * (8 * planes), 8), 8 * planes)
-        return pltpu.make_async_copy(out_ref.at[:, rows, :], out_any.at[:, rows, :], sems.at[2 + chunk])
+        return pltpu.make_async_copy(out_ref.at[:, rows, :], out_any.at[:, rows, :], sems.at[3 + chunk])
 
     def rotate_step(chunk, plane):
         rows = aligned(chunk)
@@ -545,10 +570,7 @@
         link_rows = site_rows(plane, chunk, planes)
         for direction in range(3):
             link = load_link(links_ref, direction, link_rows)
-            if direction == 0:
-                ahead = load_gauge(g_ref, plane + 1, rows)
-            else:
-                ahead = load_gauge((y_ref, z_ref)[direction - 1], plane, rows)
+            ahead = load_ahead(direction, g_ref, y_ref, moved_ref, plane, chunk)
             for i in range(3):
                 row = row_times_dagger(row_times(gauge[i], link), ahead)
                 for j in range(3):
@@ -577,53 +599,49 @@
     return total
 
 
-def sink_kernel(times, split, scalar_ref, first_any, second_ref, own_early_ref, *rest):
-    early = (own_early_ref,) + rest[: times - 1]
+def sink_kernel(times, split, sink_ref, src_time_ref, src_site_ref, first_any, second_ref, source_ref, own_early_any, *rest):
+    early = (own_early_any,) + rest[: times - 1]
     own = rest[times - 1 : times - 1 + split]
     late = rest[times - 1 + split : 2 * times - 2 + split]
-    sources_any = rest[2 * times - 2 + split : 2 * times - 2 + 2 * split]
-    out_ref, source_ref, x_ref, gauge_ref, sum_ref, before_ref, anchor_ref, sems = rest[2 * times - 2 + 2 * split :]
+    partners_any = rest[2 * times - 2 + split : 2 * times - 3 + 2 * split]
+    out_ref, partner_ref, x_ref, gauge_ref, sum_ref, before_ref, anchor_ref, sems = rest[2 * times - 3 + 2 * split :]
     per = early[0].shape[1]
-    pairs = source_ref.shape[1] // 2
+    pairs = source_ref.shape[0] // 2
     groups = pairs // 3
     _, slots, half, lanes = second_ref.shape
     planes = slots - 1
     mine = lax.axis_index("tm")
-    local = sources_any[0].at[:, pl.ds(share_start(0, split, per), per), :]
-    sink = scalar_ref[0]
-    column = scalar_ref[2] % (half * lanes)
-    plane = scalar_ref[2] // (half * lanes) - lax.axis_index("space") * planes
-    present = (scalar_ref[1] == mine) & (plane >= 0) & (plane < planes)
+    sink = sink_ref[0]
+    column = src_site_ref[0] % (half * lanes)
+    plane = src_site_ref[0] // (half * lanes) - lax.axis_index("space") * planes
+    present = (src_time_ref[0] == mine) & (plane >= 0) & (plane < planes)
     safe = jnp.clip(plane, 0, planes - 1)
     row = column // lanes
     block = pl.ds(pl.multiple_of(row // 8 * 8, 8), 8)
-    before = pltpu.make_async_copy(first_any.at[:, safe, block, :], before_ref, sems.at[split])
-    copies = [
-        pltpu.make_async_copy(sources_any[shift] if shift else local, source_ref.at[shift], sems.at[shift])
-        for shift in range(split)
-    ]
+    before = pltpu.make_async_copy(first_any.at[:, safe, block, :], before_ref, sems.at[0])
+    fetches = [pltpu.make_async_copy(early[0], x_ref.at[k], sems.at[1 + k]) for k in range(2)]
+    partners = [
+        pltpu.make_async_copy(partner, partner_ref.at[k], sems.at[3 + k])
+        for k, partner in enumerate(partners_any)
+    ]
+
+    def fetch(condition, value, to):
+        @pl.when(condition)
+        def _():
+            pltpu.make_async_copy(value, x_ref.at[to], sems.at[1 + to]).start()
+
+    for shift in range(times):
+        fetch((mine - sink) % times == shift, early[shift], 0)
+    for at in range(split):
+        fetch((mine == sink) & (mine % split == at), own[at], 1)
+    for at in range(times - 1):
+        fetch((mine != sink) & (jnp.where(mine > sink, mine - 1, mine) == at), late[at], 1)
+    for copy in partners:
+        copy.start()
     before.start()
-    for copy in copies:
-        copy.start()
-    wanted = (mine - sink) % times
-    for shift in range(times):
-
-        @pl.when(wanted == shift)
-        def _(shift=shift):
-            x_ref[0] = early[shift][...]
-
-    for at in range(split):
-
-        @pl.when((mine == sink) & (mine % split == at))
-        def _(at=at):
-            x_ref[1] = own[at][...]
-
-    for at in range(times - 1):
-
-        @pl.when((mine != sink) & (jnp.where(mine > sink, mine - 1, mine) == at))
-        def _(at=at):
-            x_ref[1] = late[at][...]
-
+    sum_ref[...] = jnp.zeros_like(sum_ref)
+    for copy in fetches:
+        copy.wait()
     chunks = per // 8
     for chunk in range(chunks):
         rows = slice(chunk * 8, chunk * 8 + 8)
@@ -632,20 +650,20 @@
             for j in range(3):
                 gauge_ref[3 * i + j, rows, :] = gauge[i][j][0]
                 gauge_ref[9 + 3 * i + j, rows, :] = gauge[i][j][1]
-    sum_ref[...] = jnp.zeros_like(sum_ref)
     for shift in range(split):
-        copies[shift].wait()
+        if shift:
+            partners[shift - 1].wait()
+        block_ref = partner_ref.at[shift - 1] if shift else source_ref
+        offset = 0 if shift else share_start(0, split, per)
         base = (mine - mine % split + (mine - shift) % split) * pairs
 
-        def run(group, carry, shift=shift, base=base):
+        def run(group, carry, block_ref=block_ref, offset=offset, base=base):
             sums = [None] * 3
             for chunk in range(chunks):
                 rows = slice(chunk * 8, chunk * 8 + 8)
+                own_rows = pl.ds(pl.multiple_of(offset + chunk * 8, 8), 8)
                 column = [
-                    (
-                        source_ref[shift, 3 * group + c, rows, :],
-                        source_ref[shift, pairs + 3 * group + c, rows, :],
-                    )
+                    (block_ref[3 * group + c, own_rows, :], block_ref[pairs + 3 * group + c, own_rows, :])
                     for c in range(3)
                 ]
                 for a in range(3):
@@ -789,7 +807,10 @@
     gauge_scratch = [
         VMEM((18, slots, half, lanes), F32),
         VMEM((18, planes, half, lanes), F32),
-        VMEM((18, planes, half, lanes), F32),
+    ]
+    shift_scratch = [
+        VMEM((18 * planes * half, 2 * lanes), BF16),
+        VMEM((18 * planes * half, 2 * lanes), F32),
     ]
     flat_scratch = [VMEM((8, per * split, lanes), F32)]
     algebra_shape = shape(8, slots, half, lanes)
@@ -812,21 +833,27 @@
     source = interleave(propagator, 2 * pairs)
     if per * split > sites:
         source = jnp.pad(source, ((0, 0), (0, per * split - sites), (0, 0)))
-    scalars = jnp.concatenate([sink_time % times, src_time % times, src_site])
-    spectrum, *cuts = call(
-        functools.partial(start_kernel, split),
-        [spectrum_shape] + [shape(2 * pairs, per, lanes)] * (split - 1),
-        [VMEM_SPEC] + [HBM_SPEC] * (split - 1),
-        [lattice, forward, source],
-        [HBM_SPEC] * 3,
-        [
-            VMEM((split - 1, 2 * pairs, per, lanes), F32),
-            VMEM(lattice.shape, F32),
-            VMEM(forward.shape, BF16),
-        ]
+    scalars = [sink_time % times, src_time % times, jnp.maximum(src_site, 0)]
+    (spectrum,) = call(
+        start_kernel,
+        [spectrum_shape],
+        [VMEM_SPEC],
+        [lattice, forward],
+        [HBM_SPEC] * 2,
+        [VMEM(lattice.shape, F32), VMEM(forward.shape, BF16)]
         + divergence_scratch
+        + shift_scratch
         + transform_scratch
-        + [pltpu.SemaphoreType.DMA((4,)), pltpu.SemaphoreType.DMA((2, split - 1))],
+        + [pltpu.SemaphoreType.DMA((4,))],
+    )
+    spectrum, uncut = lax.optimization_barrier((spectrum, source))
+    cuts = call(
+        functools.partial(cut_kernel, split),
+        [shape(2 * pairs, per, lanes)] * (split - 1),
+        [HBM_SPEC] * (split - 1),
+        [uncut],
+        [HBM_SPEC],
+        [VMEM((split - 1, 2 * pairs, per, lanes), F32), pltpu.SemaphoreType.DMA((2, split - 1))],
     )
     sources = [
         lax.ppermute(block, "tm", [(i, within(i, shift)) for i in range(times)])
@@ -844,6 +871,7 @@
         [VMEM(algebra_shape.shape, F32)]
         + gauge_scratch
         + divergence_scratch
+        + shift_scratch
         + transform_scratch
         + flat_scratch
         + [pltpu.SemaphoreType.DMA((split + 1,))],
@@ -855,10 +883,10 @@
     second, *shares = call(
         last_transform_kernel,
         [algebra_shape] + share_shapes,
-        [VMEM_SPEC] * (1 + split),
+        [VMEM_SPEC] + [HBM_SPEC] * split,
         [spectrum, inverse],
         [VMEM_SPEC] * 2,
-        transform_scratch + flat_scratch,
+        transform_scratch + flat_scratch + [pltpu.SemaphoreType.DMA((split,))],
     )
 
     def sent_from(source_index):
@@ -876,14 +904,16 @@
         finish_kernel,
         [shape(54, sites, lanes)],
         [HBM_SPEC],
-        [lattice, first, second],
-        [HBM_SPEC] * 2 + [VMEM_SPEC],
+        [lattice, first, inverse, second],
+        [HBM_SPEC] * 3 + [VMEM_SPEC],
         gauge_scratch
+        + shift_scratch
         + [
             VMEM(lattice.shape, F32),
             VMEM(algebra_shape.shape, F32),
+            VMEM((2 * lanes, 2 * lanes), BF16),
             VMEM(lattice.shape, F32),
-            pltpu.SemaphoreType.DMA((2 + half // 8,)),
+            pltpu.SemaphoreType.DMA((3 + half // 8,)),
         ],
     )
     width = -(-(SC * SC + 24) // lanes)
@@ -892,16 +922,21 @@
         functools.partial(sink_kernel, times, split),
         [shape(devices, 2 * width, lanes)],
         [VMEM_SPEC],
-        [scalars, first, second, early[0]] + first_shares + shares + list(second_shares) + [source] + sources,
-        [SMEM_SPEC, HBM_SPEC] + [VMEM_SPEC] * (2 * times + split) + [HBM_SPEC] + [ANY_SPEC] * (split - 1),
+        scalars + [first, second, source, early[0]] + first_shares + shares + list(second_shares) + sources,
+        [SMEM_SPEC] * 3
+        + [HBM_SPEC]
+        + [VMEM_SPEC] * 2
+        + [HBM_SPEC]
+        + [ANY_SPEC] * (times - 1)
+        + [HBM_SPEC] * (times - 2 + 2 * split),
         [
-            VMEM((split, 2 * pairs, per, lanes), F32),
+            VMEM((max(1, split - 1), 2 * pairs, per, lanes), F32),
             VMEM((2, 8, per, lanes), F32),
             VMEM((18, per, lanes), F32),
             VMEM((2, SC * SC * 8, lanes), F32),
             VMEM((8, 8, lanes), F32),
             VMEM((24, lanes), F32),
-            pltpu.SemaphoreType.DMA((split + 1,)),
+            pltpu.SemaphoreType.DMA((2 + split,)),
         ],
     )
     gathered = lax.all_to_all(payload, ("space", "tm"), 0, 0, tiled=True)

time: 95.8 us -> 97.5 us (1.018)
  starting transfers between devices: 22.1 us -> 29.5 us
  waiting for transfers between devices: 25 us -> 18.9 us
  local copies, waits for them, and re-layouts: 0.04 us -> 1.78 us
  Pallas kernels: 23.7 us -> 22.4 us
    ppermute x3, starting transfers between devices: 4.68 us -> 10.6 us  [forwarded(): lax.ppermute(value, 'tm', [(i, (i + shift) % times) for i in range(times)])]
    ppermute x3, waiting for transfers between devices: 9.05 us -> 3.25 us  [send(): lax.ppermute(blocks[to % split], 'tm', [(source_index, to)])]
    unnamed x12 -> x16, local copies, waits for them, and re-layouts: 0.04 us -> 1.78 us
    all_to_all x1, starting transfers between devices: 3.11 us -> 4.69 us  [body(): gathered = lax.all_to_all(payload, ('space', 'tm'), 0, 0, tiled=True)]
    all_to_all x2, waiting for transfers between devices: 11.6 us -> 10.1 us  [turn(): return lax.all_to_all(spectrum, 'space', 0, 0, tiled=True)]
    all_to_all x1, waiting for transfers between devices: 0.94 us -> 2.31 us  [body(): gathered = lax.all_to_all(payload, ('space', 'tm'), 0, 0, tiled=True)]
    pallas_call x8 -> x9, Pallas kernels: 23.7 us -> 22.4 us  [call(): pl.pallas_call(kernel, out_shape=outs, in_specs=in_specs, out_specs=out_s...]
  transfers between devices with their start and end apart: 10 -> 10, of which waited for: 6 -> 5; matrix products, arithmetic and copies ran while one was open for 0% -> 0% of each run, Pallas kernels for 15% -> 15%
where the time goes in v2:
time: 97.5 us; the launch traced here: 96.9 us
  starting transfers between devices  29.5 us (30%)
  Pallas kernels  22.4 us (23%)
  blocking collectives  21.5 us (22%)
  waiting for transfers between devices  18.9 us (19%)
  between operations  2.76 us (3%)
  local copies, waits for them, and re-layouts  1.78 us (2%)
    pallas_call x9, Pallas kernels, call(): pl.pallas_call(kernel, out_shape=outs, in_specs=in_specs, out_specs=out_s...  22.4 us
    all_to_all x2, blocking collectives, turn(): return lax.all_to_all(spectrum, 'space', 0, 0, tiled=True)  21.5 us
    ppermute x3, starting transfers between devices, forwarded(): lax.ppermute(value, 'tm', [(i, (i + shift) % times) for i in range(times)])  10.6 us
    all_to_all x2, waiting for transfers between devices, turn(): return lax.all_to_all(spectrum, 'space', 0, 0, tiled=True)  10.1 us
    all_to_all x2, starting transfers between devices, turn(): return lax.all_to_all(spectrum, 'space', 0, 0, tiled=True)  8.66 us
    all_to_all x1, starting transfers between devices, body(): gathered = lax.all_to_all(payload, ('space', 'tm'), 0, 0, tiled=True)  4.69 us
    ppermute x3, starting transfers between devices, send(): lax.ppermute(blocks[to % split], 'tm', [(source_index, to)])  3.92 us
    ppermute x3, waiting for transfers between devices, send(): lax.ppermute(blocks[to % split], 'tm', [(source_index, to)])  3.25 us
  transfers between devices with their start and end apart: 10, of which 5 were waited for; matrix products, arithmetic and copies ran while one was open for 0% of the time, Pallas kernels for 15%

profile of v2, /device:TPU:0, one launch (start us, length us, event | category | flops | bytes accessed | tf_op | source)
XLA Modules:
  0.0 96.9 jit_solution(9499725015194238701)
XLA Ops:
  0.6 3.3 %shard_map.95 = f32[8,96,128]{2,1,0:T(8,128)} custom-call(f32[54,64,128]{2,1,0:T(8,128)} %bitcast.19, bf16[896,256]{1,0:T(8,128)(2,1)} %constant.44.clone.table_any.forward_ref), custom_call_target="tpu_custom_call" | custom-call | tf_op jit(solution)/shard_map/pallas_call | solution.py:757
  4.0 5.2 %all-to-all-start = ((f32[8,96,128]{2,1,0:T(8,128)}), f32[8,96,128]{2,1,0:T(8,128)S(1)}, u32[]{:S(2)}, u32[]{:S(2)}) async-start(f32[8,96,128]{2,1,0:T(8,128)} %shard_map.95), calls=%async_computation | async-start | bytes 786432 | tf_op jit(solution)/shard_map/all_to_all | solution.py:820
  9.2 0.0 copy-start.2
  9.2 0.0 copy-start.3
  9.2 2.5 %shard_map.101 = f32[72,32,128]{2,1,0:T(8,128)} custom-call(f32[72,64,128]{2,1,0:T(8,128)} %bitcast.22), custom_call_target="tpu_custom_call" | custom-call | tf_op jit(solution)/shard_map/pallas_call | solution.py:757
  11.7 1.6 %collective-permute-start.15 = (f32[72,32,128]{2,1,0:T(8,128)}, f32[72,32,128]{2,1,0:T(8,128)}, u32[]{:S(2)}, u32[]{:S(2)}) collective-permute-start(f32[72,32,128]{2,1,0:T(8,128)} %shard_map.101), channel_id=1, source_target_pairs={{0,1},{1,0},{2,3},{3,2},{4,5},{5,4},{6,7},{7,6},{8,9},{9,8},{10,11... | collective-permute-start | bytes 3538952 | tf_op jit(solution)/shard_map/ppermute | solution.py:859
  13.3 4.2 %all-to-all-done.in_ref = f32[8,96,128]{2,1,0:T(8,128)S(1)} async-done(((f32[8,96,128]{2,1,0:T(8,128)}), f32[8,96,128]{2,1,0:T(8,128)S(1)}, u32[]{:S(2)}, u32[]{:S(2)}) %all-to-all-start) | async-done | bytes 393248 | tf_op jit(solution)/shard_map/all_to_all | solution.py:820
  17.5 0.2 shard_map.96
  17.7 10.7 %all_to_all.25.in_ref = f32[8,96,128]{2,1,0:T(8,128)S(1)} all-to-all(f32[8,96,128]{2,1,0:T(8,128)S(1)} %shard_map.96), channel_id=1, replica_groups=mesh['space'=8,'tm'=4] {'space'}, dimensions={0} | all-to-all | bytes 786432 | tf_op jit(solution)/shard_map/all_to_all | solution.py:820
  28.4 4.2 %shard_map.97 = (f32[8,96,128]{2,1,0:T(8,128)S(1)}, f32[8,3,32,128]{3,2,1,0:T(8,128)}, f32[8,32,128]{2,1,0:T(8,128)}, f32[8,32,128]{2,1,0:T(8,128)}) custom-call(f32[8,96,128]{2,1,0:T(8,128)S(1)} %all_to_all.25.in_ref, f32[54,64,128]{2,1,0:T(8,128)S(1)} %bitcast.21, bf16[896,256]{1,0:T(8,128)(2,1)S(1)} %copy-done.2, bf16[896,256]{1,0:T(8,128)(2,1)S(1)} %copy-done.3), custom_call_target="tpu_custom_call" | custom-call | tf_op jit(solution)/shard_map/pallas_call | solution.py:757
  32.7 0.0 copy-start.1
  32.7 10.8 %all_to_all.26.in_ref = f32[8,96,128]{2,1,0:T(8,128)S(1)} all-to-all(f32[8,96,128]{2,1,0:T(8,128)S(1)} %get-tuple-element.40), channel_id=1, replica_groups=mesh['space'=8,'tm'=4] {'space'}, dimensions={0} | all-to-all | bytes 786432 | tf_op jit(solution)/shard_map/all_to_all | solution.py:820
  43.5 1.0 %shard_map.98 = f32[8,96,128]{2,1,0:T(8,128)} custom-call(f32[8,96,128]{2,1,0:T(8,128)S(1)} %all_to_all.26.in_ref, f32[2,9,16,128]{3,2,1,0:T(8,128)S(1)} %copy-done.6), custom_call_target="tpu_custom_call" | custom-call | tf_op jit(solution)/shard_map/pallas_call | solution.py:757
  44.5 3.5 %all-to-all-start.3 = ((f32[8,96,128]{2,1,0:T(8,128)}), f32[8,96,128]{2,1,0:T(8,128)S(1)}, u32[]{:S(2)}, u32[]{:S(2)}) async-start(f32[8,96,128]{2,1,0:T(8,128)} %shard_map.98), calls=%async_computation.3 | async-start | bytes 786432 | tf_op jit(solution)/shard_map/all_to_all | solution.py:820
  48.6 1.6 %collective-permute-start.12 = (f32[8,32,128]{2,1,0:T(8,128)}, f32[8,32,128]{2,1,0:T(8,128)S(1)}, u32[]{:S(2)}, u32[]{:S(2)}) collective-permute-start(f32[8,32,128]{2,1,0:T(8,128)} %get-tuple-element.43), channel_id=1, source_target_pairs={{0,1},{1,2},{2,3},{3,0},{4,5},{5,6},{6,7},{7,4},{8,9},{9,10},{10,1... | collective-permute-start | bytes 393224 | tf_op jit(solution)/shard_map/ppermute | solution.py:792
  50.3 6.0 %all-to-all-done.3.in_ref = f32[8,96,128]{2,1,0:T(8,128)S(1)} async-done(((f32[8,96,128]{2,1,0:T(8,128)}), f32[8,96,128]{2,1,0:T(8,128)S(1)}, u32[]{:S(2)}, u32[]{:S(2)}) %all-to-all-start.3) | async-done | bytes 393248 | tf_op jit(solution)/shard_map/all_to_all | solution.py:820
  56.2 0.7 copy-done.4
  57.0 1.0 %copy-done.5 = f32[8,96,128]{2,1,0:T(8,128)S(1)} copy-done((f32[8,96,128]{2,1,0:T(8,128)S(1)}, f32[8,96,128]{2,1,0:T(8,128)}, u32[]{:S(2)}) %copy-start.5) | copy-done | bytes 393240
  58.0 1.3 %shard_map.99 = (f32[8,3,32,128]{3,2,1,0:T(8,128)S(1)}, f32[8,32,128]{2,1,0:T(8,128)}, f32[8,32,128]{2,1,0:T(8,128)}) custom-call(f32[8,96,128]{2,1,0:T(8,128)S(1)} %copy-done.5, bf16[896,256]{1,0:T(8,128)(2,1)S(1)} %copy-done.2), custom_call_target="tpu_custom_call" | custom-call | tf_op jit(solution)/shard_map/pallas_call | solution.py:757
  59.3 7.2 %conditional.1 = (f32[8,32,128]{2,1,0:T(8,128)}, f32[8,32,128]{2,1,0:T(8,128)}, f32[8,32,128]{2,1,0:T(8,128)}) conditional(s32[]{:T(128)} %clamp.3, (f32[8,32,128]{2,1,0:T(8,128)}, f32[8,32,128]{2,1,0:T(8,128)}) %tuple.26, (f32[8,32,128]{2,1,0:T(8,128)}, f32[8,32,128]{2,1,0:T(8,128)}) %tuple.27, ...), branch_computations={%region_0.1_spmd, %region_1.2_spmd, %region_2.3_spmd, %region_3.4_... | conditional | bytes 1573008 | solution.py:902
  59.3 1.3 %collective-permute-start.3 = (f32[8,32,128]{2,1,0:T(8,128)}, f32[8,32,128]{2,1,0:T(8,128)}, u32[]{:S(2)}, u32[]{:S(2)}) collective-permute-start(f32[8,32,128]{2,1,0:T(8,128)} %get-tuple-element.18), channel_id=1, source_target_pairs={{1,0},{5,4},{9,8},{13,12},{17,16},{21,20},{25,24},{29,28}} | collective-permute-start | bytes 393224 | tf_op jit(solution)/shard_map/cond/branch_1_fun/ppermute | solution.py:895
  60.6 1.3 %collective-permute-start.4 = (f32[8,32,128]{2,1,0:T(8,128)}, f32[8,32,128]{2,1,0:T(8,128)}, u32[]{:S(2)}, u32[]{:S(2)}) collective-permute-start(f32[8,32,128]{2,1,0:T(8,128)} %get-tuple-element.18), channel_id=1, source_target_pairs={{1,2},{5,6},{9,10},{13,14},{17,18},{21,22},{25,26},{29,30}} | collective-permute-start | bytes 393224 | tf_op jit(solution)/shard_map/cond/branch_1_fun/ppermute | solution.py:895
  61.9 1.3 %collective-permute-start.5 = (f32[8,32,128]{2,1,0:T(8,128)}, f32[8,32,128]{2,1,0:T(8,128)}, u32[]{:S(2)}, u32[]{:S(2)}) collective-permute-start(f32[8,32,128]{2,1,0:T(8,128)} %get-tuple-element.19), channel_id=1, source_target_pairs={{1,3},{5,7},{9,11},{13,15},{17,19},{21,23},{25,27},{29,31}} | collective-permute-start | bytes 393224 | tf_op jit(solution)/shard_map/cond/branch_1_fun/ppermute | solution.py:895
  63.2 3.2 %collective-permute-done.3 = f32[8,32,128]{2,1,0:T(8,128)} collective-permute-done((f32[8,32,128]{2,1,0:T(8,128)}, f32[8,32,128]{2,1,0:T(8,128)}, u32[]{:S(2)}, u32[]{:S(2)}) %collective-permute-start.3) | collective-permute-done | bytes 131104 | tf_op jit(solution)/shard_map/cond/branch_1_fun/ppermute | solution.py:895
  66.5 6.6 %collective-permute-start.13 = (f32[8,32,128]{2,1,0:T(8,128)S(1)}, f32[8,32,128]{2,1,0:T(8,128)S(1)}, u32[]{:S(2)}, u32[]{:S(2)}) collective-permute-start(f32[8,32,128]{2,1,0:T(8,128)S(1)} %copy-done.7), channel_id=1, source_target_pairs={{0,2},{1,3},{2,0},{3,1},{4,6},{5,7},{6,4},{7,5},{8,10},{9,11},{10,... | collective-permute-start | bytes 393224 | tf_op jit(solution)/shard_map/ppermute | solution.py:792
  73.1 2.3 %collective-permute-start.14 = (f32[8,32,128]{2,1,0:T(8,128)}, f32[8,32,128]{2,1,0:T(8,128)S(1)}, u32[]{:S(2)}, u32[]{:S(2)}) collective-permute-start(f32[8,32,128]{2,1,0:T(8,128)} %get-tuple-element.43), channel_id=1, source_target_pairs={{0,3},{1,0},{2,1},{3,2},{4,7},{5,4},{6,5},{7,6},{8,11},{9,8},{10,9... | collective-permute-start | bytes 393224 | tf_op jit(solution)/shard_map/ppermute | solution.py:792
  76.8 3.2 %collective-permute-done.13.rest_1_ = f32[8,32,128]{2,1,0:T(8,128)S(1)} collective-permute-done((f32[8,32,128]{2,1,0:T(8,128)S(1)}, f32[8,32,128]{2,1,0:T(8,128)S(1)}, u32[]{:S(2)}, u32[]{:S(2)}) %collective-permute-start.13) | collective-permute-done | bytes 131104 | tf_op jit(solution)/shard_map/ppermute | solution.py:792
  80.0 3.9 %shard_map.102 = f32[32,4,128]{2,1,0:T(4,128)} custom-call(s32[1]{0:T(128)S(6)} %select_n.17.sink_ref, s32[1]{0:T(128)S(6)} %select_n.18.src_time_ref, s32[1]{0:T(128)S(6)} %max.3.src_site_ref, f32[8,3,32,128]{3,2,1,0:T(8,128)} %get-tuple-element.39.first_any, f32[8,3,32,128]{3,2,1,0:T(8,128)S(1)} %get-tuple-element.41.second_ref, ...), custom_call_target="tpu_custom_call" | custom-call | tf_op jit(solution)/shard_map/pallas_call | solution.py:757
  83.9 4.7 %all-to-all-start.4 = ((f32[32,4,128]{2,1,0:T(4,128)}), f32[32,4,128]{2,1,0:T(4,128)S(1)}, u32[]{:S(2)}, u32[]{:S(2)}) async-start(f32[32,4,128]{2,1,0:T(4,128)} %shard_map.102), calls=%async_computation.4 | async-start | bytes 131072 | tf_op jit(solution)/shard_map/all_to_all | solution.py:942
  88.6 5.2 %shard_map.100 = f32[54,64,128]{2,1,0:T(8,128)} custom-call(f32[54,64,128]{2,1,0:T(8,128)} %bitcast.20, f32[8,3,32,128]{3,2,1,0:T(8,128)} %get-tuple-element.39.first_any, bf16[896,256]{1,0:T(8,128)(2,1)} %constant.45.clone.inverse_ref.table_any, f32[8,3,32,128]{3,2,1,0:T(8,128)S(1)} %get-tuple-element.41.second_ref), custom_call_target="tpu_custom_call" | custom-call | tf_op jit(solution)/shard_map/pallas_call | solution.py:757
  93.8 2.3 %all-to-all-done.4.in_ref = f32[32,4,128]{2,1,0:T(4,128)S(1)} async-done(((f32[32,4,128]{2,1,0:T(4,128)}), f32[32,4,128]{2,1,0:T(4,128)S(1)}, u32[]{:S(2)}, u32[]{:S(2)}) %all-to-all-start.4) | async-done | bytes 65568 | tf_op jit(solution)/shard_map/all_to_all | solution.py:942
  96.1 0.7 shard_map.103
  (16 shorter events, 0.0 us)
Async XLA Ops:
  4.0 13.5 %all-to-all-start = ((f32[8,96,128]{2,1,0:T(8,128)}), f32[8,96,128]{2,1,0:T(8,128)S(1)}, u32[]{:S(2)}, u32[]{:S(2)}) async-start(f32[8,96,128]{2,1,0:T(8,128)} %shard_map.95), calls=%async_computation | async-start | bytes 786432 | tf_op jit(solution)/shard_map/all_to_all | solution.py:820
  9.2 8.3 %copy-start.6 = (f32[2,9,16,128]{3,2,1,0:T(8,128)S(1)}, f32[2,9,16,128]{3,2,1,0:T(8,128)}, u32[]{:S(2)}) copy-start(f32[2,9,16,128]{3,2,1,0:T(8,128)} %constant.46.clone.table_ref) | copy-start | bytes 442372
  9.2 19.3 %copy-start = (f32[1,3,2,3,3,2,4096]{6,5,4,3,2,1,0:T(2,128)S(1)}, f32[1,3,2,3,3,2,4096]{6,5,4,3,2,1,0:T(2,128)}, u32[]{:S(2)}) copy-start(f32[1,3,2,3,3,2,4096]{6,5,4,3,2,1,0:T(2,128)} %param.12) | copy-start | bytes 5308420
  9.2 19.3 %copy-start.2 = (bf16[896,256]{1,0:T(8,128)(2,1)S(1)}, bf16[896,256]{1,0:T(8,128)(2,1)}, u32[]{:S(2)}) copy-start(bf16[896,256]{1,0:T(8,128)(2,1)} %constant.45.clone.inverse_ref.table_any) | copy-start | bytes 1376260
  9.2 19.2 %copy-start.3 = (bf16[896,256]{1,0:T(8,128)(2,1)S(1)}, bf16[896,256]{1,0:T(8,128)(2,1)}, u32[]{:S(2)}) copy-start(bf16[896,256]{1,0:T(8,128)(2,1)} %constant.44.clone.table_any.forward_ref) | copy-start | bytes 1376260
  11.7 68.3 %collective-permute-start.15 = (f32[72,32,128]{2,1,0:T(8,128)}, f32[72,32,128]{2,1,0:T(8,128)}, u32[]{:S(2)}, u32[]{:S(2)}) collective-permute-start(f32[72,32,128]{2,1,0:T(8,128)} %shard_map.101), channel_id=1, source_target_pairs={{0,1},{1,0},{2,3},{3,2},{4,5},{5,4},{6,7},{7,6},{8,9},{9,8},{10,11... | collective-permute-start | bytes 3538952 | tf_op jit(solution)/shard_map/ppermute | solution.py:859
  32.7 33.8 %copy-start.7 = (f32[8,32,128]{2,1,0:T(8,128)S(1)}, f32[8,32,128]{2,1,0:T(8,128)}, u32[]{:S(2)}) copy-start(f32[8,32,128]{2,1,0:T(8,128)} %get-tuple-element.42.own_early_any) | copy-start | bytes 393220
  32.7 47.3 %copy-start.1 = (f32[2,36,2,4096]{3,2,1,0:T(2,128)S(1)}, f32[2,36,2,4096]{3,2,1,0:T(2,128)}, u32[]{:S(2)}) copy-start(f32[2,36,2,4096]{3,2,1,0:T(2,128)} %param.13) | copy-start | bytes 7077892
  44.5 11.7 %all-to-all-start.3 = ((f32[8,96,128]{2,1,0:T(8,128)}), f32[8,96,128]{2,1,0:T(8,128)S(1)}, u32[]{:S(2)}, u32[]{:S(2)}) async-start(f32[8,96,128]{2,1,0:T(8,128)} %shard_map.98), calls=%async_computation.3 | async-start | bytes 786432 | tf_op jit(solution)/shard_map/all_to_all | solution.py:820
  48.6 28.1 %collective-permute-start.12 = (f32[8,32,128]{2,1,0:T(8,128)}, f32[8,32,128]{2,1,0:T(8,128)S(1)}, u32[]{:S(2)}, u32[]{:S(2)}) collective-permute-start(f32[8,32,128]{2,1,0:T(8,128)} %get-tuple-element.43), channel_id=1, source_target_pairs={{0,1},{1,2},{2,3},{3,0},{4,5},{5,6},{6,7},{7,4},{8,9},{9,10},{10,1... | collective-permute-start | bytes 393224 | tf_op jit(solution)/shard_map/ppermute | solution.py:792
  56.2 0.7 copy-start.4
  57.0 1.0 %copy-start.5 = (f32[8,96,128]{2,1,0:T(8,128)S(1)}, f32[8,96,128]{2,1,0:T(8,128)}, u32[]{:S(2)}) copy-start(f32[8,96,128]{2,1,0:T(8,128)} %copy-done.4) | copy-start | bytes 1179652
  59.3 7.2 %collective-permute-start.3 = (f32[8,32,128]{2,1,0:T(8,128)}, f32[8,32,128]{2,1,0:T(8,128)}, u32[]{:S(2)}, u32[]{:S(2)}) collective-permute-start(f32[8,32,128]{2,1,0:T(8,128)} %get-tuple-element.18), channel_id=1, source_target_pairs={{1,0},{5,4},{9,8},{13,12},{17,16},{21,20},{25,24},{29,28}} | collective-permute-start | bytes 393224 | tf_op jit(solution)/shard_map/cond/branch_1_fun/ppermute | solution.py:895
  60.6 5.9 %collective-permute-start.4 = (f32[8,32,128]{2,1,0:T(8,128)}, f32[8,32,128]{2,1,0:T(8,128)}, u32[]{:S(2)}, u32[]{:S(2)}) collective-permute-start(f32[8,32,128]{2,1,0:T(8,128)} %get-tuple-element.18), channel_id=1, source_target_pairs={{1,2},{5,6},{9,10},{13,14},{17,18},{21,22},{25,26},{29,30}} | collective-permute-start | bytes 393224 | tf_op jit(solution)/shard_map/cond/branch_1_fun/ppermute | solution.py:895
  61.9 4.6 %collective-permute-start.5 = (f32[8,32,128]{2,1,0:T(8,128)}, f32[8,32,128]{2,1,0:T(8,128)}, u32[]{:S(2)}, u32[]{:S(2)}) collective-permute-start(f32[8,32,128]{2,1,0:T(8,128)} %get-tuple-element.19), channel_id=1, source_target_pairs={{1,3},{5,7},{9,11},{13,15},{17,19},{21,23},{25,27},{29,31}} | collective-permute-start | bytes 393224 | tf_op jit(solution)/shard_map/cond/branch_1_fun/ppermute | solution.py:895
  66.5 13.5 %collective-permute-start.13 = (f32[8,32,128]{2,1,0:T(8,128)S(1)}, f32[8,32,128]{2,1,0:T(8,128)S(1)}, u32[]{:S(2)}, u32[]{:S(2)}) collective-permute-start(f32[8,32,128]{2,1,0:T(8,128)S(1)} %copy-done.7), channel_id=1, source_target_pairs={{0,2},{1,3},{2,0},{3,1},{4,6},{5,7},{6,4},{7,5},{8,10},{9,11},{10,... | collective-permute-start | bytes 393224 | tf_op jit(solution)/shard_map/ppermute | solution.py:792
  73.1 6.8 %collective-permute-start.14 = (f32[8,32,128]{2,1,0:T(8,128)}, f32[8,32,128]{2,1,0:T(8,128)S(1)}, u32[]{:S(2)}, u32[]{:S(2)}) collective-permute-start(f32[8,32,128]{2,1,0:T(8,128)} %get-tuple-element.43), channel_id=1, source_target_pairs={{0,3},{1,0},{2,1},{3,2},{4,7},{5,4},{6,5},{7,6},{8,11},{9,8},{10,9... | collective-permute-start | bytes 393224 | tf_op jit(solution)/shard_map/ppermute | solution.py:792
  83.9 12.2 %all-to-all-start.4 = ((f32[32,4,128]{2,1,0:T(4,128)}), f32[32,4,128]{2,1,0:T(4,128)S(1)}, u32[]{:S(2)}, u32[]{:S(2)}) async-start(f32[32,4,128]{2,1,0:T(4,128)} %shard_map.102), calls=%async_computation.4 | async-start | bytes 131072 | tf_op jit(solution)/shard_map/all_to_all | solution.py:942

commit v3 on v2

--- a/solution.py
+++ b/solution.py
@@ -1,5 +1,6 @@
 import functools
 import math
+from typing import NamedTuple
 
 import jax
 import jax.numpy as jnp
@@ -213,10 +214,11 @@
     out_ref[...] = dot(high, first) + dot(low_ref[...], first) + dot(high, table_ref[size : 2 * size])
 
 
-def forward_transform(d_ref, table_ref, high_ref, low_ref, spec_ref, out_ref):
+def forward_transform(d_ref, table_ref, high_ref, low_ref, spec_ref, out_ref, out_any, sems):
     slots, _, half, lanes = d_ref.shape
-    parts = out_ref.shape[0] // 4
+    parts = out_ref.shape[1] // 4
     rows = half // parts
+    size = 4 * half
     for slot in range(slots):
         stacked = jnp.concatenate(
             [
@@ -233,16 +235,24 @@
             at = (slot * 4 + f) * half
             high_ref[at : at + half, :] = high
             low_ref[at : at + half, :] = low
-    right_transform(high_ref, low_ref, table_ref, spec_ref)
+    copies = []
     for slot in range(slots):
+        rows_of = pl.ds(slot * size, size)
+        right_transform(high_ref.at[rows_of], low_ref.at[rows_of], table_ref, spec_ref.at[rows_of])
         for f in range(4):
             for part in range(parts):
                 at = (slot * 4 + f) * half + part * rows
                 for c in range(2):
-                    to = (slot * 2 + c) * rows
-                    out_ref[f * parts + part, to : to + rows, :] = spec_ref[
+                    out_ref[slot, f * parts + part, c * rows : (c + 1) * rows, :] = spec_ref[
                         at : at + rows, c * lanes : (c + 1) * lanes
                     ]
+        copies.append(
+            pltpu.make_async_copy(
+                out_ref.at[slot], out_any.at[:, pl.ds(slot * 2 * rows, 2 * rows), :], sems.at[slot]
+            )
+        )
+        copies[-1].start()
+    return copies
 
 
 def inverse_transform(in_ref, table_ref, high_ref, low_ref, spec_ref, x_ref):
@@ -368,28 +378,55 @@
         d_ref[planes, comp] = before
 
 
-def cut_kernel(split, source_any, *rest):
-    cut_refs = rest[: split - 1]
-    held_ref, sems = rest[split - 1 :]
-    per = held_ref.shape[2]
-    reads, writes = [], []
-    for shift, cut in enumerate(cut_refs, 1):
-        rows = pl.ds(share_start(shift, split, per), per)
-        reads.append(
-            pltpu.make_async_copy(source_any.at[:, rows, :], held_ref.at[shift - 1], sems.at[0, shift - 1])
-        )
-        writes.append(pltpu.make_async_copy(held_ref.at[shift - 1], cut, sems.at[1, shift - 1]))
-    for copy in reads:
-        copy.start()
-    for read, write in zip(reads, writes):
-        read.wait()
-        write.start()
-    for write in writes:
-        write.wait()
-
-
-def start_kernel(links_any, table_any, out_ref, links_ref, table_ref, v_ref, d_ref, stack_ref, moved_ref, high_ref, low_ref, spec_ref, sems):
+class Split(NamedTuple):
+    times: int
+    group: int
+    wide: int
+    near: int
+
+    @property
+    def rows(self):
+        return self.wide + self.near
+
+    @property
+    def offset(self):
+        return self.times * self.wide
+
+    @property
+    def total(self):
+        return self.offset + self.group * self.near
+
+    @property
+    def peers(self):
+        groups = self.times // self.group
+        steps = [(g, m) for g in range(groups) for m in range(self.group)]
+        return steps[1:]
+
+    def block(self, step):
+        return self.wide if step[0] else self.rows
+
+    def moved(self, device, step, back=False):
+        sign = -1 if back else 1
+        groups = self.times // self.group
+        home = (device // self.group + sign * step[0]) % groups
+        return home * self.group + (device % self.group + sign * step[1]) % self.group
+
+    def starts(self, device):
+        wide = device * self.wide
+        near = self.offset + device % self.group * self.near
+        if isinstance(device, int):
+            return wide, near
+        return pl.multiple_of(wide, 8), pl.multiple_of(near, 8)
+
+
+def start_kernel(split, links_any, table_any, source_any, out_any, *rest):
+    peers = split.peers
+    cut_refs, held_refs = rest[: len(peers)], rest[len(peers) : 2 * len(peers)]
+    links_ref, table_ref, v_ref, d_ref, stack_ref, moved_ref, high_ref, low_ref, spec_ref, out_ref, sems, cut_sems, out_sems = rest[
+        2 * len(peers) :
+    ]
     _, _, planes, half, _ = v_ref.shape
+    mine = lax.axis_index("tm")
     copies = [
         pltpu.make_async_copy(
             links_any.at[pl.ds(18 * direction, 18)], links_ref.at[pl.ds(18 * direction, 18)], sems.at[direction]
@@ -397,7 +434,18 @@
         for direction in range(3)
     ]
     copies.append(pltpu.make_async_copy(table_any, table_ref, sems.at[3]))
-    for copy in copies:
+    reads, writes = [], []
+    for k, (step, cut, held) in enumerate(zip(peers, cut_refs, held_refs)):
+        wide, near = split.starts(split.moved(mine, step))
+        pieces = [(wide, 0, split.wide)] if step[0] else [(wide, 0, split.wide), (near, split.wide, split.near)]
+        for part, (start, to, size) in enumerate(pieces):
+            reads.append(
+                pltpu.make_async_copy(
+                    source_any.at[:, pl.ds(start, size), :], held.at[:, pl.ds(to, size), :], cut_sems.at[part, k]
+                )
+            )
+        writes.append(pltpu.make_async_copy(held, cut, cut_sems.at[2, k]))
+    for copy in copies + reads:
         copy.start()
     for direction in range(3):
         copies[direction].wait()
@@ -408,9 +456,15 @@
                 v_ref[direction, comp, plane, aligned(chunk), :] = value
 
         chunk_loop(planes, half // 8, step)
+    for copy in reads:
+        copy.wait()
+    for copy in writes:
+        copy.start()
     copies[3].wait()
     divergence(v_ref, table_ref, stack_ref, moved_ref, d_ref)
-    forward_transform(d_ref, table_ref, high_ref, low_ref, spec_ref, out_ref)
+    outs = forward_transform(d_ref, table_ref, high_ref, low_ref, spec_ref, out_ref, out_any, out_sems)
+    for copy in writes + outs:
+        copy.wait()
 
 
 def convolve_kernel(planes, in_ref, table_ref, out_ref):
@@ -448,35 +502,47 @@
     lax.fori_loop(0, 2 * (rows // step), run, 0)
 
 
-def flatten_shares(x_ref, flat_ref, planes):
+def flatten_shares(x_ref, flat_ref, planes, split):
     half = x_ref.shape[2]
+    first = half // 2
     if flat_ref.shape[1] > planes * half:
         flat_ref[...] = jnp.zeros_like(flat_ref)
     for comp in range(8):
         for plane in range(planes):
-            flat_ref[comp, pl.ds(plane, half, stride=planes), :] = x_ref[comp, plane]
-
-
-def share_start(shift, count, per):
-    return pl.multiple_of((lax.axis_index("tm") + shift) % count * per, 8)
-
-
-def middle_kernel(shares, in_ref, links_ref, inverse_ref, forward_ref, *rest):
-    out_ref, x_any = rest[:2]
-    share_refs = rest[2 : 2 + shares]
-    x_ref, g_ref, y_ref, v_ref, d_ref, stack_ref, moved_ref, high_ref, low_ref, spec_ref, flat_ref, sems = rest[2 + shares :]
+            value = x_ref[comp, plane]
+            flat_ref[comp, pl.ds(plane, first, stride=planes), :] = value[:first]
+            flat_ref[comp, pl.ds(split.offset + plane, half - first, stride=planes), :] = value[first:]
+
+
+def share_copies(flat_ref, share_refs, split, devices, sems):
+    copies = []
+    for k, (share_ref, device) in enumerate(zip(share_refs, devices)):
+        wide, near = split.starts(device)
+        copies.append(
+            pltpu.make_async_copy(
+                flat_ref.at[:, pl.ds(wide, split.wide), :], share_ref.at[:, : split.wide, :], sems.at[0, k]
+            )
+        )
+        copies.append(
+            pltpu.make_async_copy(
+                flat_ref.at[:, pl.ds(near, split.near), :], share_ref.at[:, split.wide :, :], sems.at[1, k]
+            )
+        )
+    return copies
+
+
+def middle_kernel(split, in_ref, links_ref, inverse_ref, forward_ref, *rest):
+    out_any, x_any = rest[:2]
+    share_refs = rest[2 : 2 + split.times]
+    x_ref, g_ref, y_ref, v_ref, d_ref, stack_ref, moved_ref, high_ref, low_ref, spec_ref, flat_ref, out_ref, sems, share_sems, out_sems = rest[2 + split.times :]
     _, slots, half, _ = x_ref.shape
     planes = slots - 1
-    per = share_refs[0].shape[1]
     inverse_transform(in_ref, inverse_ref, high_ref, low_ref, spec_ref, x_ref)
-    flatten_shares(x_ref, flat_ref, planes)
-    copies = [
-        pltpu.make_async_copy(
-            flat_ref.at[:, pl.ds(share_start(shift, shares, per), per), :], share_refs[shift], sems.at[shift]
-        )
-        for shift in range(shares)
-    ]
-    copies.append(pltpu.make_async_copy(x_ref, x_any, sems.at[shares]))
+    flatten_shares(x_ref, flat_ref, planes, split)
+    mine = lax.axis_index("tm")
+    devices = [(mine + shift) % split.times for shift in range(split.times)]
+    copies = share_copies(flat_ref, share_refs, split, devices, share_sems)
+    copies.append(pltpu.make_async_copy(x_ref, x_any, sems))
     for copy in copies:
         copy.start()
 
@@ -501,25 +567,22 @@
 
     chunk_loop(planes, half // 8, rotate_step)
     divergence(v_ref, forward_ref, stack_ref, moved_ref, d_ref)
-    forward_transform(d_ref, forward_ref, high_ref, low_ref, spec_ref, out_ref)
+    copies += forward_transform(
+        d_ref, forward_ref, high_ref, low_ref, spec_ref, out_ref, out_any, out_sems
+    )
     for copy in copies:
         copy.wait()
 
 
-def last_transform_kernel(in_ref, inverse_ref, x_ref, *rest):
-    share_refs = rest[:-5]
-    high_ref, low_ref, spec_ref, flat_ref, sems = rest[-5:]
-    per = share_refs[0].shape[1]
+def last_transform_kernel(split, in_ref, inverse_ref, x_ref, *rest):
+    share_refs = rest[: split.times]
+    high_ref, low_ref, spec_ref, flat_ref = rest[split.times :]
     inverse_transform(in_ref, inverse_ref, high_ref, low_ref, spec_ref, x_ref)
-    flatten_shares(x_ref, flat_ref, x_ref.shape[1] - 1)
-    copies = [
-        pltpu.make_async_copy(flat_ref.at[:, to * per : (to + 1) * per, :], share_ref, sems.at[to])
-        for to, share_ref in enumerate(share_refs)
-    ]
-    for copy in copies:
-        copy.start()
-    for copy in copies:
-        copy.wait()
+    flatten_shares(x_ref, flat_ref, x_ref.shape[1] - 1, split)
+    for device, share_ref in enumerate(share_refs):
+        wide, near = split.starts(device)
+        share_ref[:, : split.wide, :] = flat_ref[:, wide : wide + split.wide, :]
+        share_ref[:, split.wide :, :] = flat_ref[:, near : near + split.near, :]
 
 
 def total_of(first, second):
@@ -599,13 +662,23 @@
     return total
 
 
-def sink_kernel(times, split, sink_ref, src_time_ref, src_site_ref, first_any, second_ref, source_ref, own_early_any, *rest):
-    early = (own_early_any,) + rest[: times - 1]
-    own = rest[times - 1 : times - 1 + split]
-    late = rest[times - 1 + split : 2 * times - 2 + split]
-    partners_any = rest[2 * times - 2 + split : 2 * times - 3 + 2 * split]
-    out_ref, partner_ref, x_ref, gauge_ref, sum_ref, before_ref, anchor_ref, sems = rest[2 * times - 3 + 2 * split :]
-    per = early[0].shape[1]
+def load_rows(ref, rows):
+    return [[(ref[3 * i + j, rows, :], ref[9 + 3 * i + j, rows, :]) for j in range(3)] for i in range(3)]
+
+
+def sink_kernel(split, sink_ref, src_time_ref, src_site_ref, first_any, second_ref, source_ref, own_early_any, *rest):
+    times, group, per = split.times, split.group, split.rows
+    rest = list(rest)
+
+    def take(count):
+        taken = rest[:count]
+        del rest[:count]
+        return taken
+
+    early = [own_early_any] + take(times - 1)
+    own, late = take(times), take(times - 1)
+    partners_any = take(times - 1)
+    out_ref, near_ref, wide_ref, x_ref, gauge_ref, sum_ref, before_ref, anchor_ref, sems = rest
     pairs = source_ref.shape[0] // 2
     groups = pairs // 3
     _, slots, half, lanes = second_ref.shape
@@ -620,9 +693,10 @@
     block = pl.ds(pl.multiple_of(row // 8 * 8, 8), 8)
     before = pltpu.make_async_copy(first_any.at[:, safe, block, :], before_ref, sems.at[0])
     fetches = [pltpu.make_async_copy(early[0], x_ref.at[k], sems.at[1 + k]) for k in range(2)]
+    held = [near_ref.at[k] for k in range(group - 1)] + [wide_ref.at[k] for k in range(times - group)]
     partners = [
-        pltpu.make_async_copy(partner, partner_ref.at[k], sems.at[3 + k])
-        for k, partner in enumerate(partners_any)
+        pltpu.make_async_copy(partner, to, sems.at[3 + k])
+        for k, (partner, to) in enumerate(zip(partners_any, held))
     ]
 
     def fetch(condition, value, to):
@@ -632,38 +706,39 @@
 
     for shift in range(times):
         fetch((mine - sink) % times == shift, early[shift], 0)
-    for at in range(split):
-        fetch((mine == sink) & (mine % split == at), own[at], 1)
+    for at in range(times):
+        fetch((mine == sink) & (mine == at), own[at], 1)
     for at in range(times - 1):
         fetch((mine != sink) & (jnp.where(mine > sink, mine - 1, mine) == at), late[at], 1)
     for copy in partners:
         copy.start()
     before.start()
-    sum_ref[...] = jnp.zeros_like(sum_ref)
-    for copy in fetches:
-        copy.wait()
     chunks = per // 8
-    for chunk in range(chunks):
-        rows = slice(chunk * 8, chunk * 8 + 8)
-        gauge = total_of([x_ref[0, k, rows, :] for k in range(8)], [x_ref[1, k, rows, :] for k in range(8)])
-        for i in range(3):
-            for j in range(3):
-                gauge_ref[3 * i + j, rows, :] = gauge[i][j][0]
-                gauge_ref[9 + 3 * i + j, rows, :] = gauge[i][j][1]
-    for shift in range(split):
-        if shift:
-            partners[shift - 1].wait()
-        block_ref = partner_ref.at[shift - 1] if shift else source_ref
-        offset = 0 if shift else share_start(0, split, per)
-        base = (mine - mine % split + (mine - shift) % split) * pairs
-
-        def run(group, carry, block_ref=block_ref, offset=offset, base=base):
+    for number in range(2):
+        fetches[number].wait()
+        for chunk in range(chunks):
+            rows = slice(chunk * 8, chunk * 8 + 8)
+            turn = exponential([x_ref[number, k, rows, :] for k in range(8)])
+            if number:
+                turn = [row_times(turn[i], load_rows(gauge_ref, rows)) for i in range(3)]
+            for i in range(3):
+                for j in range(3):
+                    gauge_ref[3 * i + j, rows, :] = turn[i][j][0]
+                    gauge_ref[9 + 3 * i + j, rows, :] = turn[i][j][1]
+
+    def accumulate(block_ref, offset, first, count, source_device, add):
+        base = source_device * pairs
+
+        def run(group_at, carry):
             sums = [None] * 3
-            for chunk in range(chunks):
-                rows = slice(chunk * 8, chunk * 8 + 8)
+            for chunk in range(count // 8):
+                rows = slice(first + chunk * 8, first + chunk * 8 + 8)
                 own_rows = pl.ds(pl.multiple_of(offset + chunk * 8, 8), 8)
                 column = [
-                    (block_ref[3 * group + c, own_rows, :], block_ref[pairs + 3 * group + c, own_rows, :])
+                    (
+                        block_ref[3 * group_at + c, own_rows, :],
+                        block_ref[pairs + 3 * group_at + c, own_rows, :],
+                    )
                     for c in range(3)
                 ]
                 for a in range(3):
@@ -673,12 +748,23 @@
                         )
                         sums[a] = part if sums[a] is None else (sums[a][0] + part[0], sums[a][1] + part[1])
             for a in range(3):
-                to = pl.ds(pl.multiple_of((base + 3 * group + a) * 8, 8), 8)
-                sum_ref[0, to, :] = sums[a][0]
-                sum_ref[1, to, :] = sums[a][1]
+                to = pl.ds(pl.multiple_of((base + 3 * group_at + a) * 8, 8), 8)
+                re, im = sums[a]
+                if add:
+                    re, im = re + sum_ref[0, to, :], im + sum_ref[1, to, :]
+                sum_ref[0, to, :] = re
+                sum_ref[1, to, :] = im
             return carry
 
         lax.fori_loop(0, groups, run, 0, unroll=2 if groups % 2 == 0 else 1)
+
+    wide_start, near_start = split.starts(mine)
+    accumulate(source_ref, wide_start, 0, split.wide, mine, False)
+    accumulate(source_ref, near_start, split.wide, split.near, mine, True)
+    for k, step in enumerate(split.peers):
+        partners[k].wait()
+        owner = split.moved(mine, step, back=True)
+        accumulate(held[k], 0, 0, split.block(step), owner, False)
     before.wait()
     total = total_of([before_ref[k] for k in range(8)], [second_ref[k, safe, block, :] for k in range(8)])
     wide = (8, lanes)
@@ -775,8 +861,9 @@
     parts = count // 4
     rows = half // parts
     sites = planes * half
-    split = 2 if times % 2 == 0 else 1
-    per = 8 * -(-sites // (8 * split))
+    group = 2 if times % 2 == 0 else 1
+    spread = sites // 2
+    split = Split(times, group, 8 * -(-spread // (8 * times)), 8 * -(-(sites - spread) // (8 * group)))
     pairs = propagator.shape[1]
 
     forward = jnp.asarray(transform_table(side, False))
@@ -790,9 +877,6 @@
 
     def forwarded(value, shift):
         return lax.ppermute(value, "tm", [(i, (i + shift) % times) for i in range(times)])
-
-    def within(i, shift):
-        return i - i % split + (i + shift) % split
 
     spectrum_shape = shape(count, slots * 2 * rows, lanes)
     transform_scratch = [
@@ -812,9 +896,10 @@
         VMEM((18 * planes * half, 2 * lanes), BF16),
         VMEM((18 * planes * half, 2 * lanes), F32),
     ]
-    flat_scratch = [VMEM((8, per * split, lanes), F32)]
+    out_scratch = [VMEM((slots, count, 2 * rows, lanes), F32)]
+    flat_scratch = [VMEM((8, split.total, lanes), F32)]
     algebra_shape = shape(8, slots, half, lanes)
-    share_shapes = [shape(8, per, lanes)] * split
+    share_shapes = [shape(8, split.rows, lanes)] * times
 
     def turn(spectrum):
         return lax.all_to_all(spectrum, "space", 0, 0, tiled=True)
@@ -831,41 +916,46 @@
         return out
 
     source = interleave(propagator, 2 * pairs)
-    if per * split > sites:
-        source = jnp.pad(source, ((0, 0), (0, per * split - sites), (0, 0)))
+    if split.total > sites:
+        fill = jnp.zeros((2 * pairs, split.offset - spread, lanes), F32)
+        source = jnp.concatenate([source[:, :spread], fill, source[:, spread:]], axis=1)
     scalars = [sink_time % times, src_time % times, jnp.maximum(src_site, 0)]
-    (spectrum,) = call(
-        start_kernel,
-        [spectrum_shape],
-        [VMEM_SPEC],
-        [lattice, forward],
-        [HBM_SPEC] * 2,
-        [VMEM(lattice.shape, F32), VMEM(forward.shape, BF16)]
+    cut_shapes = [shape(2 * pairs, split.block(step), lanes) for step in split.peers]
+    spectrum, *cuts = call(
+        functools.partial(start_kernel, split),
+        [spectrum_shape] + cut_shapes,
+        [HBM_SPEC] * times,
+        [lattice, forward, source],
+        [HBM_SPEC] * 3,
+        [VMEM(cut.shape, F32) for cut in cut_shapes]
+        + [VMEM(lattice.shape, F32), VMEM(forward.shape, BF16)]
         + divergence_scratch
         + shift_scratch
         + transform_scratch
-        + [pltpu.SemaphoreType.DMA((4,))],
-    )
-    spectrum, uncut = lax.optimization_barrier((spectrum, source))
-    cuts = call(
-        functools.partial(cut_kernel, split),
-        [shape(2 * pairs, per, lanes)] * (split - 1),
-        [HBM_SPEC] * (split - 1),
-        [uncut],
-        [HBM_SPEC],
-        [VMEM((split - 1, 2 * pairs, per, lanes), F32), pltpu.SemaphoreType.DMA((2, split - 1))],
-    )
+        + out_scratch
+        + [
+            pltpu.SemaphoreType.DMA((4,)),
+            pltpu.SemaphoreType.DMA((3, times - 1)),
+            pltpu.SemaphoreType.DMA((slots,)),
+        ],
+    )
+    held_scratch = [
+        VMEM((max(1, group - 1), 2 * pairs, split.rows, lanes), F32),
+        VMEM((max(1, times - group), 2 * pairs, split.wide, lanes), F32),
+    ]
+    scalars = [sink_time % times, src_time % times, jnp.maximum(src_site, 0)]
     sources = [
-        lax.ppermute(block, "tm", [(i, within(i, shift)) for i in range(times)])
-        for shift, block in enumerate(cuts, 1)
-    ]
+        lax.ppermute(cut, "tm", [(i, split.moved(i, step)) for i in range(times)])
+        for step, cut in zip(split.peers, cuts)
+    ]
+
     spectrum = turn(spectrum)
     spectrum = convolve(spectrum)
     spectrum = turn(spectrum)
     spectrum, first, *early = call(
         functools.partial(middle_kernel, split),
         [spectrum_shape, algebra_shape] + share_shapes,
-        [VMEM_SPEC] + [HBM_SPEC] * (1 + split),
+        [HBM_SPEC] * (2 + times),
         [spectrum, lattice, inverse, forward],
         [VMEM_SPEC] * 4,
         [VMEM(algebra_shape.shape, F32)]
@@ -874,25 +964,30 @@
         + shift_scratch
         + transform_scratch
         + flat_scratch
-        + [pltpu.SemaphoreType.DMA((split + 1,))],
-    )
-    first_shares = [forwarded(early[shift % split], shift) for shift in range(1, times)]
+        + out_scratch
+        + [
+            pltpu.SemaphoreType.DMA,
+            pltpu.SemaphoreType.DMA((2, times)),
+            pltpu.SemaphoreType.DMA((slots,)),
+        ],
+    )
+    first_shares = [forwarded(early[shift], shift) for shift in range(1, times)]
     spectrum = turn(spectrum)
     spectrum = convolve(spectrum)
     spectrum = turn(spectrum)
     second, *shares = call(
-        last_transform_kernel,
+        functools.partial(last_transform_kernel, split),
         [algebra_shape] + share_shapes,
-        [VMEM_SPEC] + [HBM_SPEC] * split,
+        [VMEM_SPEC] * (1 + times),
         [spectrum, inverse],
         [VMEM_SPEC] * 2,
-        transform_scratch + flat_scratch + [pltpu.SemaphoreType.DMA((split,))],
+        transform_scratch + flat_scratch,
     )
 
     def sent_from(source_index):
         def send(*blocks):
             return tuple(
-                lax.ppermute(blocks[to % split], "tm", [(source_index, to)])
+                lax.ppermute(blocks[to], "tm", [(source_index, to)])
                 for to in range(times)
                 if to != source_index
             )
@@ -919,7 +1014,7 @@
     width = -(-(SC * SC + 24) // lanes)
     devices = count * times
     (payload,) = call(
-        functools.partial(sink_kernel, times, split),
+        functools.partial(sink_kernel, split),
         [shape(devices, 2 * width, lanes)],
         [VMEM_SPEC],
         scalars + [first, second, source, early[0]] + first_shares + shares + list(second_shares) + sources,
@@ -927,16 +1022,16 @@
         + [HBM_SPEC]
         + [VMEM_SPEC] * 2
         + [HBM_SPEC]
-        + [ANY_SPEC] * (times - 1)
-        + [HBM_SPEC] * (times - 2 + 2 * split),
-        [
-            VMEM((max(1, split - 1), 2 * pairs, per, lanes), F32),
-            VMEM((2, 8, per, lanes), F32),
-            VMEM((18, per, lanes), F32),
+        + [ANY_SPEC] * (2 * times - 1)
+        + [HBM_SPEC] * (2 * times - 2),
+        held_scratch
+        + [
+            VMEM((2, 8, split.rows, lanes), F32),
+            VMEM((18, split.rows, lanes), F32),
             VMEM((2, SC * SC * 8, lanes), F32),
             VMEM((8, 8, lanes), F32),
             VMEM((24, lanes), F32),
-            pltpu.SemaphoreType.DMA((2 + split,)),
+            pltpu.SemaphoreType.DMA((2 + times,)),
         ],
     )
     gathered = lax.all_to_all(payload, ("space", "tm"), 0, 0, tiled=True)

time: 97.5 us -> 111 us (1.14)
  waiting for transfers between devices: 18.9 us -> 28.9 us
  blocking collectives: 21.5 us -> 24.3 us
  starting transfers between devices: 29.5 us -> 31.1 us
  Pallas kernels: 22.4 us -> 20.9 us
    ppermute x4 -> x6, starting transfers between devices: 5.56 us -> 16.1 us  [the longest x3 12.2 us: body(): lax.ppermute(cut, 'tm', [(i, split.moved(i, step)) for i in range(times)])]
    ppermute x3, starting transfers between devices: 10.6 us -> 3.88 us  [forwarded(): lax.ppermute(value, 'tm', [(i, (i + shift) % times) for i in range(times)])]
    ppermute x3, waiting for transfers between devices: 3.21 us -> 9.39 us  [forwarded(): lax.ppermute(value, 'tm', [(i, (i + shift) % times) for i in range(times)])]
    all_to_all x2, blocking collectives: 21.5 us -> 24.3 us  [turn(): return lax.all_to_all(spectrum, 'space', 0, 0, tiled=True)]
    ppermute x4 -> x6, waiting for transfers between devices: 3.26 us -> 5.65 us  [the longest x3 2.91 us: body(): lax.ppermute(cut, 'tm', [(i, split.moved(i, step)) for i in range(times)])]
    all_to_all x2, starting transfers between devices: 8.66 us -> 7.05 us  [turn(): return lax.all_to_all(spectrum, 'space', 0, 0, tiled=True)]
    pallas_call x9 -> x8, Pallas kernels: 22.4 us -> 20.9 us  [call(): pl.pallas_call(kernel, out_shape=outs, in_specs=in_specs, out_specs=out_s...]
    all_to_all x2, waiting for transfers between devices: 10.1 us -> 11.5 us  [turn(): return lax.all_to_all(spectrum, 'space', 0, 0, tiled=True)]
  transfers between devices with their start and end apart: 10 -> 12, of which waited for: 5 -> 7; matrix products, arithmetic and copies ran while one was open for 0% -> 0% of each run, Pallas kernels for 15% -> 7%
where the time goes in v3:
time: 111 us; the launch traced here: 110 us
  starting transfers between devices  31.1 us (28%)
  waiting for transfers between devices  28.9 us (26%)
  blocking collectives  24.3 us (22%)
  Pallas kernels  20.9 us (19%)
  between operations  2.76 us (2%)
  local copies, waits for them, and re-layouts  2.42 us (2%)
    all_to_all x2, blocking collectives, turn(): return lax.all_to_all(spectrum, 'space', 0, 0, tiled=True)  24.3 us
    pallas_call x8, Pallas kernels, call(): pl.pallas_call(kernel, out_shape=outs, in_specs=in_specs, out_specs=out_s...  20.9 us
    ppermute x3, starting transfers between devices, body(): lax.ppermute(cut, 'tm', [(i, split.moved(i, step)) for i in range(times)])  12.2 us
    all_to_all x2, waiting for transfers between devices, turn(): return lax.all_to_all(spectrum, 'space', 0, 0, tiled=True)  11.5 us
    ppermute x3, waiting for transfers between devices, forwarded(): lax.ppermute(value, 'tm', [(i, (i + shift) % times) for i in range(times)])  9.39 us
    all_to_all x2, starting transfers between devices, turn(): return lax.all_to_all(spectrum, 'space', 0, 0, tiled=True)  7.05 us
    all_to_all x1, starting transfers between devices, body(): gathered = lax.all_to_all(payload, ('space', 'tm'), 0, 0, tiled=True)  4.16 us
    ppermute x3, starting transfers between devices, forwarded(): lax.ppermute(value, 'tm', [(i, (i + shift) % times) for i in range(times)])  3.88 us
  transfers between devices with their start and end apart: 12, of which 7 were waited for; matrix products, arithmetic and copies ran while one was open for 0% of the time, Pallas kernels for 7%

profile of v3, /device:TPU:0, one launch (start us, length us, event | category | flops | bytes accessed | tf_op | source)
XLA Modules:
  0.0 110.4 jit_solution(195790556756130820)
XLA Ops:
  0.7 3.7 %shard_map.95 = (f32[8,96,128]{2,1,0:T(8,128)}, f32[72,24,128]{2,1,0:T(8,128)}, f32[72,8,128]{2,1,0:T(8,128)}, f32[72,8,128]{2,1,0:T(8,128)}) custom-call(f32[54,64,128]{2,1,0:T(8,128)} %bitcast.19, bf16[896,256]{1,0:T(8,128)(2,1)} %constant.44.clone.table_any.forward_ref, f32[72,64,128]{2,1,0:T(8,128)} %bitcast.22), custom_call_target="tpu_custom_call" | custom-call | tf_op jit(solution)/shard_map/pallas_call | solution.py:843
  4.4 13.6 %all_to_all.25.in_ref = f32[8,96,128]{2,1,0:T(8,128)S(1)} all-to-all(f32[8,96,128]{2,1,0:T(8,128)} %get-tuple-element.56), channel_id=1, replica_groups=mesh['space'=8,'tm'=4] {'space'}, dimensions={0} | all-to-all | bytes 786432 | tf_op jit(solution)/shard_map/all_to_all | solution.py:905
  18.0 0.2 shard_map.96
  18.3 10.7 %all_to_all.26.in_ref = f32[8,96,128]{2,1,0:T(8,128)S(1)} all-to-all(f32[8,96,128]{2,1,0:T(8,128)S(1)} %shard_map.96), channel_id=1, replica_groups=mesh['space'=8,'tm'=4] {'space'}, dimensions={0} | all-to-all | bytes 786432 | tf_op jit(solution)/shard_map/all_to_all | solution.py:905
  29.0 4.9 %shard_map.97 = (f32[8,96,128]{2,1,0:T(8,128)}, f32[8,3,32,128]{3,2,1,0:T(8,128)}, f32[8,24,128]{2,1,0:T(8,128)}, f32[8,24,128]{2,1,0:T(8,128)}, f32[8,24,128]{2,1,0:T(8,128)}, /*index=5*/f32[8,24,128]{2,1,0:T(8,128)}) custom-call(f32[8,96,128]{2,1,0:T(8,128)S(1)} %all_to_all.26.in_ref, f32[54,64,128]{2,1,0:T(8,128)S(1)} %bitcast.21, ...), custom_call_target="tpu_custom_call" | custom-call | tf_op jit(solution)/shard_map/pallas_call | solution.py:843
  34.0 3.6 %all-to-all-start.2 = ((f32[8,96,128]{2,1,0:T(8,128)}), f32[8,96,128]{2,1,0:T(8,128)S(1)}, u32[]{:S(2)}, u32[]{:S(2)}) async-start(f32[8,96,128]{2,1,0:T(8,128)} %get-tuple-element.58), calls=%async_computation.2 | async-start | bytes 786432 | tf_op jit(solution)/shard_map/all_to_all | solution.py:905
  37.6 1.6 %collective-permute-start.15 = (f32[72,24,128]{2,1,0:T(8,128)}, f32[72,24,128]{2,1,0:T(8,128)}, u32[]{:S(2)}, u32[]{:S(2)}) collective-permute-start(f32[72,24,128]{2,1,0:T(8,128)} %get-tuple-element.71), channel_id=1, source_target_pairs={{0,1},{1,0},{2,3},{3,2},{4,5},{5,4},{6,7},{7,6},{8,9},{9,8},{10,11... | collective-permute-start | bytes 2654216 | tf_op jit(solution)/shard_map/ppermute | solution.py:948
  39.2 6.6 %all-to-all-done.2.in_ref = f32[8,96,128]{2,1,0:T(8,128)S(1)} async-done(((f32[8,96,128]{2,1,0:T(8,128)}), f32[8,96,128]{2,1,0:T(8,128)S(1)}, u32[]{:S(2)}, u32[]{:S(2)}) %all-to-all-start.2) | async-done | bytes 393248 | tf_op jit(solution)/shard_map/all_to_all | solution.py:905
  45.8 1.0 shard_map.98
  46.8 3.5 %all-to-all-start.3 = ((f32[8,96,128]{2,1,0:T(8,128)}), f32[8,96,128]{2,1,0:T(8,128)S(1)}, u32[]{:S(2)}, u32[]{:S(2)}) async-start(f32[8,96,128]{2,1,0:T(8,128)} %shard_map.98), calls=%async_computation.3 | async-start | bytes 786432 | tf_op jit(solution)/shard_map/all_to_all | solution.py:905
  50.3 2.7 %collective-permute-start.16 = (f32[72,8,128]{2,1,0:T(8,128)}, f32[72,8,128]{2,1,0:T(8,128)S(1)}, u32[]{:S(2)}, u32[]{:S(2)}) collective-permute-start(f32[72,8,128]{2,1,0:T(8,128)} %get-tuple-element.72), channel_id=1, source_target_pairs={{0,2},{1,3},{2,0},{3,1},{4,6},{5,7},{6,4},{7,5},{8,10},{9,11},{10,... | collective-permute-start | bytes 884744 | tf_op jit(solution)/shard_map/ppermute | solution.py:948
  53.6 4.9 %all-to-all-done.3.in_ref = f32[8,96,128]{2,1,0:T(8,128)S(1)} async-done(((f32[8,96,128]{2,1,0:T(8,128)}), f32[8,96,128]{2,1,0:T(8,128)S(1)}, u32[]{:S(2)}, u32[]{:S(2)}) %all-to-all-start.3) | async-done | bytes 393248 | tf_op jit(solution)/shard_map/all_to_all | solution.py:905
  58.5 0.8 copy-done.4
  59.3 1.0 copy-done.5
  60.3 1.3 %shard_map.99 = (f32[8,3,32,128]{3,2,1,0:T(8,128)S(1)}, f32[8,24,128]{2,1,0:T(8,128)S(1)}, f32[8,24,128]{2,1,0:T(8,128)}, f32[8,24,128]{2,1,0:T(8,128)}, f32[8,24,128]{2,1,0:T(8,128)}) custom-call(f32[8,96,128]{2,1,0:T(8,128)S(1)} %copy-done.5, bf16[896,256]{1,0:T(8,128)(2,1)S(1)} %copy-done.2), custom_call_target="tpu_custom_call" | custom-call | tf_op jit(solution)/shard_map/pallas_call | solution.py:843
  61.6 0.6 copy-done.9
  62.2 6.6 %conditional.1 = (f32[8,24,128]{2,1,0:T(8,128)}, f32[8,24,128]{2,1,0:T(8,128)}, f32[8,24,128]{2,1,0:T(8,128)}) conditional(s32[]{:T(128)} %clamp.3, (f32[8,24,128]{2,1,0:T(8,128)}, f32[8,24,128]{2,1,0:T(8,128)}, f32[8,24,128]{2,1,0:T(8,128)}) %tuple.24, (f32[8,24,128]{2,1,0:T(8,128)S(1)}, f32[8,24,128]{2,1,0:T(8,128)}, ...), branch_computations={%region_0.1_spmd, %region_1.2_spmd, %region_2.3_spmd, %region_3.4_... | conditional | bytes 1179792 | solution.py:997
  62.2 1.3 %collective-permute-start.3 = (f32[8,24,128]{2,1,0:T(8,128)S(1)}, f32[8,24,128]{2,1,0:T(8,128)}, u32[]{:S(2)}, u32[]{:S(2)}) collective-permute-start(f32[8,24,128]{2,1,0:T(8,128)S(1)} %get-tuple-element.27), channel_id=1, source_target_pairs={{1,0},{5,4},{9,8},{13,12},{17,16},{21,20},{25,24},{29,28}} | collective-permute-start | bytes 294920 | tf_op jit(solution)/shard_map/cond/branch_1_fun/ppermute | solution.py:990
  63.5 1.3 %collective-permute-start.4 = (f32[8,24,128]{2,1,0:T(8,128)}, f32[8,24,128]{2,1,0:T(8,128)}, u32[]{:S(2)}, u32[]{:S(2)}) collective-permute-start(f32[8,24,128]{2,1,0:T(8,128)} %get-tuple-element.28), channel_id=1, source_target_pairs={{1,2},{5,6},{9,10},{13,14},{17,18},{21,22},{25,26},{29,30}} | collective-permute-start | bytes 294920 | tf_op jit(solution)/shard_map/cond/branch_1_fun/ppermute | solution.py:990
  64.8 1.3 %collective-permute-start.5 = (f32[8,24,128]{2,1,0:T(8,128)}, f32[8,24,128]{2,1,0:T(8,128)}, u32[]{:S(2)}, u32[]{:S(2)}) collective-permute-start(f32[8,24,128]{2,1,0:T(8,128)} %get-tuple-element.29), channel_id=1, source_target_pairs={{1,3},{5,7},{9,11},{13,15},{17,19},{21,23},{25,27},{29,31}} | collective-permute-start | bytes 294920 | tf_op jit(solution)/shard_map/cond/branch_1_fun/ppermute | solution.py:990
  66.1 2.7 %collective-permute-done.3 = f32[8,24,128]{2,1,0:T(8,128)} collective-permute-done((f32[8,24,128]{2,1,0:T(8,128)S(1)}, f32[8,24,128]{2,1,0:T(8,128)}, u32[]{:S(2)}, u32[]{:S(2)}) %collective-permute-start.3) | collective-permute-done | bytes 98336 | tf_op jit(solution)/shard_map/cond/branch_1_fun/ppermute | solution.py:990
  68.9 7.9 %collective-permute-start.17 = (f32[72,8,128]{2,1,0:T(8,128)}, f32[72,8,128]{2,1,0:T(8,128)S(1)}, u32[]{:S(2)}, u32[]{:S(2)}) collective-permute-start(f32[72,8,128]{2,1,0:T(8,128)} %get-tuple-element.73), channel_id=1, source_target_pairs={{0,3},{1,2},{2,1},{3,0},{4,7},{5,6},{6,5},{7,4},{8,11},{9,10},{10,... | collective-permute-start | bytes 884744 | tf_op jit(solution)/shard_map/ppermute | solution.py:948
  76.7 0.6 collective-permute-start.13
  77.3 3.3 %collective-permute-start.14 = (f32[8,24,128]{2,1,0:T(8,128)}, f32[8,24,128]{2,1,0:T(8,128)S(1)}, u32[]{:S(2)}, u32[]{:S(2)}) collective-permute-start(f32[8,24,128]{2,1,0:T(8,128)} %get-tuple-element.63), channel_id=1, source_target_pairs={{0,3},{1,0},{2,1},{3,2},{4,7},{5,4},{6,5},{7,6},{8,11},{9,8},{10,9... | collective-permute-start | bytes 294920 | tf_op jit(solution)/shard_map/ppermute | solution.py:879
  82.0 2.9 %collective-permute-done.17.rest_12_ = f32[72,8,128]{2,1,0:T(8,128)S(1)} collective-permute-done((f32[72,8,128]{2,1,0:T(8,128)}, f32[72,8,128]{2,1,0:T(8,128)S(1)}, u32[]{:S(2)}, u32[]{:S(2)}) %collective-permute-start.17) | collective-permute-done | bytes 294944 | tf_op jit(solution)/shard_map/ppermute | solution.py:948
  84.9 1.3 %collective-permute-done.12.rest_0_ = f32[8,24,128]{2,1,0:T(8,128)S(1)} collective-permute-done((f32[8,24,128]{2,1,0:T(8,128)}, f32[8,24,128]{2,1,0:T(8,128)S(1)}, u32[]{:S(2)}, u32[]{:S(2)}) %collective-permute-start.12) | collective-permute-done | bytes 98336 | tf_op jit(solution)/shard_map/ppermute | solution.py:879
  86.2 8.0 %collective-permute-done.13.rest_1_ = f32[8,24,128]{2,1,0:T(8,128)S(1)} collective-permute-done((f32[8,24,128]{2,1,0:T(8,128)}, f32[8,24,128]{2,1,0:T(8,128)S(1)}, u32[]{:S(2)}, u32[]{:S(2)}) %collective-permute-start.13) | collective-permute-done | bytes 98336 | tf_op jit(solution)/shard_map/ppermute | solution.py:879
  94.3 3.7 %shard_map.101 = f32[32,4,128]{2,1,0:T(4,128)} custom-call(s32[1]{0:T(128)S(6)} %select_n.17.sink_ref, s32[1]{0:T(128)S(6)} %select_n.18.src_time_ref, s32[1]{0:T(128)S(6)} %max.3.src_site_ref, f32[8,3,32,128]{3,2,1,0:T(8,128)} %get-tuple-element.57.first_any, f32[8,3,32,128]{3,2,1,0:T(8,128)S(1)} %get-tuple-element.59.second_ref, ...), custom_call_target="tpu_custom_call" | custom-call | tf_op jit(solution)/shard_map/pallas_call | solution.py:843
  98.0 4.2 %all-to-all-start.4 = ((f32[32,4,128]{2,1,0:T(4,128)}), f32[32,4,128]{2,1,0:T(4,128)S(1)}, u32[]{:S(2)}, u32[]{:S(2)}) async-start(f32[32,4,128]{2,1,0:T(4,128)} %shard_map.101), calls=%async_computation.4 | async-start | bytes 131072 | tf_op jit(solution)/shard_map/all_to_all | solution.py:1037
  102.2 5.2 %shard_map.100 = f32[54,64,128]{2,1,0:T(8,128)} custom-call(f32[54,64,128]{2,1,0:T(8,128)} %bitcast.20, f32[8,3,32,128]{3,2,1,0:T(8,128)} %get-tuple-element.57.first_any, bf16[896,256]{1,0:T(8,128)(2,1)} %constant.45.clone.inverse_ref.table_any, f32[8,3,32,128]{3,2,1,0:T(8,128)S(1)} %get-tuple-element.59.second_ref), custom_call_target="tpu_custom_call" | custom-call | tf_op jit(solution)/shard_map/pallas_call | solution.py:843
  107.4 2.3 %all-to-all-done.4.in_ref = f32[32,4,128]{2,1,0:T(4,128)S(1)} async-done(((f32[32,4,128]{2,1,0:T(4,128)}), f32[32,4,128]{2,1,0:T(4,128)S(1)}, u32[]{:S(2)}, u32[]{:S(2)}) %all-to-all-start.4) | async-done | bytes 65568 | tf_op jit(solution)/shard_map/all_to_all | solution.py:1037
  109.7 0.7 shard_map.102
  (23 shorter events, 0.1 us)
Async XLA Ops:
  0.6 17.4 %copy-start.6 = (f32[2,9,16,128]{3,2,1,0:T(8,128)S(1)}, f32[2,9,16,128]{3,2,1,0:T(8,128)}, u32[]{:S(2)}) copy-start(f32[2,9,16,128]{3,2,1,0:T(8,128)} %constant.46.clone.table_ref) | copy-start | bytes 442372
  0.6 28.4 %copy-start.3 = (bf16[896,256]{1,0:T(8,128)(2,1)S(1)}, bf16[896,256]{1,0:T(8,128)(2,1)}, u32[]{:S(2)}) copy-start(bf16[896,256]{1,0:T(8,128)(2,1)} %constant.44.clone.table_any.forward_ref) | copy-start | bytes 1376260
  4.4 24.6 %copy-start = (f32[1,3,2,3,3,2,4096]{6,5,4,3,2,1,0:T(2,128)S(1)}, f32[1,3,2,3,3,2,4096]{6,5,4,3,2,1,0:T(2,128)}, u32[]{:S(2)}) copy-start(f32[1,3,2,3,3,2,4096]{6,5,4,3,2,1,0:T(2,128)} %param.12) | copy-start | bytes 5308420
  4.4 24.6 %copy-start.2 = (bf16[896,256]{1,0:T(8,128)(2,1)S(1)}, bf16[896,256]{1,0:T(8,128)(2,1)}, u32[]{:S(2)}) copy-start(bf16[896,256]{1,0:T(8,128)(2,1)} %constant.45.clone.inverse_ref.table_any) | copy-start | bytes 1376260
  34.0 60.3 %copy-start.1 = (f32[2,36,2,4096]{3,2,1,0:T(2,128)S(1)}, f32[2,36,2,4096]{3,2,1,0:T(2,128)}, u32[]{:S(2)}) copy-start(f32[2,36,2,4096]{3,2,1,0:T(2,128)} %param.13) | copy-start | bytes 7077892
  34.0 11.8 %all-to-all-start.2 = ((f32[8,96,128]{2,1,0:T(8,128)}), f32[8,96,128]{2,1,0:T(8,128)S(1)}, u32[]{:S(2)}, u32[]{:S(2)}) async-start(f32[8,96,128]{2,1,0:T(8,128)} %get-tuple-element.58), calls=%async_computation.2 | async-start | bytes 786432 | tf_op jit(solution)/shard_map/all_to_all | solution.py:905
  37.6 56.7 %collective-permute-start.15 = (f32[72,24,128]{2,1,0:T(8,128)}, f32[72,24,128]{2,1,0:T(8,128)}, u32[]{:S(2)}, u32[]{:S(2)}) collective-permute-start(f32[72,24,128]{2,1,0:T(8,128)} %get-tuple-element.71), channel_id=1, source_target_pairs={{0,1},{1,0},{2,3},{3,2},{4,5},{5,4},{6,7},{7,6},{8,9},{9,8},{10,11... | collective-permute-start | bytes 2654216 | tf_op jit(solution)/shard_map/ppermute | solution.py:948
  46.8 11.7 %all-to-all-start.3 = ((f32[8,96,128]{2,1,0:T(8,128)}), f32[8,96,128]{2,1,0:T(8,128)S(1)}, u32[]{:S(2)}, u32[]{:S(2)}) async-start(f32[8,96,128]{2,1,0:T(8,128)} %shard_map.98), calls=%async_computation.3 | async-start | bytes 786432 | tf_op jit(solution)/shard_map/all_to_all | solution.py:905
  50.3 27.0 %collective-permute-start.16 = (f32[72,8,128]{2,1,0:T(8,128)}, f32[72,8,128]{2,1,0:T(8,128)S(1)}, u32[]{:S(2)}, u32[]{:S(2)}) collective-permute-start(f32[72,8,128]{2,1,0:T(8,128)} %get-tuple-element.72), channel_id=1, source_target_pairs={{0,2},{1,3},{2,0},{3,1},{4,6},{5,7},{6,4},{7,5},{8,10},{9,11},{10,... | collective-permute-start | bytes 884744 | tf_op jit(solution)/shard_map/ppermute | solution.py:948
  58.5 0.8 copy-start.4
  59.3 1.0 copy-start.5
  61.6 0.6 copy-start.9
  62.2 6.6 %collective-permute-start.3 = (f32[8,24,128]{2,1,0:T(8,128)S(1)}, f32[8,24,128]{2,1,0:T(8,128)}, u32[]{:S(2)}, u32[]{:S(2)}) collective-permute-start(f32[8,24,128]{2,1,0:T(8,128)S(1)} %get-tuple-element.27), channel_id=1, source_target_pairs={{1,0},{5,4},{9,8},{13,12},{17,16},{21,20},{25,24},{29,28}} | collective-permute-start | bytes 294920 | tf_op jit(solution)/shard_map/cond/branch_1_fun/ppermute | solution.py:990
  63.5 5.3 %collective-permute-start.4 = (f32[8,24,128]{2,1,0:T(8,128)}, f32[8,24,128]{2,1,0:T(8,128)}, u32[]{:S(2)}, u32[]{:S(2)}) collective-permute-start(f32[8,24,128]{2,1,0:T(8,128)} %get-tuple-element.28), channel_id=1, source_target_pairs={{1,2},{5,6},{9,10},{13,14},{17,18},{21,22},{25,26},{29,30}} | collective-permute-start | bytes 294920 | tf_op jit(solution)/shard_map/cond/branch_1_fun/ppermute | solution.py:990
  64.8 4.0 %collective-permute-start.5 = (f32[8,24,128]{2,1,0:T(8,128)}, f32[8,24,128]{2,1,0:T(8,128)}, u32[]{:S(2)}, u32[]{:S(2)}) collective-permute-start(f32[8,24,128]{2,1,0:T(8,128)} %get-tuple-element.29), channel_id=1, source_target_pairs={{1,3},{5,7},{9,11},{13,15},{17,19},{21,23},{25,27},{29,31}} | collective-permute-start | bytes 294920 | tf_op jit(solution)/shard_map/cond/branch_1_fun/ppermute | solution.py:990
  68.9 16.0 %collective-permute-start.17 = (f32[72,8,128]{2,1,0:T(8,128)}, f32[72,8,128]{2,1,0:T(8,128)S(1)}, u32[]{:S(2)}, u32[]{:S(2)}) collective-permute-start(f32[72,8,128]{2,1,0:T(8,128)} %get-tuple-element.73), channel_id=1, source_target_pairs={{0,3},{1,2},{2,1},{3,0},{4,7},{5,6},{6,5},{7,4},{8,11},{9,10},{10,... | collective-permute-start | bytes 884744 | tf_op jit(solution)/shard_map/ppermute | solution.py:948
  76.7 9.5 %collective-permute-start.12 = (f32[8,24,128]{2,1,0:T(8,128)}, f32[8,24,128]{2,1,0:T(8,128)S(1)}, u32[]{:S(2)}, u32[]{:S(2)}) collective-permute-start(f32[8,24,128]{2,1,0:T(8,128)} %get-tuple-element.61), channel_id=1, source_target_pairs={{0,1},{1,2},{2,3},{3,0},{4,5},{5,6},{6,7},{7,4},{8,9},{9,10},{10,1... | collective-permute-start | bytes 294920 | tf_op jit(solution)/shard_map/ppermute | solution.py:879
  76.7 17.5 %collective-permute-start.13 = (f32[8,24,128]{2,1,0:T(8,128)}, f32[8,24,128]{2,1,0:T(8,128)S(1)}, u32[]{:S(2)}, u32[]{:S(2)}) collective-permute-start(f32[8,24,128]{2,1,0:T(8,128)} %get-tuple-element.62), channel_id=1, source_target_pairs={{0,2},{1,3},{2,0},{3,1},{4,6},{5,7},{6,4},{7,5},{8,10},{9,11},{10,... | collective-permute-start | bytes 294920 | tf_op jit(solution)/shard_map/ppermute | solution.py:879
  77.3 16.9 %copy-start.7 = (f32[72,8,128]{2,1,0:T(8,128)}, f32[72,8,128]{2,1,0:T(8,128)S(1)}, u32[]{:S(2)}) copy-start(f32[72,8,128]{2,1,0:T(8,128)S(1)} %collective-permute-done.16.rest_11_) | copy-start | bytes 884740
  77.3 16.9 %collective-permute-start.14 = (f32[8,24,128]{2,1,0:T(8,128)}, f32[8,24,128]{2,1,0:T(8,128)S(1)}, u32[]{:S(2)}, u32[]{:S(2)}) collective-permute-start(f32[8,24,128]{2,1,0:T(8,128)} %get-tuple-element.63), channel_id=1, source_target_pairs={{0,3},{1,0},{2,1},{3,2},{4,7},{5,4},{6,5},{7,6},{8,11},{9,8},{10,9... | collective-permute-start | bytes 294920 | tf_op jit(solution)/shard_map/ppermute | solution.py:879
  84.9 9.4 %copy-start.8 = (f32[72,8,128]{2,1,0:T(8,128)}, f32[72,8,128]{2,1,0:T(8,128)S(1)}, u32[]{:S(2)}) copy-start(f32[72,8,128]{2,1,0:T(8,128)S(1)} %collective-permute-done.17.rest_12_) | copy-start | bytes 884740
  98.0 11.7 %all-to-all-start.4 = ((f32[32,4,128]{2,1,0:T(4,128)}), f32[32,4,128]{2,1,0:T(4,128)S(1)}, u32[]{:S(2)}, u32[]{:S(2)}) async-start(f32[32,4,128]{2,1,0:T(4,128)} %shard_map.101), calls=%async_computation.4 | async-start | bytes 131072 | tf_op jit(solution)/shard_map/all_to_all | solution.py:1037

commit v4 on v3

--- a/solution.py
+++ b/solution.py
@@ -349,19 +349,24 @@
     return [[(at(3 * i + j), at(9 + 3 * i + j)) for j in range(3)] for i in range(3)]
 
 
-def divergence(v_ref, shift_ref, stack_ref, moved_ref, d_ref):
+def divergence(v_ref, shift_ref, stack_ref, moved_ref, rest_ref, d_ref):
     _, comps, planes, half, lanes = v_ref.shape
     size = comps * planes * half
     for direction in (1, 2):
         for comp in range(comps):
             for plane in range(planes):
                 at = (direction - 1) * size + (comp * planes + plane) * half
-                stack_ref[at : at + half, :] = jnp.concatenate(
-                    halves(v_ref[direction, comp, plane]), axis=1
-                )
+                value = v_ref[direction, comp, plane]
+                high, low = halves(value)
+                stack_ref[at : at + half, :] = jnp.concatenate([high, low], axis=1)
+                rest = (value - high.astype(F32)) - low.astype(F32)
+                rest_ref[at : at + half, :] = rest.astype(BF16)
     first = shift_ref.shape[0] - 2 * lanes
-    moved_ref[:size, :lanes] = dot(stack_ref[:size], shift_ref[first:, :lanes])
-    moved_ref[size : 2 * size, :lanes] = dot(stack_ref[size : 2 * size], shift_ref[first:, lanes:])
+    for k in range(2):
+        part, columns = slice(k * size, (k + 1) * size), slice(k * lanes, (k + 1) * lanes)
+        moved_ref[part, :lanes] = dot(stack_ref[part], shift_ref[first:, columns]) + dot(
+            rest_ref[part], shift_ref[first + lanes :, columns]
+        )
     for comp in range(comps):
         before = None
         for plane in range(planes):
@@ -422,7 +427,7 @@
 def start_kernel(split, links_any, table_any, source_any, out_any, *rest):
     peers = split.peers
     cut_refs, held_refs = rest[: len(peers)], rest[len(peers) : 2 * len(peers)]
-    links_ref, table_ref, v_ref, d_ref, stack_ref, moved_ref, high_ref, low_ref, spec_ref, out_ref, sems, cut_sems, out_sems = rest[
+    links_ref, table_ref, v_ref, d_ref, rest_ref, stack_ref, moved_ref, high_ref, low_ref, spec_ref, out_ref, sems, cut_sems, out_sems = rest[
         2 * len(peers) :
     ]
     _, _, planes, half, _ = v_ref.shape
@@ -461,7 +466,7 @@
     for copy in writes:
         copy.start()
     copies[3].wait()
-    divergence(v_ref, table_ref, stack_ref, moved_ref, d_ref)
+    divergence(v_ref, table_ref, stack_ref, moved_ref, rest_ref, d_ref)
     outs = forward_transform(d_ref, table_ref, high_ref, low_ref, spec_ref, out_ref, out_any, out_sems)
     for copy in writes + outs:
         copy.wait()
@@ -534,7 +539,7 @@
 def middle_kernel(split, in_ref, links_ref, inverse_ref, forward_ref, *rest):
     out_any, x_any = rest[:2]
     share_refs = rest[2 : 2 + split.times]
-    x_ref, g_ref, y_ref, v_ref, d_ref, stack_ref, moved_ref, high_ref, low_ref, spec_ref, flat_ref, out_ref, sems, share_sems, out_sems = rest[2 + split.times :]
+    x_ref, g_ref, y_ref, v_ref, d_ref, rest_ref, stack_ref, moved_ref, high_ref, low_ref, spec_ref, flat_ref, out_ref, sems, share_sems, out_sems = rest[2 + split.times :]
     _, slots, half, _ = x_ref.shape
     planes = slots - 1
     inverse_transform(in_ref, inverse_ref, high_ref, low_ref, spec_ref, x_ref)
@@ -566,7 +571,7 @@
                 v_ref[direction, comp, plane, rows, :] = value
 
     chunk_loop(planes, half // 8, rotate_step)
-    divergence(v_ref, forward_ref, stack_ref, moved_ref, d_ref)
+    divergence(v_ref, forward_ref, stack_ref, moved_ref, rest_ref, d_ref)
     copies += forward_transform(
         d_ref, forward_ref, high_ref, low_ref, spec_ref, out_ref, out_any, out_sems
     )
@@ -887,6 +892,7 @@
     divergence_scratch = [
         VMEM((3, 8, planes, half, lanes), F32),
         VMEM((slots, 8, half, lanes), F32),
+        VMEM((16 * planes * half, lanes), BF16),
     ]
     gauge_scratch = [
         VMEM((18, slots, half, lanes), F32),

time: 111 us -> 111 us (level)
  no operation moved by 1% of the time
where the time goes in v4:
time: 111 us
  starting transfers between devices  31.1 us (28%)
  waiting for transfers between devices  28.9 us (26%)
  blocking collectives  24.3 us (22%)
  Pallas kernels  21 us (19%)
  between operations  2.76 us (2%)
  local copies, waits for them, and re-layouts  2.42 us (2%)
    all_to_all x2, blocking collectives, turn(): return lax.all_to_all(spectrum, 'space', 0, 0, tiled=True)  24.3 us
    pallas_call x8, Pallas kernels, call(): pl.pallas_call(kernel, out_shape=outs, in_specs=in_specs, out_specs=out_s...  21 us
    ppermute x3, starting transfers between devices, body(): lax.ppermute(cut, 'tm', [(i, split.moved(i, step)) for i in range(times)])  12.2 us
    all_to_all x2, waiting for transfers between devices, turn(): return lax.all_to_all(spectrum, 'space', 0, 0, tiled=True)  11.5 us
    ppermute x3, waiting for transfers between devices, forwarded(): lax.ppermute(value, 'tm', [(i, (i + shift) % times) for i in range(times)])  9.39 us
    all_to_all x2, starting transfers between devices, turn(): return lax.all_to_all(spectrum, 'space', 0, 0, tiled=True)  7.05 us
    all_to_all x1, starting transfers between devices, body(): gathered = lax.all_to_all(payload, ('space', 'tm'), 0, 0, tiled=True)  4.16 us
    ppermute x3, starting transfers between devices, forwarded(): lax.ppermute(value, 'tm', [(i, (i + shift) % times) for i in range(times)])  3.88 us
  transfers between devices with their start and end apart: 12, of which 7 were waited for; matrix products, arithmetic and copies ran while one was open for 0% of the time, Pallas kernels for 7%

profile of v4, /device:TPU:0, one launch (start us, length us, event | category | flops | bytes accessed | tf_op | source)
XLA Modules:
  0.0 110.6 jit_solution(14458202835284477197)
XLA Ops:
  0.7 3.8 %shard_map.95 = (f32[8,96,128]{2,1,0:T(8,128)}, f32[72,24,128]{2,1,0:T(8,128)}, f32[72,8,128]{2,1,0:T(8,128)}, f32[72,8,128]{2,1,0:T(8,128)}) custom-call(f32[54,64,128]{2,1,0:T(8,128)} %bitcast.19, bf16[896,256]{1,0:T(8,128)(2,1)} %constant.44.clone.table_any.forward_ref, f32[72,64,128]{2,1,0:T(8,128)} %bitcast.22), custom_call_target="tpu_custom_call" | custom-call | tf_op jit(solution)/shard_map/pallas_call | solution.py:848
  4.5 13.6 %all_to_all.25.in_ref = f32[8,96,128]{2,1,0:T(8,128)S(1)} all-to-all(f32[8,96,128]{2,1,0:T(8,128)} %get-tuple-element.56), channel_id=1, replica_groups=mesh['space'=8,'tm'=4] {'space'}, dimensions={0} | all-to-all | bytes 786432 | tf_op jit(solution)/shard_map/all_to_all | solution.py:911
  18.1 0.2 shard_map.96
  18.4 10.7 %all_to_all.26.in_ref = f32[8,96,128]{2,1,0:T(8,128)S(1)} all-to-all(f32[8,96,128]{2,1,0:T(8,128)S(1)} %shard_map.96), channel_id=1, replica_groups=mesh['space'=8,'tm'=4] {'space'}, dimensions={0} | all-to-all | bytes 786432 | tf_op jit(solution)/shard_map/all_to_all | solution.py:911
  29.1 5.0 %shard_map.97 = (f32[8,96,128]{2,1,0:T(8,128)}, f32[8,3,32,128]{3,2,1,0:T(8,128)}, f32[8,24,128]{2,1,0:T(8,128)}, f32[8,24,128]{2,1,0:T(8,128)}, f32[8,24,128]{2,1,0:T(8,128)}, /*index=5*/f32[8,24,128]{2,1,0:T(8,128)}) custom-call(f32[8,96,128]{2,1,0:T(8,128)S(1)} %all_to_all.26.in_ref, f32[54,64,128]{2,1,0:T(8,128)S(1)} %bitcast.21, ...), custom_call_target="tpu_custom_call" | custom-call | tf_op jit(solution)/shard_map/pallas_call | solution.py:848
  34.1 3.6 %all-to-all-start.2 = ((f32[8,96,128]{2,1,0:T(8,128)}), f32[8,96,128]{2,1,0:T(8,128)S(1)}, u32[]{:S(2)}, u32[]{:S(2)}) async-start(f32[8,96,128]{2,1,0:T(8,128)} %get-tuple-element.58), calls=%async_computation.2 | async-start | bytes 786432 | tf_op jit(solution)/shard_map/all_to_all | solution.py:911
  37.7 1.6 %collective-permute-start.15 = (f32[72,24,128]{2,1,0:T(8,128)}, f32[72,24,128]{2,1,0:T(8,128)}, u32[]{:S(2)}, u32[]{:S(2)}) collective-permute-start(f32[72,24,128]{2,1,0:T(8,128)} %get-tuple-element.71), channel_id=1, source_target_pairs={{0,1},{1,0},{2,3},{3,2},{4,5},{5,4},{6,7},{7,6},{8,9},{9,8},{10,11... | collective-permute-start | bytes 2654216 | tf_op jit(solution)/shard_map/ppermute | solution.py:954
  39.4 6.6 %all-to-all-done.2.in_ref = f32[8,96,128]{2,1,0:T(8,128)S(1)} async-done(((f32[8,96,128]{2,1,0:T(8,128)}), f32[8,96,128]{2,1,0:T(8,128)S(1)}, u32[]{:S(2)}, u32[]{:S(2)}) %all-to-all-start.2) | async-done | bytes 393248 | tf_op jit(solution)/shard_map/all_to_all | solution.py:911
  46.0 1.0 shard_map.98
  47.0 3.5 %all-to-all-start.3 = ((f32[8,96,128]{2,1,0:T(8,128)}), f32[8,96,128]{2,1,0:T(8,128)S(1)}, u32[]{:S(2)}, u32[]{:S(2)}) async-start(f32[8,96,128]{2,1,0:T(8,128)} %shard_map.98), calls=%async_computation.3 | async-start | bytes 786432 | tf_op jit(solution)/shard_map/all_to_all | solution.py:911
  50.4 2.7 %collective-permute-start.16 = (f32[72,8,128]{2,1,0:T(8,128)}, f32[72,8,128]{2,1,0:T(8,128)S(1)}, u32[]{:S(2)}, u32[]{:S(2)}) collective-permute-start(f32[72,8,128]{2,1,0:T(8,128)} %get-tuple-element.72), channel_id=1, source_target_pairs={{0,2},{1,3},{2,0},{3,1},{4,6},{5,7},{6,4},{7,5},{8,10},{9,11},{10,... | collective-permute-start | bytes 884744 | tf_op jit(solution)/shard_map/ppermute | solution.py:954
  53.7 4.9 %all-to-all-done.3.in_ref = f32[8,96,128]{2,1,0:T(8,128)S(1)} async-done(((f32[8,96,128]{2,1,0:T(8,128)}), f32[8,96,128]{2,1,0:T(8,128)S(1)}, u32[]{:S(2)}, u32[]{:S(2)}) %all-to-all-start.3) | async-done | bytes 393248 | tf_op jit(solution)/shard_map/all_to_all | solution.py:911
  58.7 0.8 copy-done.4
  59.4 1.0 copy-done.5
  60.4 1.3 %shard_map.99 = (f32[8,3,32,128]{3,2,1,0:T(8,128)S(1)}, f32[8,24,128]{2,1,0:T(8,128)S(1)}, f32[8,24,128]{2,1,0:T(8,128)}, f32[8,24,128]{2,1,0:T(8,128)}, f32[8,24,128]{2,1,0:T(8,128)}) custom-call(f32[8,96,128]{2,1,0:T(8,128)S(1)} %copy-done.5, bf16[896,256]{1,0:T(8,128)(2,1)S(1)} %copy-done.2), custom_call_target="tpu_custom_call" | custom-call | tf_op jit(solution)/shard_map/pallas_call | solution.py:848
  61.8 0.6 copy-done.9
  62.4 6.6 %conditional.1 = (f32[8,24,128]{2,1,0:T(8,128)}, f32[8,24,128]{2,1,0:T(8,128)}, f32[8,24,128]{2,1,0:T(8,128)}) conditional(s32[]{:T(128)} %clamp.3, (f32[8,24,128]{2,1,0:T(8,128)}, f32[8,24,128]{2,1,0:T(8,128)}, f32[8,24,128]{2,1,0:T(8,128)}) %tuple.24, (f32[8,24,128]{2,1,0:T(8,128)S(1)}, f32[8,24,128]{2,1,0:T(8,128)}, ...), branch_computations={%region_0.1_spmd, %region_1.2_spmd, %region_2.3_spmd, %region_3.4_... | conditional | bytes 1179792 | solution.py:1003
  62.4 1.3 %collective-permute-start.3 = (f32[8,24,128]{2,1,0:T(8,128)S(1)}, f32[8,24,128]{2,1,0:T(8,128)}, u32[]{:S(2)}, u32[]{:S(2)}) collective-permute-start(f32[8,24,128]{2,1,0:T(8,128)S(1)} %get-tuple-element.27), channel_id=1, source_target_pairs={{1,0},{5,4},{9,8},{13,12},{17,16},{21,20},{25,24},{29,28}} | collective-permute-start | bytes 294920 | tf_op jit(solution)/shard_map/cond/branch_1_fun/ppermute | solution.py:996
  63.7 1.3 %collective-permute-start.4 = (f32[8,24,128]{2,1,0:T(8,128)}, f32[8,24,128]{2,1,0:T(8,128)}, u32[]{:S(2)}, u32[]{:S(2)}) collective-permute-start(f32[8,24,128]{2,1,0:T(8,128)} %get-tuple-element.28), channel_id=1, source_target_pairs={{1,2},{5,6},{9,10},{13,14},{17,18},{21,22},{25,26},{29,30}} | collective-permute-start | bytes 294920 | tf_op jit(solution)/shard_map/cond/branch_1_fun/ppermute | solution.py:996
  65.0 1.3 %collective-permute-start.5 = (f32[8,24,128]{2,1,0:T(8,128)}, f32[8,24,128]{2,1,0:T(8,128)}, u32[]{:S(2)}, u32[]{:S(2)}) collective-permute-start(f32[8,24,128]{2,1,0:T(8,128)} %get-tuple-element.29), channel_id=1, source_target_pairs={{1,3},{5,7},{9,11},{13,15},{17,19},{21,23},{25,27},{29,31}} | collective-permute-start | bytes 294920 | tf_op jit(solution)/shard_map/cond/branch_1_fun/ppermute | solution.py:996
  66.3 2.7 %collective-permute-done.3 = f32[8,24,128]{2,1,0:T(8,128)} collective-permute-done((f32[8,24,128]{2,1,0:T(8,128)S(1)}, f32[8,24,128]{2,1,0:T(8,128)}, u32[]{:S(2)}, u32[]{:S(2)}) %collective-permute-start.3) | collective-permute-done | bytes 98336 | tf_op jit(solution)/shard_map/cond/branch_1_fun/ppermute | solution.py:996
  69.0 7.9 %collective-permute-start.17 = (f32[72,8,128]{2,1,0:T(8,128)}, f32[72,8,128]{2,1,0:T(8,128)S(1)}, u32[]{:S(2)}, u32[]{:S(2)}) collective-permute-start(f32[72,8,128]{2,1,0:T(8,128)} %get-tuple-element.73), channel_id=1, source_target_pairs={{0,3},{1,2},{2,1},{3,0},{4,7},{5,6},{6,5},{7,4},{8,11},{9,10},{10,... | collective-permute-start | bytes 884744 | tf_op jit(solution)/shard_map/ppermute | solution.py:954
  76.9 0.6 collective-permute-start.13
  77.5 3.3 %collective-permute-start.14 = (f32[8,24,128]{2,1,0:T(8,128)}, f32[8,24,128]{2,1,0:T(8,128)S(1)}, u32[]{:S(2)}, u32[]{:S(2)}) collective-permute-start(f32[8,24,128]{2,1,0:T(8,128)} %get-tuple-element.63), channel_id=1, source_target_pairs={{0,3},{1,0},{2,1},{3,2},{4,7},{5,4},{6,5},{7,6},{8,11},{9,8},{10,9... | collective-permute-start | bytes 294920 | tf_op jit(solution)/shard_map/ppermute | solution.py:884
  82.1 2.9 %collective-permute-done.17.rest_12_ = f32[72,8,128]{2,1,0:T(8,128)S(1)} collective-permute-done((f32[72,8,128]{2,1,0:T(8,128)}, f32[72,8,128]{2,1,0:T(8,128)S(1)}, u32[]{:S(2)}, u32[]{:S(2)}) %collective-permute-start.17) | collective-permute-done | bytes 294944 | tf_op jit(solution)/shard_map/ppermute | solution.py:954
  85.0 1.3 %collective-permute-done.12.rest_0_ = f32[8,24,128]{2,1,0:T(8,128)S(1)} collective-permute-done((f32[8,24,128]{2,1,0:T(8,128)}, f32[8,24,128]{2,1,0:T(8,128)S(1)}, u32[]{:S(2)}, u32[]{:S(2)}) %collective-permute-start.12) | collective-permute-done | bytes 98336 | tf_op jit(solution)/shard_map/ppermute | solution.py:884
  86.3 8.0 %collective-permute-done.13.rest_1_ = f32[8,24,128]{2,1,0:T(8,128)S(1)} collective-permute-done((f32[8,24,128]{2,1,0:T(8,128)}, f32[8,24,128]{2,1,0:T(8,128)S(1)}, u32[]{:S(2)}, u32[]{:S(2)}) %collective-permute-start.13) | collective-permute-done | bytes 98336 | tf_op jit(solution)/shard_map/ppermute | solution.py:884
  94.4 3.7 %shard_map.101 = f32[32,4,128]{2,1,0:T(4,128)} custom-call(s32[1]{0:T(128)S(6)} %select_n.17.sink_ref, s32[1]{0:T(128)S(6)} %select_n.18.src_time_ref, s32[1]{0:T(128)S(6)} %max.3.src_site_ref, f32[8,3,32,128]{3,2,1,0:T(8,128)} %get-tuple-element.57.first_any, f32[8,3,32,128]{3,2,1,0:T(8,128)S(1)} %get-tuple-element.59.second_ref, ...), custom_call_target="tpu_custom_call" | custom-call | tf_op jit(solution)/shard_map/pallas_call | solution.py:848
  98.2 4.2 %all-to-all-start.4 = ((f32[32,4,128]{2,1,0:T(4,128)}), f32[32,4,128]{2,1,0:T(4,128)S(1)}, u32[]{:S(2)}, u32[]{:S(2)}) async-start(f32[32,4,128]{2,1,0:T(4,128)} %shard_map.101), calls=%async_computation.4 | async-start | bytes 131072 | tf_op jit(solution)/shard_map/all_to_all | solution.py:1043
  102.3 5.2 %shard_map.100 = f32[54,64,128]{2,1,0:T(8,128)} custom-call(f32[54,64,128]{2,1,0:T(8,128)} %bitcast.20, f32[8,3,32,128]{3,2,1,0:T(8,128)} %get-tuple-element.57.first_any, bf16[896,256]{1,0:T(8,128)(2,1)} %constant.45.clone.inverse_ref.table_any, f32[8,3,32,128]{3,2,1,0:T(8,128)S(1)} %get-tuple-element.59.second_ref), custom_call_target="tpu_custom_call" | custom-call | tf_op jit(solution)/shard_map/pallas_call | solution.py:848
  107.5 2.3 %all-to-all-done.4.in_ref = f32[32,4,128]{2,1,0:T(4,128)S(1)} async-done(((f32[32,4,128]{2,1,0:T(4,128)}), f32[32,4,128]{2,1,0:T(4,128)S(1)}, u32[]{:S(2)}, u32[]{:S(2)}) %all-to-all-start.4) | async-done | bytes 65568 | tf_op jit(solution)/shard_map/all_to_all | solution.py:1043
  109.8 0.7 shard_map.102
  (23 shorter events, 0.1 us)
Async XLA Ops:
  0.6 17.5 %copy-start.6 = (f32[2,9,16,128]{3,2,1,0:T(8,128)S(1)}, f32[2,9,16,128]{3,2,1,0:T(8,128)}, u32[]{:S(2)}) copy-start(f32[2,9,16,128]{3,2,1,0:T(8,128)} %constant.46.clone.table_ref) | copy-start | bytes 442372
  0.6 28.4 %copy-start.3 = (bf16[896,256]{1,0:T(8,128)(2,1)S(1)}, bf16[896,256]{1,0:T(8,128)(2,1)}, u32[]{:S(2)}) copy-start(bf16[896,256]{1,0:T(8,128)(2,1)} %constant.44.clone.table_any.forward_ref) | copy-start | bytes 1376260
  4.4 24.6 %copy-start = (f32[1,3,2,3,3,2,4096]{6,5,4,3,2,1,0:T(2,128)S(1)}, f32[1,3,2,3,3,2,4096]{6,5,4,3,2,1,0:T(2,128)}, u32[]{:S(2)}) copy-start(f32[1,3,2,3,3,2,4096]{6,5,4,3,2,1,0:T(2,128)} %param.12) | copy-start | bytes 5308420
  4.4 24.6 %copy-start.2 = (bf16[896,256]{1,0:T(8,128)(2,1)S(1)}, bf16[896,256]{1,0:T(8,128)(2,1)}, u32[]{:S(2)}) copy-start(bf16[896,256]{1,0:T(8,128)(2,1)} %constant.45.clone.inverse_ref.table_any) | copy-start | bytes 1376260
  34.1 60.3 %copy-start.1 = (f32[2,36,2,4096]{3,2,1,0:T(2,128)S(1)}, f32[2,36,2,4096]{3,2,1,0:T(2,128)}, u32[]{:S(2)}) copy-start(f32[2,36,2,4096]{3,2,1,0:T(2,128)} %param.13) | copy-start | bytes 7077892
  34.1 11.8 %all-to-all-start.2 = ((f32[8,96,128]{2,1,0:T(8,128)}), f32[8,96,128]{2,1,0:T(8,128)S(1)}, u32[]{:S(2)}, u32[]{:S(2)}) async-start(f32[8,96,128]{2,1,0:T(8,128)} %get-tuple-element.58), calls=%async_computation.2 | async-start | bytes 786432 | tf_op jit(solution)/shard_map/all_to_all | solution.py:911
  37.7 56.7 %collective-permute-start.15 = (f32[72,24,128]{2,1,0:T(8,128)}, f32[72,24,128]{2,1,0:T(8,128)}, u32[]{:S(2)}, u32[]{:S(2)}) collective-permute-start(f32[72,24,128]{2,1,0:T(8,128)} %get-tuple-element.71), channel_id=1, source_target_pairs={{0,1},{1,0},{2,3},{3,2},{4,5},{5,4},{6,7},{7,6},{8,9},{9,8},{10,11... | collective-permute-start | bytes 2654216 | tf_op jit(solution)/shard_map/ppermute | solution.py:954
  47.0 11.7 %all-to-all-start.3 = ((f32[8,96,128]{2,1,0:T(8,128)}), f32[8,96,128]{2,1,0:T(8,128)S(1)}, u32[]{:S(2)}, u32[]{:S(2)}) async-start(f32[8,96,128]{2,1,0:T(8,128)} %shard_map.98), calls=%async_computation.3 | async-start | bytes 786432 | tf_op jit(solution)/shard_map/all_to_all | solution.py:911
  50.4 27.0 %collective-permute-start.16 = (f32[72,8,128]{2,1,0:T(8,128)}, f32[72,8,128]{2,1,0:T(8,128)S(1)}, u32[]{:S(2)}, u32[]{:S(2)}) collective-permute-start(f32[72,8,128]{2,1,0:T(8,128)} %get-tuple-element.72), channel_id=1, source_target_pairs={{0,2},{1,3},{2,0},{3,1},{4,6},{5,7},{6,4},{7,5},{8,10},{9,11},{10,... | collective-permute-start | bytes 884744 | tf_op jit(solution)/shard_map/ppermute | solution.py:954
  58.7 0.8 copy-start.4
  59.4 1.0 copy-start.5
  61.8 0.6 copy-start.9
  62.4 6.6 %collective-permute-start.3 = (f32[8,24,128]{2,1,0:T(8,128)S(1)}, f32[8,24,128]{2,1,0:T(8,128)}, u32[]{:S(2)}, u32[]{:S(2)}) collective-permute-start(f32[8,24,128]{2,1,0:T(8,128)S(1)} %get-tuple-element.27), channel_id=1, source_target_pairs={{1,0},{5,4},{9,8},{13,12},{17,16},{21,20},{25,24},{29,28}} | collective-permute-start | bytes 294920 | tf_op jit(solution)/shard_map/cond/branch_1_fun/ppermute | solution.py:996
  63.7 5.3 %collective-permute-start.4 = (f32[8,24,128]{2,1,0:T(8,128)}, f32[8,24,128]{2,1,0:T(8,128)}, u32[]{:S(2)}, u32[]{:S(2)}) collective-permute-start(f32[8,24,128]{2,1,0:T(8,128)} %get-tuple-element.28), channel_id=1, source_target_pairs={{1,2},{5,6},{9,10},{13,14},{17,18},{21,22},{25,26},{29,30}} | collective-permute-start | bytes 294920 | tf_op jit(solution)/shard_map/cond/branch_1_fun/ppermute | solution.py:996
  65.0 4.0 %collective-permute-start.5 = (f32[8,24,128]{2,1,0:T(8,128)}, f32[8,24,128]{2,1,0:T(8,128)}, u32[]{:S(2)}, u32[]{:S(2)}) collective-permute-start(f32[8,24,128]{2,1,0:T(8,128)} %get-tuple-element.29), channel_id=1, source_target_pairs={{1,3},{5,7},{9,11},{13,15},{17,19},{21,23},{25,27},{29,31}} | collective-permute-start | bytes 294920 | tf_op jit(solution)/shard_map/cond/branch_1_fun/ppermute | solution.py:996
  69.0 16.0 %collective-permute-start.17 = (f32[72,8,128]{2,1,0:T(8,128)}, f32[72,8,128]{2,1,0:T(8,128)S(1)}, u32[]{:S(2)}, u32[]{:S(2)}) collective-permute-start(f32[72,8,128]{2,1,0:T(8,128)} %get-tuple-element.73), channel_id=1, source_target_pairs={{0,3},{1,2},{2,1},{3,0},{4,7},{5,6},{6,5},{7,4},{8,11},{9,10},{10,... | collective-permute-start | bytes 884744 | tf_op jit(solution)/shard_map/ppermute | solution.py:954
  76.9 9.5 %collective-permute-start.12 = (f32[8,24,128]{2,1,0:T(8,128)}, f32[8,24,128]{2,1,0:T(8,128)S(1)}, u32[]{:S(2)}, u32[]{:S(2)}) collective-permute-start(f32[8,24,128]{2,1,0:T(8,128)} %get-tuple-element.61), channel_id=1, source_target_pairs={{0,1},{1,2},{2,3},{3,0},{4,5},{5,6},{6,7},{7,4},{8,9},{9,10},{10,1... | collective-permute-start | bytes 294920 | tf_op jit(solution)/shard_map/ppermute | solution.py:884
  76.9 17.5 %collective-permute-start.13 = (f32[8,24,128]{2,1,0:T(8,128)}, f32[8,24,128]{2,1,0:T(8,128)S(1)}, u32[]{:S(2)}, u32[]{:S(2)}) collective-permute-start(f32[8,24,128]{2,1,0:T(8,128)} %get-tuple-element.62), channel_id=1, source_target_pairs={{0,2},{1,3},{2,0},{3,1},{4,6},{5,7},{6,4},{7,5},{8,10},{9,11},{10,... | collective-permute-start | bytes 294920 | tf_op jit(solution)/shard_map/ppermute | solution.py:884
  77.5 16.9 %copy-start.7 = (f32[72,8,128]{2,1,0:T(8,128)}, f32[72,8,128]{2,1,0:T(8,128)S(1)}, u32[]{:S(2)}) copy-start(f32[72,8,128]{2,1,0:T(8,128)S(1)} %collective-permute-done.16.rest_11_) | copy-start | bytes 884740
  77.5 16.9 %collective-permute-start.14 = (f32[8,24,128]{2,1,0:T(8,128)}, f32[8,24,128]{2,1,0:T(8,128)S(1)}, u32[]{:S(2)}, u32[]{:S(2)}) collective-permute-start(f32[8,24,128]{2,1,0:T(8,128)} %get-tuple-element.63), channel_id=1, source_target_pairs={{0,3},{1,0},{2,1},{3,2},{4,7},{5,4},{6,5},{7,6},{8,11},{9,8},{10,9... | collective-permute-start | bytes 294920 | tf_op jit(solution)/shard_map/ppermute | solution.py:884
  85.0 9.4 %copy-start.8 = (f32[72,8,128]{2,1,0:T(8,128)}, f32[72,8,128]{2,1,0:T(8,128)S(1)}, u32[]{:S(2)}) copy-start(f32[72,8,128]{2,1,0:T(8,128)S(1)} %collective-permute-done.17.rest_12_) | copy-start | bytes 884740
  98.2 11.7 %all-to-all-start.4 = ((f32[32,4,128]{2,1,0:T(4,128)}), f32[32,4,128]{2,1,0:T(4,128)S(1)}, u32[]{:S(2)}, u32[]{:S(2)}) async-start(f32[32,4,128]{2,1,0:T(4,128)} %shard_map.101), calls=%async_computation.4 | async-start | bytes 131072 | tf_op jit(solution)/shard_map/all_to_all | solution.py:1043

commit v5 on v4

--- a/solution.py
+++ b/solution.py
@@ -310,12 +310,12 @@
             ref[9 + 3 * i + j, plane, rows, :] = matrix[i][j][1]
 
 
-def chunk_loop(planes, chunks, step):
+def chunk_loop(planes, chunks, step, unroll=1):
     def run(index, carry):
         step(index // chunks, index % chunks)
         return carry
 
-    lax.fori_loop(0, planes * chunks, run, 0)
+    lax.fori_loop(0, planes * chunks, run, 0, unroll=unroll if planes * chunks % unroll == 0 else 1)
 
 
 def aligned(chunk):
@@ -460,7 +460,7 @@
             for comp, value in enumerate(project(load_link(links_ref, direction, rows))):
                 v_ref[direction, comp, plane, aligned(chunk), :] = value
 
-        chunk_loop(planes, half // 8, step)
+        chunk_loop(planes, half // 8, step, 4)
     for copy in reads:
         copy.wait()
     for copy in writes:
@@ -555,7 +555,7 @@
         rows = aligned(chunk)
         store_gauge(g_ref, plane, rows, exponential([x_ref[k, plane, rows, :] for k in range(8)]))
 
-    chunk_loop(slots, half // 8, raise_step)
+    chunk_loop(slots, half // 8, raise_step, 2)
     lanes = x_ref.shape[3]
     shift_gauge(g_ref, inverse_ref[inverse_ref.shape[0] - 2 * lanes :], stack_ref, moved_ref, y_ref)
 
@@ -761,7 +761,7 @@
                 sum_ref[1, to, :] = im
             return carry
 
-        lax.fori_loop(0, groups, run, 0, unroll=2 if groups % 2 == 0 else 1)
+        lax.fori_loop(0, groups, run, 0, unroll=4 if groups % 4 == 0 else 1)
 
     wide_start, near_start = split.starts(mine)
     accumulate(source_ref, wide_start, 0, split.wide, mine, False)

time: 111 us -> 111 us (level)
  no operation moved by 1% of the time
where the time goes in v5:
time: 111 us; the launch traced here: 110 us
  starting transfers between devices  31.1 us (28%)
  waiting for transfers between devices  28.9 us (26%)
  blocking collectives  24.3 us (22%)
  Pallas kernels  20.8 us (19%)
  between operations  2.76 us (2%)
  local copies, waits for them, and re-layouts  2.42 us (2%)
    all_to_all x2, blocking collectives, turn(): return lax.all_to_all(spectrum, 'space', 0, 0, tiled=True)  24.3 us
    pallas_call x8, Pallas kernels, call(): pl.pallas_call(kernel, out_shape=outs, in_specs=in_specs, out_specs=out_s...  20.8 us
    ppermute x3, starting transfers between devices, body(): lax.ppermute(cut, 'tm', [(i, split.moved(i, step)) for i in range(times)])  12.2 us
    all_to_all x2, waiting for transfers between devices, turn(): return lax.all_to_all(spectrum, 'space', 0, 0, tiled=True)  11.5 us
    ppermute x3, waiting for transfers between devices, forwarded(): lax.ppermute(value, 'tm', [(i, (i + shift) % times) for i in range(times)])  9.39 us
    all_to_all x2, starting transfers between devices, turn(): return lax.all_to_all(spectrum, 'space', 0, 0, tiled=True)  7.05 us
    all_to_all x1, starting transfers between devices, body(): gathered = lax.all_to_all(payload, ('space', 'tm'), 0, 0, tiled=True)  4.16 us
    ppermute x3, starting transfers between devices, forwarded(): lax.ppermute(value, 'tm', [(i, (i + shift) % times) for i in range(times)])  3.88 us
  transfers between devices with their start and end apart: 12, of which 7 were waited for; matrix products, arithmetic and copies ran while one was open for 0% of the time, Pallas kernels for 7%

profile of v5, /device:TPU:0, one launch (start us, length us, event | category | flops | bytes accessed | tf_op | source)
XLA Modules:
  0.0 110.4 jit_solution(10606268933374086416)
XLA Ops:
  0.7 3.8 %shard_map.95 = (f32[8,96,128]{2,1,0:T(8,128)}, f32[72,24,128]{2,1,0:T(8,128)}, f32[72,8,128]{2,1,0:T(8,128)}, f32[72,8,128]{2,1,0:T(8,128)}) custom-call(f32[54,64,128]{2,1,0:T(8,128)} %bitcast.19, bf16[896,256]{1,0:T(8,128)(2,1)} %constant.44.clone.table_any.forward_ref, f32[72,64,128]{2,1,0:T(8,128)} %bitcast.22), custom_call_target="tpu_custom_call" | custom-call | tf_op jit(solution)/shard_map/pallas_call | solution.py:848
  4.5 13.6 %all_to_all.25.in_ref = f32[8,96,128]{2,1,0:T(8,128)S(1)} all-to-all(f32[8,96,128]{2,1,0:T(8,128)} %get-tuple-element.56), channel_id=1, replica_groups=mesh['space'=8,'tm'=4] {'space'}, dimensions={0} | all-to-all | bytes 786432 | tf_op jit(solution)/shard_map/all_to_all | solution.py:911
  18.1 0.2 shard_map.96
  18.4 10.7 %all_to_all.26.in_ref = f32[8,96,128]{2,1,0:T(8,128)S(1)} all-to-all(f32[8,96,128]{2,1,0:T(8,128)S(1)} %shard_map.96), channel_id=1, replica_groups=mesh['space'=8,'tm'=4] {'space'}, dimensions={0} | all-to-all | bytes 786432 | tf_op jit(solution)/shard_map/all_to_all | solution.py:911
  29.1 5.0 %shard_map.97 = (f32[8,96,128]{2,1,0:T(8,128)}, f32[8,3,32,128]{3,2,1,0:T(8,128)}, f32[8,24,128]{2,1,0:T(8,128)}, f32[8,24,128]{2,1,0:T(8,128)}, f32[8,24,128]{2,1,0:T(8,128)}, /*index=5*/f32[8,24,128]{2,1,0:T(8,128)}) custom-call(f32[8,96,128]{2,1,0:T(8,128)S(1)} %all_to_all.26.in_ref, f32[54,64,128]{2,1,0:T(8,128)S(1)} %bitcast.21, ...), custom_call_target="tpu_custom_call" | custom-call | tf_op jit(solution)/shard_map/pallas_call | solution.py:848
  34.0 3.6 %all-to-all-start.2 = ((f32[8,96,128]{2,1,0:T(8,128)}), f32[8,96,128]{2,1,0:T(8,128)S(1)}, u32[]{:S(2)}, u32[]{:S(2)}) async-start(f32[8,96,128]{2,1,0:T(8,128)} %get-tuple-element.58), calls=%async_computation.2 | async-start | bytes 786432 | tf_op jit(solution)/shard_map/all_to_all | solution.py:911
  37.7 1.6 %collective-permute-start.15 = (f32[72,24,128]{2,1,0:T(8,128)}, f32[72,24,128]{2,1,0:T(8,128)}, u32[]{:S(2)}, u32[]{:S(2)}) collective-permute-start(f32[72,24,128]{2,1,0:T(8,128)} %get-tuple-element.71), channel_id=1, source_target_pairs={{0,1},{1,0},{2,3},{3,2},{4,5},{5,4},{6,7},{7,6},{8,9},{9,8},{10,11... | collective-permute-start | bytes 2654216 | tf_op jit(solution)/shard_map/ppermute | solution.py:954
  39.3 6.6 %all-to-all-done.2.in_ref = f32[8,96,128]{2,1,0:T(8,128)S(1)} async-done(((f32[8,96,128]{2,1,0:T(8,128)}), f32[8,96,128]{2,1,0:T(8,128)S(1)}, u32[]{:S(2)}, u32[]{:S(2)}) %all-to-all-start.2) | async-done | bytes 393248 | tf_op jit(solution)/shard_map/all_to_all | solution.py:911
  45.9 1.0 shard_map.98
  46.9 3.5 %all-to-all-start.3 = ((f32[8,96,128]{2,1,0:T(8,128)}), f32[8,96,128]{2,1,0:T(8,128)S(1)}, u32[]{:S(2)}, u32[]{:S(2)}) async-start(f32[8,96,128]{2,1,0:T(8,128)} %shard_map.98), calls=%async_computation.3 | async-start | bytes 786432 | tf_op jit(solution)/shard_map/all_to_all | solution.py:911
  50.4 2.7 %collective-permute-start.16 = (f32[72,8,128]{2,1,0:T(8,128)}, f32[72,8,128]{2,1,0:T(8,128)S(1)}, u32[]{:S(2)}, u32[]{:S(2)}) collective-permute-start(f32[72,8,128]{2,1,0:T(8,128)} %get-tuple-element.72), channel_id=1, source_target_pairs={{0,2},{1,3},{2,0},{3,1},{4,6},{5,7},{6,4},{7,5},{8,10},{9,11},{10,... | collective-permute-start | bytes 884744 | tf_op jit(solution)/shard_map/ppermute | solution.py:954
  53.7 4.9 %all-to-all-done.3.in_ref = f32[8,96,128]{2,1,0:T(8,128)S(1)} async-done(((f32[8,96,128]{2,1,0:T(8,128)}), f32[8,96,128]{2,1,0:T(8,128)S(1)}, u32[]{:S(2)}, u32[]{:S(2)}) %all-to-all-start.3) | async-done | bytes 393248 | tf_op jit(solution)/shard_map/all_to_all | solution.py:911
  58.6 0.8 copy-done.4
  59.4 1.0 copy-done.5
  60.4 1.3 %shard_map.99 = (f32[8,3,32,128]{3,2,1,0:T(8,128)S(1)}, f32[8,24,128]{2,1,0:T(8,128)S(1)}, f32[8,24,128]{2,1,0:T(8,128)}, f32[8,24,128]{2,1,0:T(8,128)}, f32[8,24,128]{2,1,0:T(8,128)}) custom-call(f32[8,96,128]{2,1,0:T(8,128)S(1)} %copy-done.5, bf16[896,256]{1,0:T(8,128)(2,1)S(1)} %copy-done.2), custom_call_target="tpu_custom_call" | custom-call | tf_op jit(solution)/shard_map/pallas_call | solution.py:848
  61.7 0.6 copy-done.9
  62.3 6.6 %conditional.1 = (f32[8,24,128]{2,1,0:T(8,128)}, f32[8,24,128]{2,1,0:T(8,128)}, f32[8,24,128]{2,1,0:T(8,128)}) conditional(s32[]{:T(128)} %clamp.3, (f32[8,24,128]{2,1,0:T(8,128)}, f32[8,24,128]{2,1,0:T(8,128)}, f32[8,24,128]{2,1,0:T(8,128)}) %tuple.24, (f32[8,24,128]{2,1,0:T(8,128)S(1)}, f32[8,24,128]{2,1,0:T(8,128)}, ...), branch_computations={%region_0.1_spmd, %region_1.2_spmd, %region_2.3_spmd, %region_3.4_... | conditional | bytes 1179792 | solution.py:1003
  62.3 1.3 %collective-permute-start.3 = (f32[8,24,128]{2,1,0:T(8,128)S(1)}, f32[8,24,128]{2,1,0:T(8,128)}, u32[]{:S(2)}, u32[]{:S(2)}) collective-permute-start(f32[8,24,128]{2,1,0:T(8,128)S(1)} %get-tuple-element.27), channel_id=1, source_target_pairs={{1,0},{5,4},{9,8},{13,12},{17,16},{21,20},{25,24},{29,28}} | collective-permute-start | bytes 294920 | tf_op jit(solution)/shard_map/cond/branch_1_fun/ppermute | solution.py:996
  63.6 1.3 %collective-permute-start.4 = (f32[8,24,128]{2,1,0:T(8,128)}, f32[8,24,128]{2,1,0:T(8,128)}, u32[]{:S(2)}, u32[]{:S(2)}) collective-permute-start(f32[8,24,128]{2,1,0:T(8,128)} %get-tuple-element.28), channel_id=1, source_target_pairs={{1,2},{5,6},{9,10},{13,14},{17,18},{21,22},{25,26},{29,30}} | collective-permute-start | bytes 294920 | tf_op jit(solution)/shard_map/cond/branch_1_fun/ppermute | solution.py:996
  64.9 1.3 %collective-permute-start.5 = (f32[8,24,128]{2,1,0:T(8,128)}, f32[8,24,128]{2,1,0:T(8,128)}, u32[]{:S(2)}, u32[]{:S(2)}) collective-permute-start(f32[8,24,128]{2,1,0:T(8,128)} %get-tuple-element.29), channel_id=1, source_target_pairs={{1,3},{5,7},{9,11},{13,15},{17,19},{21,23},{25,27},{29,31}} | collective-permute-start | bytes 294920 | tf_op jit(solution)/shard_map/cond/branch_1_fun/ppermute | solution.py:996
  66.2 2.7 %collective-permute-done.3 = f32[8,24,128]{2,1,0:T(8,128)} collective-permute-done((f32[8,24,128]{2,1,0:T(8,128)S(1)}, f32[8,24,128]{2,1,0:T(8,128)}, u32[]{:S(2)}, u32[]{:S(2)}) %collective-permute-start.3) | collective-permute-done | bytes 98336 | tf_op jit(solution)/shard_map/cond/branch_1_fun/ppermute | solution.py:996
  68.9 7.9 %collective-permute-start.17 = (f32[72,8,128]{2,1,0:T(8,128)}, f32[72,8,128]{2,1,0:T(8,128)S(1)}, u32[]{:S(2)}, u32[]{:S(2)}) collective-permute-start(f32[72,8,128]{2,1,0:T(8,128)} %get-tuple-element.73), channel_id=1, source_target_pairs={{0,3},{1,2},{2,1},{3,0},{4,7},{5,6},{6,5},{7,4},{8,11},{9,10},{10,... | collective-permute-start | bytes 884744 | tf_op jit(solution)/shard_map/ppermute | solution.py:954
  76.8 0.6 collective-permute-start.13
  77.4 3.3 %collective-permute-start.14 = (f32[8,24,128]{2,1,0:T(8,128)}, f32[8,24,128]{2,1,0:T(8,128)S(1)}, u32[]{:S(2)}, u32[]{:S(2)}) collective-permute-start(f32[8,24,128]{2,1,0:T(8,128)} %get-tuple-element.63), channel_id=1, source_target_pairs={{0,3},{1,0},{2,1},{3,2},{4,7},{5,4},{6,5},{7,6},{8,11},{9,8},{10,9... | collective-permute-start | bytes 294920 | tf_op jit(solution)/shard_map/ppermute | solution.py:884
  82.0 2.9 %collective-permute-done.17.rest_12_ = f32[72,8,128]{2,1,0:T(8,128)S(1)} collective-permute-done((f32[72,8,128]{2,1,0:T(8,128)}, f32[72,8,128]{2,1,0:T(8,128)S(1)}, u32[]{:S(2)}, u32[]{:S(2)}) %collective-permute-start.17) | collective-permute-done | bytes 294944 | tf_op jit(solution)/shard_map/ppermute | solution.py:954
  84.9 1.3 %collective-permute-done.12.rest_0_ = f32[8,24,128]{2,1,0:T(8,128)S(1)} collective-permute-done((f32[8,24,128]{2,1,0:T(8,128)}, f32[8,24,128]{2,1,0:T(8,128)S(1)}, u32[]{:S(2)}, u32[]{:S(2)}) %collective-permute-start.12) | collective-permute-done | bytes 98336 | tf_op jit(solution)/shard_map/ppermute | solution.py:884
  86.3 8.0 %collective-permute-done.13.rest_1_ = f32[8,24,128]{2,1,0:T(8,128)S(1)} collective-permute-done((f32[8,24,128]{2,1,0:T(8,128)}, f32[8,24,128]{2,1,0:T(8,128)S(1)}, u32[]{:S(2)}, u32[]{:S(2)}) %collective-permute-start.13) | collective-permute-done | bytes 98336 | tf_op jit(solution)/shard_map/ppermute | solution.py:884
  94.4 3.6 %shard_map.101 = f32[32,4,128]{2,1,0:T(4,128)} custom-call(s32[1]{0:T(128)S(6)} %select_n.17.sink_ref, s32[1]{0:T(128)S(6)} %select_n.18.src_time_ref, s32[1]{0:T(128)S(6)} %max.3.src_site_ref, f32[8,3,32,128]{3,2,1,0:T(8,128)} %get-tuple-element.57.first_any, f32[8,3,32,128]{3,2,1,0:T(8,128)S(1)} %get-tuple-element.59.second_ref, ...), custom_call_target="tpu_custom_call" | custom-call | tf_op jit(solution)/shard_map/pallas_call | solution.py:848
  98.0 4.2 %all-to-all-start.4 = ((f32[32,4,128]{2,1,0:T(4,128)}), f32[32,4,128]{2,1,0:T(4,128)S(1)}, u32[]{:S(2)}, u32[]{:S(2)}) async-start(f32[32,4,128]{2,1,0:T(4,128)} %shard_map.101), calls=%async_computation.4 | async-start | bytes 131072 | tf_op jit(solution)/shard_map/all_to_all | solution.py:1043
  102.1 5.2 %shard_map.100 = f32[54,64,128]{2,1,0:T(8,128)} custom-call(f32[54,64,128]{2,1,0:T(8,128)} %bitcast.20, f32[8,3,32,128]{3,2,1,0:T(8,128)} %get-tuple-element.57.first_any, bf16[896,256]{1,0:T(8,128)(2,1)} %constant.45.clone.inverse_ref.table_any, f32[8,3,32,128]{3,2,1,0:T(8,128)S(1)} %get-tuple-element.59.second_ref), custom_call_target="tpu_custom_call" | custom-call | tf_op jit(solution)/shard_map/pallas_call | solution.py:848
  107.3 2.3 %all-to-all-done.4.in_ref = f32[32,4,128]{2,1,0:T(4,128)S(1)} async-done(((f32[32,4,128]{2,1,0:T(4,128)}), f32[32,4,128]{2,1,0:T(4,128)S(1)}, u32[]{:S(2)}, u32[]{:S(2)}) %all-to-all-start.4) | async-done | bytes 65568 | tf_op jit(solution)/shard_map/all_to_all | solution.py:1043
  109.6 0.7 shard_map.102
  (23 shorter events, 0.1 us)
Async XLA Ops:
  0.6 17.5 %copy-start.6 = (f32[2,9,16,128]{3,2,1,0:T(8,128)S(1)}, f32[2,9,16,128]{3,2,1,0:T(8,128)}, u32[]{:S(2)}) copy-start(f32[2,9,16,128]{3,2,1,0:T(8,128)} %constant.46.clone.table_ref) | copy-start | bytes 442372
  0.6 28.4 %copy-start.3 = (bf16[896,256]{1,0:T(8,128)(2,1)S(1)}, bf16[896,256]{1,0:T(8,128)(2,1)}, u32[]{:S(2)}) copy-start(bf16[896,256]{1,0:T(8,128)(2,1)} %constant.44.clone.table_any.forward_ref) | copy-start | bytes 1376260
  4.4 24.6 %copy-start = (f32[1,3,2,3,3,2,4096]{6,5,4,3,2,1,0:T(2,128)S(1)}, f32[1,3,2,3,3,2,4096]{6,5,4,3,2,1,0:T(2,128)}, u32[]{:S(2)}) copy-start(f32[1,3,2,3,3,2,4096]{6,5,4,3,2,1,0:T(2,128)} %param.12) | copy-start | bytes 5308420
  4.4 24.6 %copy-start.2 = (bf16[896,256]{1,0:T(8,128)(2,1)S(1)}, bf16[896,256]{1,0:T(8,128)(2,1)}, u32[]{:S(2)}) copy-start(bf16[896,256]{1,0:T(8,128)(2,1)} %constant.45.clone.inverse_ref.table_any) | copy-start | bytes 1376260
  34.0 60.3 %copy-start.1 = (f32[2,36,2,4096]{3,2,1,0:T(2,128)S(1)}, f32[2,36,2,4096]{3,2,1,0:T(2,128)}, u32[]{:S(2)}) copy-start(f32[2,36,2,4096]{3,2,1,0:T(2,128)} %param.13) | copy-start | bytes 7077892
  34.0 11.8 %all-to-all-start.2 = ((f32[8,96,128]{2,1,0:T(8,128)}), f32[8,96,128]{2,1,0:T(8,128)S(1)}, u32[]{:S(2)}, u32[]{:S(2)}) async-start(f32[8,96,128]{2,1,0:T(8,128)} %get-tuple-element.58), calls=%async_computation.2 | async-start | bytes 786432 | tf_op jit(solution)/shard_map/all_to_all | solution.py:911
  37.7 56.7 %collective-permute-start.15 = (f32[72,24,128]{2,1,0:T(8,128)}, f32[72,24,128]{2,1,0:T(8,128)}, u32[]{:S(2)}, u32[]{:S(2)}) collective-permute-start(f32[72,24,128]{2,1,0:T(8,128)} %get-tuple-element.71), channel_id=1, source_target_pairs={{0,1},{1,0},{2,3},{3,2},{4,5},{5,4},{6,7},{7,6},{8,9},{9,8},{10,11... | collective-permute-start | bytes 2654216 | tf_op jit(solution)/shard_map/ppermute | solution.py:954
  46.9 11.7 %all-to-all-start.3 = ((f32[8,96,128]{2,1,0:T(8,128)}), f32[8,96,128]{2,1,0:T(8,128)S(1)}, u32[]{:S(2)}, u32[]{:S(2)}) async-start(f32[8,96,128]{2,1,0:T(8,128)} %shard_map.98), calls=%async_computation.3 | async-start | bytes 786432 | tf_op jit(solution)/shard_map/all_to_all | solution.py:911
  50.4 27.0 %collective-permute-start.16 = (f32[72,8,128]{2,1,0:T(8,128)}, f32[72,8,128]{2,1,0:T(8,128)S(1)}, u32[]{:S(2)}, u32[]{:S(2)}) collective-permute-start(f32[72,8,128]{2,1,0:T(8,128)} %get-tuple-element.72), channel_id=1, source_target_pairs={{0,2},{1,3},{2,0},{3,1},{4,6},{5,7},{6,4},{7,5},{8,10},{9,11},{10,... | collective-permute-start | bytes 884744 | tf_op jit(solution)/shard_map/ppermute | solution.py:954
  58.6 0.8 copy-start.4
  59.4 1.0 copy-start.5
  61.7 0.6 copy-start.9
  62.3 6.6 %collective-permute-start.3 = (f32[8,24,128]{2,1,0:T(8,128)S(1)}, f32[8,24,128]{2,1,0:T(8,128)}, u32[]{:S(2)}, u32[]{:S(2)}) collective-permute-start(f32[8,24,128]{2,1,0:T(8,128)S(1)} %get-tuple-element.27), channel_id=1, source_target_pairs={{1,0},{5,4},{9,8},{13,12},{17,16},{21,20},{25,24},{29,28}} | collective-permute-start | bytes 294920 | tf_op jit(solution)/shard_map/cond/branch_1_fun/ppermute | solution.py:996
  63.6 5.3 %collective-permute-start.4 = (f32[8,24,128]{2,1,0:T(8,128)}, f32[8,24,128]{2,1,0:T(8,128)}, u32[]{:S(2)}, u32[]{:S(2)}) collective-permute-start(f32[8,24,128]{2,1,0:T(8,128)} %get-tuple-element.28), channel_id=1, source_target_pairs={{1,2},{5,6},{9,10},{13,14},{17,18},{21,22},{25,26},{29,30}} | collective-permute-start | bytes 294920 | tf_op jit(solution)/shard_map/cond/branch_1_fun/ppermute | solution.py:996
  64.9 4.0 %collective-permute-start.5 = (f32[8,24,128]{2,1,0:T(8,128)}, f32[8,24,128]{2,1,0:T(8,128)}, u32[]{:S(2)}, u32[]{:S(2)}) collective-permute-start(f32[8,24,128]{2,1,0:T(8,128)} %get-tuple-element.29), channel_id=1, source_target_pairs={{1,3},{5,7},{9,11},{13,15},{17,19},{21,23},{25,27},{29,31}} | collective-permute-start | bytes 294920 | tf_op jit(solution)/shard_map/cond/branch_1_fun/ppermute | solution.py:996
  68.9 16.0 %collective-permute-start.17 = (f32[72,8,128]{2,1,0:T(8,128)}, f32[72,8,128]{2,1,0:T(8,128)S(1)}, u32[]{:S(2)}, u32[]{:S(2)}) collective-permute-start(f32[72,8,128]{2,1,0:T(8,128)} %get-tuple-element.73), channel_id=1, source_target_pairs={{0,3},{1,2},{2,1},{3,0},{4,7},{5,6},{6,5},{7,4},{8,11},{9,10},{10,... | collective-permute-start | bytes 884744 | tf_op jit(solution)/shard_map/ppermute | solution.py:954
  76.8 9.5 %collective-permute-start.12 = (f32[8,24,128]{2,1,0:T(8,128)}, f32[8,24,128]{2,1,0:T(8,128)S(1)}, u32[]{:S(2)}, u32[]{:S(2)}) collective-permute-start(f32[8,24,128]{2,1,0:T(8,128)} %get-tuple-element.61), channel_id=1, source_target_pairs={{0,1},{1,2},{2,3},{3,0},{4,5},{5,6},{6,7},{7,4},{8,9},{9,10},{10,1... | collective-permute-start | bytes 294920 | tf_op jit(solution)/shard_map/ppermute | solution.py:884
  76.8 17.5 %collective-permute-start.13 = (f32[8,24,128]{2,1,0:T(8,128)}, f32[8,24,128]{2,1,0:T(8,128)S(1)}, u32[]{:S(2)}, u32[]{:S(2)}) collective-permute-start(f32[8,24,128]{2,1,0:T(8,128)} %get-tuple-element.62), channel_id=1, source_target_pairs={{0,2},{1,3},{2,0},{3,1},{4,6},{5,7},{6,4},{7,5},{8,10},{9,11},{10,... | collective-permute-start | bytes 294920 | tf_op jit(solution)/shard_map/ppermute | solution.py:884
  77.4 16.9 %copy-start.7 = (f32[72,8,128]{2,1,0:T(8,128)}, f32[72,8,128]{2,1,0:T(8,128)S(1)}, u32[]{:S(2)}) copy-start(f32[72,8,128]{2,1,0:T(8,128)S(1)} %collective-permute-done.16.rest_11_) | copy-start | bytes 884740
  77.4 16.9 %collective-permute-start.14 = (f32[8,24,128]{2,1,0:T(8,128)}, f32[8,24,128]{2,1,0:T(8,128)S(1)}, u32[]{:S(2)}, u32[]{:S(2)}) collective-permute-start(f32[8,24,128]{2,1,0:T(8,128)} %get-tuple-element.63), channel_id=1, source_target_pairs={{0,3},{1,0},{2,1},{3,2},{4,7},{5,4},{6,5},{7,6},{8,11},{9,8},{10,9... | collective-permute-start | bytes 294920 | tf_op jit(solution)/shard_map/ppermute | solution.py:884
  84.9 9.4 %copy-start.8 = (f32[72,8,128]{2,1,0:T(8,128)}, f32[72,8,128]{2,1,0:T(8,128)S(1)}, u32[]{:S(2)}) copy-start(f32[72,8,128]{2,1,0:T(8,128)S(1)} %collective-permute-done.17.rest_12_) | copy-start | bytes 884740
  98.0 11.7 %all-to-all-start.4 = ((f32[32,4,128]{2,1,0:T(4,128)}), f32[32,4,128]{2,1,0:T(4,128)S(1)}, u32[]{:S(2)}, u32[]{:S(2)}) async-start(f32[32,4,128]{2,1,0:T(4,128)} %shard_map.101), calls=%async_computation.4 | async-start | bytes 131072 | tf_op jit(solution)/shard_map/all_to_all | solution.py:1043
